TPU v7x, 32 devices: a whole 2x2x4 slice. The times are simulated.
32 devices in a mesh: tm: 8 (over z, y), space: 4 (over x, core).
Axes of the slice: x: 2, y: 2, z: 4, core: 2. Of those that a mesh axis runs over, the one named last changes fastest.
Arguments:
- residual: float32 [8, 2, 1024, 1024], P('tm', None, 'space'), may hold values from -0.875 to 0.875
- counts: int32 [8], P('tm'), may hold values from 1 to 4
Outputs:
- fields: float32 [8, 2, 1024, 1024], P('tm', None, 'space')
All inputs are finite; a program needn't handle non-finite values.
Results may differ from a plain program's by a relative error of at most 0.0003.
Values sent between devices are 32-bit elements; how exact they have to be, the bound alone decides.
No kernel may reach another device: no remote copies, remote signals or barrier semaphores. Data moves between devices by JAX's collectives and lax.ppermute only.
A program may use at most 320 MiB of HBM per device.

v0:
```python
import functools
import math

import jax
import jax.numpy as jnp
import numpy as np
from jax import lax
from jax.experimental import pallas as pl
from jax.experimental.pallas import tpu as pltpu
from jax.sharding import Mesh
from jax.sharding import PartitionSpec as P

phase_rate = 0.004
f32 = jnp.float32
bf16 = jnp.bfloat16
NN = (((1,), (0,)), ((), ()))
NT = (((1,), (1,)), ((), ()))
TN = (((0,), (0,)), ((), ()))
SIN = (3.14159274, -5.1677103, 2.55007744, -0.598291218, 0.0776574388)
COS = (1.0, -4.93480206, 4.05870914, -1.335212, 0.23493728, -0.0243962663)


def cas_tables(length):
    quarter = length // 4
    m = np.arange(quarter, dtype=np.int64)
    j = np.arange(quarter, dtype=np.int64)

    def cas(k, sign=1):
        angle = sign * 2.0 * np.pi * ((k[:, None] * j[None, :]) % length) / length
        return np.cos(angle) + np.sin(angle)

    odd = np.block(
        [
            [cas(4 * m + 1), cas(4 * m + 1, -1)],
            [cas(4 * m + 3), -cas(4 * m + 3, -1)],
        ]
    )
    tables = []
    for table in (cas(4 * m), cas(4 * m + 2), odd):
        table = table.astype(np.float32)
        high = table.astype(jnp.bfloat16)
        low = (table - high.astype(np.float32)).astype(jnp.bfloat16)
        tables += [high, low]
    return tables


def halves(value):
    high = value.astype(bf16)
    return high, (value - high.astype(f32)).astype(bf16)


def product(left, right, form):
    dot = functools.partial(lax.dot_general, dimension_numbers=form, preferred_element_type=f32)
    return dot(left[0], right[0]) + dot(left[0], right[1]) + dot(left[1], right[0])


def fold(parts):
    even, cross = parts[0] + parts[2], parts[1] + parts[3]
    return even + cross, even - cross


def fold_odd(parts):
    return jnp.concatenate([parts[0] - parts[2], parts[1] - parts[3]], axis=-1)


def signed_wave(indices, length):
    return jnp.where(indices < length // 2, indices, indices - length).astype(f32)


def wave_at(spot, length):
    quarter = length // 4
    block = spot // quarter
    return 4 * (spot % quarter) + jnp.where(block == 1, 2, jnp.where(block == 2, 1, block))


def modulus_at(start, shape, length_x, length_y):
    place_y = start + lax.broadcasted_iota(jnp.int32, shape, 0)
    place_x = lax.broadcasted_iota(jnp.int32, shape, 1)
    wave_y = signed_wave(wave_at(place_y, length_y), length_y)
    wave_x = signed_wave(wave_at(place_x, length_x), length_x)
    return jnp.sqrt(wave_x * wave_x + wave_y * wave_y)


def turn(angle):
    part = angle - jnp.round(angle)
    square = part * part
    sine = jnp.full_like(square, SIN[-1])
    for factor in SIN[-2::-1]:
        sine = sine * square + factor
    sine = sine * part
    cosine = jnp.full_like(square, COS[-1])
    for factor in COS[-2::-1]:
        cosine = cosine * square + factor
    return 1.0 - 2.0 * sine * sine, 2.0 * sine * cosine


def place(odd, rows, length_y):
    point = lax.axis_index("point")
    band = point * lax.axis_size("space") + lax.axis_index("space")
    return odd * (length_y // 2) + band * rows, point


def rate_of(n, point, count_refs):
    points = len(count_refs)
    shift = lax.rem(point + points - n, points)
    count = count_refs[0][0]
    for d in range(1, points):
        count = jnp.where(shift == d, count_refs[d][0], count)
    return count.astype(f32) * (phase_rate / (2.0 * math.pi))


def forward_y(odd, x_ref, *refs):
    tables, out = [ref[...] for ref in refs[:-1]], refs[-1]
    quarter = x_ref.shape[-1] // 4
    bands, _, rows, slab = out.shape
    for part in range(2):
        pieces = [x_ref[part, :, q * quarter : (q + 1) * quarter] for q in range(4)]
        if odd:
            result = product(tables, halves(fold_odd(pieces)), NT)
            out[:, part] = result.reshape(bands, rows, slab)
        else:
            total, alternate = fold(pieces)
            half = bands // 2
            out[:half, part] = product(tables[:2], halves(total), NT).reshape(half, rows, slab)
            out[half:, part] = product(tables[2:], halves(alternate), NT).reshape(half, rows, slab)


def forward_x(odd, length_y, points, *refs):
    count_refs, (r_ref, *refs) = refs[:points], refs[points:]
    tables, (spectra, last) = [ref[...] for ref in refs[:-2]], refs[-2:]
    points, spaces, _, rows, slab = r_ref.shape
    start, point = place(odd, rows, length_y)
    rates = [rate_of(n, point, count_refs) for n in range(points)]
    length_x = spaces * slab
    quarter = length_x // 4
    count = points * 2 * rows
    if spaces == 4:
        pieces = [r_ref[:, s].reshape(count, slab) for s in range(4)]
    else:
        whole = jnp.concatenate([r_ref[:, s].reshape(count, slab) for s in range(spaces)], axis=-1)
        pieces = [whole[:, q * quarter : (q + 1) * quarter] for q in range(4)]
    total, alternate = fold(pieces)
    shape = (points, 2, rows, quarter)
    spectra[..., :quarter] = product(halves(total), tables[:2], NT).reshape(shape)
    spectra[..., quarter : 2 * quarter] = product(halves(alternate), tables[2:4], NT).reshape(shape)
    mixed = product(halves(fold_odd(pieces)), tables[4:], NT)
    spectra[..., 2 * quarter :] = mixed.reshape(points, 2, rows, 2 * quarter)
    block = math.gcd(rows, 8)

    def step(index, _):
        here = pl.ds(pl.multiple_of(index * block, block), block)
        modulus = modulus_at(start + index * block, (block, length_x), length_x, length_y)
        first, second = spectra[0, 0, here, :], spectra[0, 1, here, :]
        for n in range(1, points):
            cosine, sine = turn(rates[n] * modulus)
            first, second = (
                cosine * first + sine * second + spectra[n, 0, here, :],
                cosine * second - sine * first + spectra[n, 1, here, :],
            )
        last[0, here, :] = first
        last[1, here, :] = second
        return 0

    lax.fori_loop(0, rows // block, step, 0)


def finish_x(odd, length_y, points, *refs):
    count_refs, (spectra, carry, *refs) = refs[:points], refs[points:]
    tables, (out, states) = [ref[...] for ref in refs[:-2]], refs[-2:]
    points, spaces, _, rows, slab = out.shape
    length_x = spaces * slab
    quarter = length_x // 4
    count = points * 2 * rows
    block = math.gcd(rows, 8)
    scaling = 1.0 / (length_x * length_y)
    start, point = place(odd, rows, length_y)
    rates = [rate_of(n, point, count_refs) for n in range(points)]

    def step(index, _):
        here = pl.ds(pl.multiple_of(index * block, block), block)
        modulus = modulus_at(start + index * block, (block, length_x), length_x, length_y)
        first, second = carry[0, here, :], carry[1, here, :]
        for n in range(points):
            cosine, sine = turn(rates[n] * modulus)
            first, second = (
                cosine * first + sine * second + spectra[n, 0, here, :],
                cosine * second - sine * first + spectra[n, 1, here, :],
            )
            states[n, 0, here, :] = first * scaling
            states[n, 1, here, :] = second * scaling
        return 0

    lax.fori_loop(0, rows // block, step, 0)
    total = product(halves(states[..., :quarter].reshape(count, quarter)), tables[:2], NN)
    alternate = product(halves(states[..., quarter : 2 * quarter].reshape(count, quarter)), tables[2:4], NN)
    mixed = product(halves(states[..., 2 * quarter :].reshape(count, 2 * quarter)), tables[4:], NN)
    plus, minus = total + alternate, total - alternate
    straight, crossed = mixed[:, :quarter], mixed[:, quarter:]
    results = [plus + straight, minus + crossed, plus - straight, minus - crossed]
    if spaces != 4:
        whole = jnp.concatenate(results, axis=-1)
        results = [whole[:, s * slab : (s + 1) * slab] for s in range(spaces)]
    for s in range(spaces):
        out[:, s] = results[s].reshape(points, 2, rows, slab)


def inverse_y_even(r_ref, *refs):
    tables, out = [ref[...] for ref in refs[:-1]], refs[-1]
    bands, _, rows, slab = r_ref.shape
    half = bands // 2
    for part in range(2):
        total = product(halves(r_ref[:half, part].reshape(half * rows, slab)), tables[:2], TN)
        alternate = product(halves(r_ref[half:, part].reshape(half * rows, slab)), tables[2:], TN)
        out[part] = jnp.concatenate([total + alternate, total - alternate], axis=-1)


def inverse_y_odd(r_ref, even_ref, *refs):
    tables, out = [ref[...] for ref in refs[:-1]], refs[-1]
    bands, _, rows, slab = r_ref.shape
    width = even_ref.shape[-1]
    for part in range(2):
        mixed = product(halves(r_ref[:, part].reshape(bands * rows, slab)), tables, TN)
        out[part, :, :width] = even_ref[part] + mixed
        flipped = even_ref[part] - mixed
        out[part, :, width:] = flipped


def call(kernel, name, operands, outs, flops, scalars=0, scratch=()):
    space = pl.BlockSpec(memory_space=pltpu.VMEM)
    scalar = pl.BlockSpec(memory_space=pltpu.SMEM)
    shapes = [jax.ShapeDtypeStruct(shape, f32) for shape in outs]
    traffic = sum(math.prod(x.shape) * x.dtype.itemsize for x in operands)
    traffic += sum(4 * math.prod(shape) for shape in outs)
    many = len(outs) > 1
    return pl.pallas_call(
        kernel,
        name=name,
        in_specs=[scalar] * scalars + [space] * (len(operands) - scalars),
        out_specs=[space] * len(outs) if many else space,
        out_shape=shapes if many else shapes[0],
        scratch_shapes=[pltpu.VMEM(shape, f32) for shape in scratch],
        cost_estimate=pl.CostEstimate(flops=flops, bytes_accessed=traffic, transcendentals=0),
        compiler_params=pltpu.CompilerParams(vmem_limit_bytes=48 * 2**20),
    )(*operands)


def on_device(residual, counts):
    slab, length_y = residual.shape[2:]
    blocks, points, spaces = (lax.axis_size(name) for name in ("block", "point", "space"))
    length_x = slab * spaces
    group = ("point", "space")
    bands = points * spaces
    rows = length_y // (2 * bands)
    table_x, even_y = (cas_tables(length) for length in (length_x, length_y))
    odd_y, even_y = even_y[4:], even_y[:4]

    shifts = [lax.ppermute(counts, "point", [(i, (i + d) % points) for i in range(points)]) for d in range(1, points)]
    near = [counts] + shifts
    rows_total = 2 * slab

    sent = []
    for odd, tables in enumerate((even_y, odd_y)):
        sent.append(
            call(
                functools.partial(forward_y, bool(odd)),
                "forward_y_%d" % odd,
                [residual[0], *tables],
                [(bands, 2, rows, slab)],
                3 * 2 * rows_total * (length_y // 2) * (length_y // (2 if odd else 4)),
            )
        )
    sent[0], *near = lax.optimization_barrier((sent[0], *near))
    solved = []
    for odd in range(2):
        arrived = lax.all_to_all(sent[odd], group, split_axis=0, concat_axis=0, tiled=True)
        arrived = arrived.reshape(points, spaces, 2, rows, slab)
        spectra, last = call(
            functools.partial(forward_x, odd, length_y, points),
            "forward_x_%d" % odd,
            [*near, arrived, *table_x],
            [(points, 2, rows, length_x), (2, rows, length_x)],
            6 * 2 * rows * points * length_x * length_x // 2,
            scalars=points,
        )
        carry = lax.ppermute(last, "block", [(b, b + 1) for b in range(blocks - 1)])
        if blocks > 2:
            total = sum(near)[0].astype(f32) * (phase_rate / (2.0 * math.pi))
            span = lax.ppermute(total, "block", [(b, b + 1) for b in range(blocks - 1)])
            modulus = modulus_at(place(odd, rows, length_y)[0], (rows, length_x), length_x, length_y)
            reach = 1
            while reach < blocks - 1:
                steps = [(b, b + reach) for b in range(blocks - reach)]
                further = lax.ppermute(carry, "block", steps)
                cosine, sine = turn(span * modulus)
                carry = carry + jnp.stack(
                    [
                        cosine * further[0] + sine * further[1],
                        cosine * further[1] - sine * further[0],
                    ]
                )
                span = span + lax.ppermute(span, "block", steps)
                reach *= 2
        back = call(
            functools.partial(finish_x, odd, length_y, points),
            "finish_x_%d" % odd,
            [*near, spectra, carry, *table_x],
            [(points, spaces, 2, rows, slab)],
            6 * 2 * rows * points * length_x * length_x // 2,
            scalars=points,
            scratch=[(points, 2, rows, length_x)],
        )
        back = back.reshape(bands, 2, rows, slab)
        solved.append(lax.all_to_all(back, group, split_axis=0, concat_axis=0, tiled=True))
    flops = 3 * 2 * rows_total * (length_y // 2) * (length_y // 4)
    even = call(inverse_y_even, "inverse_y_0", [solved[0], *even_y], [(2, slab, length_y // 2)], flops)
    fields = call(inverse_y_odd, "inverse_y_1", [solved[1], even, *odd_y], [(2, slab, length_y)], 2 * flops)
    return fields[None]


def solution(mesh):
    times, spaces = mesh.shape["tm"], mesh.shape["space"]
    points = 4 if times % 4 == 0 else 1
    inner = Mesh(mesh.devices.reshape(times // points, points, spaces), ("block", "point", "space"))
    when = ("block", "point")
    return jax.shard_map(
        on_device,
        mesh=inner,
        in_specs=(P(when, None, "space", None), P(when)),
        out_specs=P(when, None, "space", None),
        check_vma=False,
    )
```

profile of v0, /device:TPU:0, one launch (start us, length us, event | category | flops | bytes accessed | tf_op | source)
XLA Modules:
  0.0 119.3 jit_solution(4355903368468860068)
XLA Ops:
  0.0 3.1 %collective-permute-start.1 = (s32[1]{0:T(128)}, s32[1]{0:T(128)}, u32[]{:S(2)}, u32[]{:S(2)}) collective-permute-start(s32[1]{0:T(128)} %param.15), channel_id=1, source_target_pairs={{0,8},{4,12},{8,0},{12,4},{1,9},{5,13},{9,1},{13,5},{2,10},{6,14},... | collective-permute-start | bytes 20 | tf_op jit(solution)/shard_map/ppermute | solution.py:257
  3.1 1.5 %collective-permute-start = (s32[1]{0:T(128)}, s32[1]{0:T(128)}, u32[]{:S(2)}, u32[]{:S(2)}) collective-permute-start(s32[1]{0:T(128)} %param.15), channel_id=1, source_target_pairs={{0,4},{4,8},{8,12},{12,0},{1,5},{5,9},{9,13},{13,1},{2,6},{6,10},{... | collective-permute-start | bytes 20 | tf_op jit(solution)/shard_map/ppermute | solution.py:257
  4.6 1.4 %collective-permute-start.2 = (s32[1]{0:T(128)}, s32[1]{0:T(128)}, u32[]{:S(2)}, u32[]{:S(2)}) collective-permute-start(s32[1]{0:T(128)} %param.15), channel_id=1, source_target_pairs={{0,12},{4,0},{8,4},{12,8},{1,13},{5,1},{9,5},{13,9},{2,14},{6,2},{... | collective-permute-start | bytes 20 | tf_op jit(solution)/shard_map/ppermute | solution.py:257
  6.0 1.6 %copy-done = f32[1,2,256,1024]{3,2,1,0:T(8,128)S(1)} copy-done((f32[1,2,256,1024]{3,2,1,0:T(8,128)S(1)}, f32[1,2,256,1024]{3,2,1,0:T(8,128)}, u32[]{:S(2)}) %copy-start) | copy-done | bytes 2097176
  7.6 0.9 copy-done.8
  8.5 0.9 copy-done.10
  9.4 0.9 copy-done.12
  10.3 0.9 copy-done.14
  11.2 0.6 forward_y_0.1
  11.8 1.0 copy-done.4
  12.8 0.0 collective-permute-done.1.refs_2_
  12.8 0.0 collective-permute-done.refs_1_
  12.8 0.0 collective-permute-done.2.refs_3_
  12.8 4.3 %all-to-all-start.2 = ((f32[16,2,32,256]{3,2,1,0:T(8,128)}), f32[16,2,32,256]{3,2,1,0:T(8,128)}, u32[]{:S(2)}, u32[]{:S(2)}) async-start(f32[16,2,32,256]{3,2,1,0:T(8,128)} %copy-done.4), calls=%async_computation.2 | async-start | bytes 2097152 | tf_op jit(solution)/shard_map/all_to_all | solution.py:275
  17.2 0.0 copy-done.1
  17.2 0.0 copy-done.2
  17.2 0.0 copy-done.3
  17.2 1.0 forward_y_1.1
  18.2 0.0 copy-start.7
  18.2 1.0 copy-done.7
  19.2 14.1 %all-to-all-done.2 = f32[16,2,32,256]{3,2,1,0:T(8,128)} async-done(((f32[16,2,32,256]{3,2,1,0:T(8,128)}), f32[16,2,32,256]{3,2,1,0:T(8,128)}, u32[]{:S(2)}, u32[]{:S(2)}) %all-to-all-start.2) | async-done | bytes 1048608 | tf_op jit(solution)/shard_map/all_to_all | solution.py:275
  33.3 3.7 %all-to-all-start = ((f32[16,2,32,256]{3,2,1,0:T(8,128)}), f32[16,2,32,256]{3,2,1,0:T(8,128)S(1)}, u32[]{:S(2)}, u32[]{:S(2)}) async-start(f32[16,2,32,256]{3,2,1,0:T(8,128)} %copy-done.7), calls=%async_computation | async-start | bytes 2097152 | tf_op jit(solution)/shard_map/all_to_all | solution.py:275
  37.6 0.0 copy-done.9
  37.6 0.0 copy-done.11
  37.6 0.0 copy-done.13
  37.7 0.0 copy-done.15
  37.7 4.6 %forward_x_0.1 = (f32[4,2,32,1024]{3,2,1,0:T(8,128)S(1)}, f32[2,32,1024]{2,1,0:T(8,128)S(1)}) custom-call(s32[1]{0:T(128)S(6)} %copy.15.refs_0_, s32[1]{0:T(128)} %collective-permute-done.refs_1_, s32[1]{0:T(128)} %collective-permute-done.1.refs_2_, s32[1]{0:T(128)} %collective-permute-done.2.refs_3_, f32[4,4,2,32,256]{4,3,2,1,0:T(8,128)} %bitcast.3.refs_4_, ...), custom_call_target="tpu_custom_call" | custom-call | flops 805306368 | bytes 3932176 | tf_op jit(solution)/shard_map/forward_x_0/pallas_call | solution.py:235
  42.2 4.5 %collective-permute-start.4 = (f32[2,32,1024]{2,1,0:T(8,128)S(1)}, f32[2,32,1024]{2,1,0:T(8,128)S(1)}, u32[]{:S(2)}, u32[]{:S(2)}) collective-permute-start(f32[2,32,1024]{2,1,0:T(8,128)S(1)} %get-tuple-element.22), channel_id=1, source_target_pairs={{0,16},{1,17},{2,18},{3,19},{4,20},{5,21},{6,22},{7,23},{8,24},{9,... | collective-permute-start | bytes 786440 | tf_op jit(solution)/shard_map/ppermute | solution.py:285
  46.7 8.0 %collective-permute-done.4.refs_5_ = f32[2,32,1024]{2,1,0:T(8,128)S(1)} collective-permute-done((f32[2,32,1024]{2,1,0:T(8,128)S(1)}, f32[2,32,1024]{2,1,0:T(8,128)S(1)}, u32[]{:S(2)}, u32[]{:S(2)}) %collective-permute-start.4) | collective-permute-done | bytes 262176 | tf_op jit(solution)/shard_map/ppermute | solution.py:285
  54.8 4.5 %finish_x_0.1 = f32[4,4,2,32,256]{4,3,2,1,0:T(8,128)} custom-call(s32[1]{0:T(128)S(6)} %copy.15.refs_0_, s32[1]{0:T(128)} %collective-permute-done.refs_1_, s32[1]{0:T(128)} %collective-permute-done.1.refs_2_, s32[1]{0:T(128)} %collective-permute-done.2.refs_3_, f32[4,2,32,1024]{3,2,1,0:T(8,128)S(1)} %get-tuple-element.21.refs_4_, ...), custom_call_target="tpu_custom_call" | custom-call | flops 805306368 | bytes 3932176 | tf_op jit(solution)/shard_map/finish_x_0/pallas_call | solution.py:235
  59.3 0.0 all-to-all-done
  59.3 1.0 copy-done.17
  60.3 8.5 %all-to-all-start.3 = ((f32[16,2,32,256]{3,2,1,0:T(8,128)}), f32[16,2,32,256]{3,2,1,0:T(8,128)S(1)}, u32[]{:S(2)}, u32[]{:S(2)}) async-start(f32[16,2,32,256]{3,2,1,0:T(8,128)} %bitcast.4), calls=%async_computation.3 | async-start | bytes 2097152 | tf_op jit(solution)/shard_map/all_to_all | solution.py:313
  68.8 0.0 copy-start.18
  68.8 1.2 %copy-done.18 = f32[16,2,32,256]{3,2,1,0:T(8,128)S(1)} copy-done((f32[16,2,32,256]{3,2,1,0:T(8,128)S(1)}, f32[16,2,32,256]{3,2,1,0:T(8,128)}, u32[]{:S(2)}) %copy-start.18) | copy-done | bytes 1048600
  70.1 3.3 %forward_x_1.1 = (f32[4,2,32,1024]{3,2,1,0:T(8,128)S(1)}, f32[2,32,1024]{2,1,0:T(8,128)S(1)}) custom-call(s32[1]{0:T(128)S(6)} %copy.15.refs_0_, s32[1]{0:T(128)} %collective-permute-done.refs_1_, s32[1]{0:T(128)} %collective-permute-done.1.refs_2_, s32[1]{0:T(128)} %collective-permute-done.2.refs_3_, f32[4,4,2,32,256]{4,3,2,1,0:T(8,128)S(1)} %bitcast.8, ...), custom_call_target="tpu_custom_call" | custom-call | flops 805306368 | bytes 3932176 | tf_op jit(solution)/shard_map/forward_x_1/pallas_call | solution.py:235
  73.4 5.3 %collective-permute-start.3 = (f32[2,32,1024]{2,1,0:T(8,128)S(1)}, f32[2,32,1024]{2,1,0:T(8,128)S(1)}, u32[]{:S(2)}, u32[]{:S(2)}) collective-permute-start(f32[2,32,1024]{2,1,0:T(8,128)S(1)} %get-tuple-element.19), channel_id=1, source_target_pairs={{0,16},{1,17},{2,18},{3,19},{4,20},{5,21},{6,22},{7,23},{8,24},{9,... | collective-permute-start | bytes 786440 | tf_op jit(solution)/shard_map/ppermute | solution.py:285
  78.7 8.2 %collective-permute-done.3.refs_5_ = f32[2,32,1024]{2,1,0:T(8,128)S(1)} collective-permute-done((f32[2,32,1024]{2,1,0:T(8,128)S(1)}, f32[2,32,1024]{2,1,0:T(8,128)S(1)}, u32[]{:S(2)}, u32[]{:S(2)}) %collective-permute-start.3) | collective-permute-done | bytes 262176 | tf_op jit(solution)/shard_map/ppermute | solution.py:285
  87.0 4.5 %finish_x_1.1 = f32[4,4,2,32,256]{4,3,2,1,0:T(8,128)} custom-call(s32[1]{0:T(128)S(6)} %copy.15.refs_0_, s32[1]{0:T(128)} %collective-permute-done.refs_1_, s32[1]{0:T(128)} %collective-permute-done.1.refs_2_, s32[1]{0:T(128)} %collective-permute-done.2.refs_3_, f32[4,2,32,1024]{3,2,1,0:T(8,128)S(1)} %get-tuple-element.18.refs_4_, ...), custom_call_target="tpu_custom_call" | custom-call | flops 805306368 | bytes 3932176 | tf_op jit(solution)/shard_map/finish_x_1/pallas_call | solution.py:235
  91.5 0.0 all-to-all-done.3.r_ref
  91.5 1.0 copy-done.5
  92.5 8.3 %all-to-all-start.1 = ((f32[16,2,32,256]{3,2,1,0:T(8,128)}), f32[16,2,32,256]{3,2,1,0:T(8,128)S(1)}, u32[]{:S(2)}, u32[]{:S(2)}) async-start(f32[16,2,32,256]{3,2,1,0:T(8,128)} %bitcast.2), calls=%async_computation.1 | async-start | bytes 2097152 | tf_op jit(solution)/shard_map/all_to_all | solution.py:313
  100.8 0.0 copy-start.6
  100.8 1.2 %copy-done.6 = f32[16,2,32,256]{3,2,1,0:T(8,128)S(1)} copy-done((f32[16,2,32,256]{3,2,1,0:T(8,128)S(1)}, f32[16,2,32,256]{3,2,1,0:T(8,128)}, u32[]{:S(2)}) %copy-start.6) | copy-done | bytes 1048600
  102.0 0.9 copy-done.16
  102.9 0.6 inverse_y_0.1.even_ref
  103.6 13.4 %all-to-all-done.1.r_ref = f32[16,2,32,256]{3,2,1,0:T(8,128)S(1)} async-done(((f32[16,2,32,256]{3,2,1,0:T(8,128)}), f32[16,2,32,256]{3,2,1,0:T(8,128)S(1)}, u32[]{:S(2)}, u32[]{:S(2)}) %all-to-all-start.1) | async-done | bytes 1048608 | tf_op jit(solution)/shard_map/all_to_all | solution.py:313
  116.9 2.3 %inverse_y_1.1 = f32[2,256,1024]{2,1,0:T(8,128)} custom-call(f32[16,2,32,256]{3,2,1,0:T(8,128)S(1)} %all-to-all-done.1.r_ref, f32[2,256,512]{2,1,0:T(8,128)S(1)} %inverse_y_0.1.even_ref, bf16[512,512]{1,0:T(8,128)(2,1)S(1)} %copy-done.3, bf16[512,512]{1,0:T(8,128)(2,1)S(1)} %copy-done.2), custom_call_target="tpu_custom_call" | custom-call | flops 805306368 | bytes 5242880 | tf_op jit(solution)/shard_map/inverse_y_1/pallas_call | solution.py:235
  (16 shorter events, 0.0 us)
Async XLA Ops:
  0.0 12.8 %collective-permute-start.1 = (s32[1]{0:T(128)}, s32[1]{0:T(128)}, u32[]{:S(2)}, u32[]{:S(2)}) collective-permute-start(s32[1]{0:T(128)} %param.15), channel_id=1, source_target_pairs={{0,8},{4,12},{8,0},{12,4},{1,9},{5,13},{9,1},{13,5},{2,10},{6,14},... | collective-permute-start | bytes 20 | tf_op jit(solution)/shard_map/ppermute | solution.py:257
  3.1 9.8 %collective-permute-start = (s32[1]{0:T(128)}, s32[1]{0:T(128)}, u32[]{:S(2)}, u32[]{:S(2)}) collective-permute-start(s32[1]{0:T(128)} %param.15), channel_id=1, source_target_pairs={{0,4},{4,8},{8,12},{12,0},{1,5},{5,9},{9,13},{13,1},{2,6},{6,10},{... | collective-permute-start | bytes 20 | tf_op jit(solution)/shard_map/ppermute | solution.py:257
  4.6 8.2 %collective-permute-start.2 = (s32[1]{0:T(128)}, s32[1]{0:T(128)}, u32[]{:S(2)}, u32[]{:S(2)}) collective-permute-start(s32[1]{0:T(128)} %param.15), channel_id=1, source_target_pairs={{0,12},{4,0},{8,4},{12,8},{1,13},{5,1},{9,5},{13,9},{2,14},{6,2},{... | collective-permute-start | bytes 20 | tf_op jit(solution)/shard_map/ppermute | solution.py:257
  6.0 1.6 %copy-start = (f32[1,2,256,1024]{3,2,1,0:T(8,128)S(1)}, f32[1,2,256,1024]{3,2,1,0:T(8,128)}, u32[]{:S(2)}) copy-start(f32[1,2,256,1024]{3,2,1,0:T(8,128)} %param.14) | copy-start | bytes 6291460
  7.6 0.9 copy-start.8
  8.5 0.9 copy-start.10
  9.4 0.9 copy-start.12
  10.3 0.9 copy-start.14
  11.2 6.0 %copy-start.1 = (f32[1,2,256,1024]{3,2,1,0:T(8,128)S(1)}, f32[1,2,256,1024]{3,2,1,0:T(8,128)}, u32[]{:S(2)}) copy-start(f32[1,2,256,1024]{3,2,1,0:T(8,128)} %param.14) | copy-start | bytes 6291460
  11.2 6.0 %copy-start.2 = (bf16[512,512]{1,0:T(8,128)(2,1)S(1)}, bf16[512,512]{1,0:T(8,128)(2,1)}, u32[]{:S(2)}) copy-start(bf16[512,512]{1,0:T(8,128)(2,1)} %constant.17.clone.refs_1_.refs_10_.refs_11_) | copy-start | bytes 1572868
  11.2 6.0 %copy-start.3 = (bf16[512,512]{1,0:T(8,128)(2,1)S(1)}, bf16[512,512]{1,0:T(8,128)(2,1)}, u32[]{:S(2)}) copy-start(bf16[512,512]{1,0:T(8,128)(2,1)} %constant.16.clone.refs_0_.refs_9_.refs_10_) | copy-start | bytes 1572868
  11.8 1.0 copy-start.4
  12.8 20.5 %all-to-all-start.2 = ((f32[16,2,32,256]{3,2,1,0:T(8,128)}), f32[16,2,32,256]{3,2,1,0:T(8,128)}, u32[]{:S(2)}, u32[]{:S(2)}) async-start(f32[16,2,32,256]{3,2,1,0:T(8,128)} %copy-done.4), calls=%async_computation.2 | async-start | bytes 2097152 | tf_op jit(solution)/shard_map/all_to_all | solution.py:275
  18.2 1.0 copy-start.7
  19.2 18.4 %copy-start.9 = (bf16[256,256]{1,0:T(8,128)(2,1)S(1)}, bf16[256,256]{1,0:T(8,128)(2,1)}, u32[]{:S(2)}) copy-start(bf16[256,256]{1,0:T(8,128)(2,1)} %constant.15.clone.refs_3_.refs_8_.refs_9_) | copy-start | bytes 393220
  19.2 18.4 %copy-start.11 = (bf16[256,256]{1,0:T(8,128)(2,1)S(1)}, bf16[256,256]{1,0:T(8,128)(2,1)}, u32[]{:S(2)}) copy-start(bf16[256,256]{1,0:T(8,128)(2,1)} %constant.14.clone.refs_2_.refs_7_.refs_8_) | copy-start | bytes 393220
  19.2 18.4 %copy-start.13 = (bf16[256,256]{1,0:T(8,128)(2,1)S(1)}, bf16[256,256]{1,0:T(8,128)(2,1)}, u32[]{:S(2)}) copy-start(bf16[256,256]{1,0:T(8,128)(2,1)} %constant.13.clone.refs_1_.refs_6_.refs_7_) | copy-start | bytes 393220
  19.2 18.4 %copy-start.15 = (bf16[256,256]{1,0:T(8,128)(2,1)S(1)}, bf16[256,256]{1,0:T(8,128)(2,1)}, u32[]{:S(2)}) copy-start(bf16[256,256]{1,0:T(8,128)(2,1)} %constant.12.clone.refs_0_.refs_5_.refs_6_) | copy-start | bytes 393220
  33.3 26.0 %all-to-all-start = ((f32[16,2,32,256]{3,2,1,0:T(8,128)}), f32[16,2,32,256]{3,2,1,0:T(8,128)S(1)}, u32[]{:S(2)}, u32[]{:S(2)}) async-start(f32[16,2,32,256]{3,2,1,0:T(8,128)} %copy-done.7), calls=%async_computation | async-start | bytes 2097152 | tf_op jit(solution)/shard_map/all_to_all | solution.py:275
  42.2 12.5 %collective-permute-start.4 = (f32[2,32,1024]{2,1,0:T(8,128)S(1)}, f32[2,32,1024]{2,1,0:T(8,128)S(1)}, u32[]{:S(2)}, u32[]{:S(2)}) collective-permute-start(f32[2,32,1024]{2,1,0:T(8,128)S(1)} %get-tuple-element.22), channel_id=1, source_target_pairs={{0,16},{1,17},{2,18},{3,19},{4,20},{5,21},{6,22},{7,23},{8,24},{9,... | collective-permute-start | bytes 786440 | tf_op jit(solution)/shard_map/ppermute | solution.py:285
  59.3 1.0 copy-start.17
  60.3 31.2 %all-to-all-start.3 = ((f32[16,2,32,256]{3,2,1,0:T(8,128)}), f32[16,2,32,256]{3,2,1,0:T(8,128)S(1)}, u32[]{:S(2)}, u32[]{:S(2)}) async-start(f32[16,2,32,256]{3,2,1,0:T(8,128)} %bitcast.4), calls=%async_computation.3 | async-start | bytes 2097152 | tf_op jit(solution)/shard_map/all_to_all | solution.py:313
  68.8 1.2 %copy-start.18 = (f32[16,2,32,256]{3,2,1,0:T(8,128)S(1)}, f32[16,2,32,256]{3,2,1,0:T(8,128)}, u32[]{:S(2)}) copy-start(f32[16,2,32,256]{3,2,1,0:T(8,128)} %copy-done.17) | copy-start | bytes 3145732
  73.4 13.6 %collective-permute-start.3 = (f32[2,32,1024]{2,1,0:T(8,128)S(1)}, f32[2,32,1024]{2,1,0:T(8,128)S(1)}, u32[]{:S(2)}, u32[]{:S(2)}) collective-permute-start(f32[2,32,1024]{2,1,0:T(8,128)S(1)} %get-tuple-element.19), channel_id=1, source_target_pairs={{0,16},{1,17},{2,18},{3,19},{4,20},{5,21},{6,22},{7,23},{8,24},{9,... | collective-permute-start | bytes 786440 | tf_op jit(solution)/shard_map/ppermute | solution.py:285
  91.5 1.0 copy-start.5
  92.5 24.5 %all-to-all-start.1 = ((f32[16,2,32,256]{3,2,1,0:T(8,128)}), f32[16,2,32,256]{3,2,1,0:T(8,128)S(1)}, u32[]{:S(2)}, u32[]{:S(2)}) async-start(f32[16,2,32,256]{3,2,1,0:T(8,128)} %bitcast.2), calls=%async_computation.1 | async-start | bytes 2097152 | tf_op jit(solution)/shard_map/all_to_all | solution.py:313
  100.8 1.2 %copy-start.6 = (f32[16,2,32,256]{3,2,1,0:T(8,128)S(1)}, f32[16,2,32,256]{3,2,1,0:T(8,128)}, u32[]{:S(2)}) copy-start(f32[16,2,32,256]{3,2,1,0:T(8,128)} %copy-done.5) | copy-start | bytes 3145732
  102.0 0.9 copy-start.16
where the time goes:
time: 120 us; the launch traced here: 119 us
  waiting for transfers between devices  43.8 us (36%)
  starting transfers between devices  40.7 us (34%)
  Pallas kernels  21.6 us (18%)
  local copies, waits for them, and re-layouts  12.4 us (10%)
    pallas_call x8, Pallas kernels, call(): pl.pallas_call(kernel, name=name, in_specs=[scalar] * scalars + [space] *...  21.6 us
    all_to_all x2, starting transfers between devices, on_device(): lax.all_to_all(back, group, split_axis=0, concat_axis=0, tiled=True)  16.9 us
    ppermute x2, waiting for transfers between devices, on_device(): carry = lax.ppermute(last, 'block', [(b, b + 1) for b in range(blocks - 1)])  16.3 us
    all_to_all x2, waiting for transfers between devices, on_device(): lax.all_to_all(sent[odd], group, split_axis=0, concat_axis=0, tiled=True)  14.1 us
    all_to_all x2, waiting for transfers between devices, on_device(): lax.all_to_all(back, group, split_axis=0, concat_axis=0, tiled=True)  13.4 us
    unnamed x38, local copies, waits for them, and re-layouts  12.4 us
    ppermute x2, starting transfers between devices, on_device(): carry = lax.ppermute(last, 'block', [(b, b + 1) for b in range(blocks - 1)])  9.8 us
    all_to_all x2, starting transfers between devices, on_device(): lax.all_to_all(sent[odd], group, split_axis=0, concat_axis=0, tiled=True)  8.01 us
  transfers between devices with their start and end apart: 9, of which 4 were waited for; matrix products, arithmetic and copies ran while one was open for 0% of the time, Pallas kernels for 16%

commit v1 on v0

v1 whole, which is shorter than its diff:
```python
import functools
import math

import jax
import jax.numpy as jnp
import numpy as np
from jax import lax
from jax.experimental import pallas as pl
from jax.experimental.pallas import tpu as pltpu
from jax.sharding import Mesh
from jax.sharding import PartitionSpec as P


phase_rate = 0.004
f32 = jnp.float32
bf16 = jnp.bfloat16
NN = (((1,), (0,)), ((), ()))
NT = (((1,), (1,)), ((), ()))
TN = (((0,), (0,)), ((), ()))
SIN = (3.14159274, -5.1677103, 2.55007744, -0.598291218, 0.0776574388)
COS = (1.0, -4.93480206, 4.05870914, -1.335212, 0.23493728, -0.0243962663)


def cas_tables(length):
    quarter = length // 4
    m = np.arange(quarter, dtype=np.int64)
    j = np.arange(quarter, dtype=np.int64)

    def cas(k, sign=1):
        angle = sign * 2.0 * np.pi * ((k[:, None] * j[None, :]) % length) / length
        return np.cos(angle) + np.sin(angle)

    odd = np.block(
        [
            [cas(4 * m + 1), cas(4 * m + 1, -1)],
            [cas(4 * m + 3), -cas(4 * m + 3, -1)],
        ]
    )
    tables = []
    for table in (cas(4 * m), cas(4 * m + 2), odd):
        table = table.astype(np.float32)
        high = table.astype(jnp.bfloat16)
        low = (table - high.astype(np.float32)).astype(jnp.bfloat16)
        tables += [high, low]
    return tables


def halves(value):
    high = value.astype(bf16)
    return high, (value - high.astype(f32)).astype(bf16)


def product(left, right, form):
    dot = functools.partial(lax.dot_general, dimension_numbers=form, preferred_element_type=f32)
    return dot(left[0], right[0]) + dot(left[0], right[1]) + dot(left[1], right[0])


def fold(parts):
    even, cross = parts[0] + parts[2], parts[1] + parts[3]
    return even + cross, even - cross


def fold_odd(parts):
    return jnp.concatenate([parts[0] - parts[2], parts[1] - parts[3]], axis=-1)


def signed_wave(indices, length):
    return jnp.where(indices < length // 2, indices, indices - length).astype(f32)


def wave_at(spot, length):
    quarter = length // 4
    block = spot // quarter
    return 4 * (spot % quarter) + jnp.where(block == 1, 2, jnp.where(block == 2, 1, block))


def modulus_at(start, start_x, shape, length_x, length_y):
    place_y = start + lax.broadcasted_iota(jnp.int32, shape, 0)
    place_x = start_x + lax.broadcasted_iota(jnp.int32, shape, 1)
    wave_y = signed_wave(wave_at(place_y, length_y), length_y)
    wave_x = signed_wave(wave_at(place_x, length_x), length_x)
    return jnp.sqrt(wave_x * wave_x + wave_y * wave_y)


def turn(angle):
    part = angle - jnp.round(angle)
    square = part * part
    sine = jnp.full_like(square, SIN[-1])
    for factor in SIN[-2::-1]:
        sine = sine * square + factor
    sine = sine * part
    cosine = jnp.full_like(square, COS[-1])
    for factor in COS[-2::-1]:
        cosine = cosine * square + factor
    return 1.0 - 2.0 * sine * sine, 2.0 * sine * cosine


def place(odd, rows, length_y):
    point = lax.axis_index("point")
    band = point * lax.axis_size("space") + lax.axis_index("space")
    return odd * (length_y // 2) + band * rows, point


def rate_of(n, point, count_refs):
    points = len(count_refs)
    shift = lax.rem(point + points - n, points)
    count = count_refs[0][0]
    for d in range(1, points):
        count = jnp.where(shift == d, count_refs[d][0], count)
    return count.astype(f32) * (phase_rate / (2.0 * math.pi))


def copy_in(pairs, sems):
    copies = [pltpu.make_async_copy(source, target, sems.at[i]) for i, (source, target) in enumerate(pairs)]
    for copy in copies:
        copy.start()
    return copies


def copy_out(copies, source, target, sem):
    copies.append(pltpu.make_async_copy(source, target, sem))
    copies[-1].start()


def wait_all(copies):
    for copy in copies:
        copy.wait()


def forward_y(odd, x_hbm, *refs):
    number = (len(refs) - 5) // 2
    tables_hbm, (out_hbm, x_ref, out), refs = refs[:number], refs[number : number + 3], refs[number + 3 :]
    table_refs, (sems, out_sems) = refs[:number], refs[number:]
    pairs = [(x_hbm.at[0], x_ref.at[0])] + list(zip(tables_hbm, table_refs)) + [(x_hbm.at[1], x_ref.at[1])]
    copies = copy_in(pairs, sems)
    wait_all(copies[:-1])
    tables = [ref[...] for ref in table_refs]
    quarter = x_ref.shape[-1] // 4
    _, bands, rows, slab = out.shape
    stores = []
    for part in range(2):
        if part:
            copies[-1].wait()
        pieces = [x_ref[part, :, q * quarter : (q + 1) * quarter] for q in range(4)]
        if odd:
            result = product(tables, halves(fold_odd(pieces)), NT)
            out[part] = result.reshape(bands, rows, slab)
        else:
            total, alternate = fold(pieces)
            half = bands // 2
            out[part, :half] = product(tables[:2], halves(total), NT).reshape(half, rows, slab)
            out[part, half:] = product(tables[2:], halves(alternate), NT).reshape(half, rows, slab)
        copy_out(stores, out.at[part], out_hbm.at[:, part], out_sems.at[part])
    wait_all(stores)


def rotations(odd, length_x, length_y, points, *refs):
    count_refs, (out_hbm, out, sems) = refs[:points], refs[points:]
    _, _, _, rows, quarter = out.shape
    block = math.gcd(rows, 8)
    start, point = place(odd, rows, length_y)
    rates = [rate_of(n, point, count_refs) for n in range(points)]
    stores = []
    for q in range(4):

        def step(index, _):
            here = pl.ds(pl.multiple_of(index * block, block), block)
            modulus = modulus_at(start + index * block, q * quarter, (block, quarter), length_x, length_y)
            for n in range(points):
                out[q, 0, n, here, :], out[q, 1, n, here, :] = turn(rates[n] * modulus)
            return 0

        lax.fori_loop(0, rows // block, step, 0)
        copy_out(stores, out.at[q], out_hbm.at[q], sems.at[q])
    wait_all(stores)


def forward_x(r_ref, turns_hbm, *refs):
    tables, refs = [ref[...] for ref in refs[:-6]], refs[-6:]
    spectra_hbm, last, turns, spectra, sems, out_sems = refs
    points, spaces, _, rows, slab = r_ref.shape
    quarter = spaces * slab // 4
    count = points * 2 * rows
    copies = copy_in([(turns_hbm.at[q], turns.at[q]) for q in range(4)], sems)
    pieces = [r_ref[:, s].reshape(count, slab) for s in range(spaces)]
    if spaces != 4:
        whole = jnp.concatenate(pieces, axis=-1)
        pieces = [whole[:, q * quarter : (q + 1) * quarter] for q in range(4)]
    total, alternate = fold(pieces)
    stores = []

    def finish(q, result):
        result = result.reshape(points, 2, rows, quarter)
        spectra[q] = result
        copy_out(stores, spectra.at[q], spectra_hbm.at[q], out_sems.at[q])
        copies[q].wait()
        first, second = result[0, 0], result[0, 1]
        for n in range(1, points):
            cosine, sine = turns[q, 0, n], turns[q, 1, n]
            first, second = (
                cosine * first + sine * second + result[n, 0],
                cosine * second - sine * first + result[n, 1],
            )
        here = slice(q * quarter, (q + 1) * quarter)
        last[0, :, here] = first
        last[1, :, here] = second

    finish(0, product(halves(total), tables[:2], NT))
    finish(1, product(halves(alternate), tables[2:4], NT))
    mixed = product(halves(fold_odd(pieces)), tables[4:], NT)
    finish(2, mixed[:, :quarter])
    finish(3, mixed[:, quarter:])
    wait_all(stores)


def finish_x(scaling, spectra_hbm, carry, turns_hbm, *refs):
    tables, refs = [ref[...] for ref in refs[:-7]], refs[-7:]
    out_hbm, out, spectra, turns, states, sems, out_sems = refs
    spaces, points, _, rows, slab = out.shape
    quarter = spaces * slab // 4
    count = points * 2 * rows
    pairs = []
    for q in range(4):
        pairs += [(spectra_hbm.at[q], spectra.at[q]), (turns_hbm.at[q], turns.at[q])]
    copies = copy_in(pairs, sems)
    for q in range(4):
        wait_all(copies[2 * q : 2 * q + 2])
        here = slice(q * quarter, (q + 1) * quarter)
        first, second = carry[0, :, here], carry[1, :, here]
        for n in range(points):
            cosine, sine = turns[q, 0, n], turns[q, 1, n]
            first, second = (
                cosine * first + sine * second + spectra[q, n, 0],
                cosine * second - sine * first + spectra[q, n, 1],
            )
            states[n, 0, :, here] = first * scaling
            states[n, 1, :, here] = second * scaling
    total = product(halves(states[..., :quarter].reshape(count, quarter)), tables[:2], NN)
    alternate = product(halves(states[..., quarter : 2 * quarter].reshape(count, quarter)), tables[2:4], NN)
    mixed = product(halves(states[..., 2 * quarter :].reshape(count, 2 * quarter)), tables[4:], NN)
    plus, minus = total + alternate, total - alternate
    straight, crossed = mixed[:, :quarter], mixed[:, quarter:]
    results = [plus + straight, minus + crossed, plus - straight, minus - crossed]
    if spaces != 4:
        whole = jnp.concatenate(results, axis=-1)
        results = [whole[:, s * slab : (s + 1) * slab] for s in range(spaces)]
    stores = []
    for s in range(spaces):
        out[s] = results[s].reshape(points, 2, rows, slab)
        copy_out(stores, out.at[s], out_hbm.at[:, s], out_sems.at[s])
    wait_all(stores)


def inverse_y_even(r_hbm, *refs):
    tables, (out_hbm, r_ref, out, in_sems, sems) = [ref[...] for ref in refs[:-5]], refs[-5:]
    wait_all(copy_in([(r_hbm, r_ref)], in_sems))
    bands, _, rows, slab = r_ref.shape
    half = bands // 2
    stores = []
    for part in range(2):
        total = product(halves(r_ref[:half, part].reshape(half * rows, slab)), tables[:2], TN)
        alternate = product(halves(r_ref[half:, part].reshape(half * rows, slab)), tables[2:], TN)
        out[part] = jnp.concatenate([total + alternate, total - alternate], axis=-1)
        copy_out(stores, out.at[part], out_hbm.at[part], sems.at[part])
    wait_all(stores)


def inverse_y_odd(r_ref, even_hbm, *refs):
    tables, (out_hbm, even, out, sems, out_sems) = [ref[...] for ref in refs[:-5]], refs[-5:]
    bands, _, rows, slab = r_ref.shape
    width = even.shape[-1]
    copies = copy_in([(even_hbm.at[part], even.at[part]) for part in range(2)], sems)
    stores = []
    for part in range(2):
        mixed = product(halves(r_ref[:, part].reshape(bands * rows, slab)), tables, TN)
        copies[part].wait()
        out[part, :, :width] = even[part] + mixed
        out[part, :, width:] = even[part] - mixed
        copy_out(stores, out.at[part], out_hbm.at[part], out_sems.at[part])
    wait_all(stores)


def call(kernel, operands, outs, flops, spaces, out_spaces, scratch=(), limit=20):
    shapes = [space(shape, f32) for shape, space in zip(outs, out_spaces)]
    traffic = sum(math.prod(x.shape) * x.dtype.itemsize for x in operands)
    traffic += sum(4 * math.prod(shape) for shape in outs)
    many = len(outs) > 1
    specs = [pl.BlockSpec(memory_space=space) for space in out_spaces]
    operands = [pltpu.with_memory_space_constraint(x, s) if s == pltpu.HBM else x for x, s in zip(operands, spaces)]
    return pl.pallas_call(
        kernel,
        in_specs=[pl.BlockSpec(memory_space=space) for space in spaces],
        out_specs=specs if many else specs[0],
        out_shape=shapes if many else shapes[0],
        scratch_shapes=list(scratch),
        cost_estimate=pl.CostEstimate(flops=flops, bytes_accessed=traffic, transcendentals=0),
        compiler_params=pltpu.CompilerParams(vmem_limit_bytes=limit * 2**20),
    )(*operands)


def on_device(residual, counts):
    slab, length_y = residual.shape[2:]
    blocks, points, spaces = (lax.axis_size(name) for name in ("block", "point", "space"))
    length_x = slab * spaces
    group = ("point", "space")
    bands = points * spaces
    rows = length_y // (2 * bands)
    quarter = length_x // 4
    table_x, tables_y = (cas_tables(length) for length in (length_x, length_y))
    tables_y = (tables_y[:4], tables_y[4:])
    near = [counts]
    for d in range(1, points):
        near.append(lax.ppermute(counts, "point", [(i, (i + d) % points) for i in range(points)]))
    flops_y = [3 * 4 * slab * (length_y // 2) * (length_y // wide) for wide in (4, 2)]
    flops_x = 3 * 4 * rows * points * length_x * 3 * length_x // 8
    vmem, smem, hbm, sems = pltpu.VMEM, pltpu.SMEM, pltpu.HBM, pltpu.SemaphoreType.DMA
    spectra_shape = (4, points, 2, rows, quarter)
    turns_shape = (4, 2, points, rows, quarter)

    sent = []
    for odd in range(2):
        tables = tables_y[odd]
        sent.append(
            call(
                functools.partial(forward_y, odd),
                [residual[0], *tables],
                [(bands, 2, rows, slab)],
                flops_y[odd],
                [hbm] * (1 + len(tables)),
                [hbm],
                scratch=[
                    vmem(residual.shape[1:], f32),
                    vmem((2, bands, rows, slab), f32),
                    *[vmem(table.shape, bf16) for table in tables],
                    sems((2 + len(tables),)),
                    sems((2,)),
                ],
            )
        )
    sent[0], *near = lax.optimization_barrier((sent[0], *near))
    turns = [
        call(
            functools.partial(rotations, odd, length_x, length_y, points),
            near,
            [turns_shape],
            40 * points * rows * length_x,
            [smem] * points,
            [hbm],
            scratch=[vmem(turns_shape, f32), sems((4,))],
        )
        for odd in range(2)
    ]
    spectra, carry = [None] * 2, [None] * 2
    for odd in range(2):
        arrived = lax.all_to_all(sent[odd], group, split_axis=0, concat_axis=0, tiled=True)
        spectra[odd], last = call(
            forward_x,
            [arrived.reshape(points, spaces, 2, rows, slab), turns[odd], *table_x],
            [spectra_shape, (2, rows, length_x)],
            flops_x,
            [vmem, hbm] + [vmem] * len(table_x),
            [hbm, vmem],
            scratch=[
                vmem(turns_shape, f32),
                vmem(spectra_shape, f32),
                sems((4,)),
                sems((4,)),
            ],
        )
        carry[odd] = lax.ppermute(last, "block", [(b, b + 1) for b in range(blocks - 1)])
        if blocks > 2:
            total = sum(near)[0].astype(f32) * (phase_rate / (2.0 * math.pi))
            span = lax.ppermute(total, "block", [(b, b + 1) for b in range(blocks - 1)])
            modulus = modulus_at(place(odd, rows, length_y)[0], 0, (rows, length_x), length_x, length_y)
            reach = 1
            while reach < blocks - 1:
                steps = [(b, b + reach) for b in range(blocks - reach)]
                further = lax.ppermute(carry[odd], "block", steps)
                cosine, sine = turn(span * modulus)
                carry[odd] = carry[odd] + jnp.stack(
                    [
                        cosine * further[0] + sine * further[1],
                        cosine * further[1] - sine * further[0],
                    ]
                )
                span = span + lax.ppermute(span, "block", steps)
                reach *= 2
    carry[0], spectra[1] = lax.optimization_barrier((carry[0], spectra[1]))
    solved = []
    for odd in range(2):
        back = call(
            functools.partial(finish_x, 1.0 / (length_x * length_y)),
            [spectra[odd], carry[odd], turns[odd], *table_x],
            [(points, spaces, 2, rows, slab)],
            flops_x,
            [hbm, vmem, hbm] + [vmem] * len(table_x),
            [hbm],
            scratch=[
                vmem((spaces, points, 2, rows, slab), f32),
                vmem(spectra_shape, f32),
                vmem(turns_shape, f32),
                vmem((points, 2, rows, length_x), f32),
                sems((8,)),
                sems((spaces,)),
            ],
        )
        back = back.reshape(bands, 2, rows, slab)
        solved.append(lax.all_to_all(back, group, split_axis=0, concat_axis=0, tiled=True))
    half = (2, slab, length_y // 2)
    even = call(
        inverse_y_even,
        [solved[0], *tables_y[0]],
        [half],
        flops_y[0],
        [hbm] + [vmem] * len(tables_y[0]),
        [hbm],
        scratch=[vmem((bands, 2, rows, slab), f32), vmem(half, f32), sems((1,)), sems((2,))],
    )
    fields = call(
        inverse_y_odd,
        [solved[1], even, *tables_y[1]],
        [(2, slab, length_y)],
        flops_y[1],
        [vmem, hbm] + [vmem] * len(tables_y[1]),
        [hbm],
        scratch=[vmem(half, f32), vmem((2, slab, length_y), f32), sems((2,)), sems((2,))],
    )
    return fields[None]


def solution(mesh):
    times, spaces = mesh.shape["tm"], mesh.shape["space"]
    points = 4 if times % 4 == 0 else 1
    inner = Mesh(mesh.devices.reshape(times // points, points, spaces), ("block", "point", "space"))
    when = ("block", "point")
    return jax.shard_map(
        on_device,
        mesh=inner,
        in_specs=(P(when, None, "space", None), P(when)),
        out_specs=P(when, None, "space", None),
        check_vma=False,
    )
```

time: 120 us -> 113 us (0.942)
  Pallas kernels: 21.6 us -> 32.8 us
  local copies, waits for them, and re-layouts: 12.4 us -> 3.22 us
  waiting for transfers between devices: 43.8 us -> 37.9 us
  starting transfers between devices: 40.7 us -> 37.2 us
    pallas_call x8 -> x10, Pallas kernels: 21.6 us -> 32.8 us  [call(): pl.pallas_call(kernel, in_specs=[pl.BlockSpec(memory_space=space) for spa...]
    unnamed x38 -> x18, local copies, waits for them, and re-layouts: 12.4 us -> 3.22 us
    ppermute x2, waiting for transfers between devices: 16.3 us -> 12.8 us  [on_device(): lax.ppermute(last, 'block', [(b, b + 1) for b in range(blocks - 1)])]
    all_to_all x2, starting transfers between devices: 16.9 us -> 13.8 us  [on_device(): lax.all_to_all(back, group, split_axis=0, concat_axis=0, tiled=True)]
    all_to_all x2, waiting for transfers between devices: 14.1 us -> 11.7 us  [on_device(): lax.all_to_all(sent[odd], group, split_axis=0, concat_axis=0, tiled=True)]
  transfers between devices with their start and end apart: 9 -> 9, of which waited for: 4 -> 3; matrix products, arithmetic and copies ran while one was open for 0% -> 0% of each run, Pallas kernels for 16% -> 23%
where the time goes in v1:
time: 113 us; the launch traced here: 112 us
  waiting for transfers between devices  37.9 us (34%)
  starting transfers between devices  37.2 us (33%)
  Pallas kernels  32.8 us (29%)
  local copies, waits for them, and re-layouts  3.22 us (3%)
    pallas_call x10, Pallas kernels, call(): pl.pallas_call(kernel, in_specs=[pl.BlockSpec(memory_space=space) for spa...  32.8 us
    all_to_all x2, starting transfers between devices, on_device(): lax.all_to_all(back, group, split_axis=0, concat_axis=0, tiled=True)  13.8 us
    all_to_all x2, waiting for transfers between devices, on_device(): lax.all_to_all(back, group, split_axis=0, concat_axis=0, tiled=True)  13.5 us
    ppermute x2, waiting for transfers between devices, on_device(): lax.ppermute(last, 'block', [(b, b + 1) for b in range(blocks - 1)])  12.8 us
    all_to_all x2, waiting for transfers between devices, on_device(): lax.all_to_all(sent[odd], group, split_axis=0, concat_axis=0, tiled=True)  11.7 us
    ppermute x2, starting transfers between devices, on_device(): lax.ppermute(last, 'block', [(b, b + 1) for b in range(blocks - 1)])  9.82 us
    all_to_all x2, starting transfers between devices, on_device(): lax.all_to_all(sent[odd], group, split_axis=0, concat_axis=0, tiled=True)  7.58 us
    ppermute x3, starting transfers between devices, on_device(): lax.ppermute(counts, 'point', [(i, (i + d) % points) for i in range(point...  5.98 us
  transfers between devices with their start and end apart: 9, of which 3 were waited for; matrix products, arithmetic and copies ran while one was open for 0% of the time, Pallas kernels for 23%

profile of v1, /device:TPU:0, one launch (start us, length us, event | category | flops | bytes accessed | tf_op | source)
XLA Modules:
  0.0 112.0 jit_solution(2977025927489018228)
XLA Ops:
  0.0 3.1 %collective-permute-start.1 = (s32[1]{0:T(128)}, s32[1]{0:T(128)}, u32[]{:S(2)}, u32[]{:S(2)}) collective-permute-start(s32[1]{0:T(128)} %param.15), channel_id=1, source_target_pairs={{0,8},{4,12},{8,0},{12,4},{1,9},{5,13},{9,1},{13,5},{2,10},{6,14},... | collective-permute-start | bytes 20 | tf_op jit(solution)/shard_map/ppermute | solution.py:313
  3.1 1.5 %collective-permute-start = (s32[1]{0:T(128)}, s32[1]{0:T(128)}, u32[]{:S(2)}, u32[]{:S(2)}) collective-permute-start(s32[1]{0:T(128)} %param.15), channel_id=1, source_target_pairs={{0,4},{4,8},{8,12},{12,0},{1,5},{5,9},{9,13},{13,1},{2,6},{6,10},{... | collective-permute-start | bytes 20 | tf_op jit(solution)/shard_map/ppermute | solution.py:313
  4.6 1.4 %collective-permute-start.2 = (s32[1]{0:T(128)}, s32[1]{0:T(128)}, u32[]{:S(2)}, u32[]{:S(2)}) collective-permute-start(s32[1]{0:T(128)} %param.15), channel_id=1, source_target_pairs={{0,12},{4,0},{8,4},{12,8},{1,13},{5,1},{9,5},{13,9},{2,14},{6,2},{... | collective-permute-start | bytes 20 | tf_op jit(solution)/shard_map/ppermute | solution.py:313
  6.0 3.1 %shard_map.136 = f32[16,2,32,256]{3,2,1,0:T(8,128)} custom-call(f32[2,256,1024]{2,1,0:T(8,128)} %bitcast.8, bf16[256,256]{1,0:T(8,128)(2,1)} %constant.12.clone.refs_0_, bf16[256,256]{1,0:T(8,128)(2,1)} %constant.13.clone.refs_1_, bf16[256,256]{1,0:T(8,128)(2,1)} %constant.14.clone.refs_2_, bf16[256,256]{1,0:T(8,128)(2,1)} %constant.15.clone.refs_3_), custom_call_target="tpu_custom_call" | custom-call | flops 402653184 | bytes 3670016 | tf_op jit(solution)/shard_map/pallas_call | solution.py:290
  9.0 0.0 collective-permute-done.1.refs_2_
  9.1 0.0 collective-permute-done.refs_1_
  9.1 0.0 collective-permute-done.2.refs_3_
  9.1 3.9 %all-to-all-start = ((f32[16,2,32,256]{3,2,1,0:T(8,128)}), f32[16,2,32,256]{3,2,1,0:T(8,128)S(1)}, u32[]{:S(2)}, u32[]{:S(2)}) async-start(f32[16,2,32,256]{3,2,1,0:T(8,128)} %shard_map.136), calls=%async_computation | async-start | bytes 2097152 | tf_op jit(solution)/shard_map/all_to_all | solution.py:355
  13.0 4.4 %shard_map.139 = f32[16,2,32,256]{3,2,1,0:T(8,128)} custom-call(f32[2,256,1024]{2,1,0:T(8,128)} %bitcast.9, bf16[512,512]{1,0:T(8,128)(2,1)} %constant.16.clone.refs_4_.refs_0_, bf16[512,512]{1,0:T(8,128)(2,1)} %constant.17.clone.refs_5_.refs_1_), custom_call_target="tpu_custom_call" | custom-call | flops 805306368 | bytes 4194304 | tf_op jit(solution)/shard_map/pallas_call | solution.py:290
  17.4 0.0 copy-start
  17.4 0.0 copy-start.1
  17.4 0.0 copy-start.2
  17.4 0.0 copy-start.3
  17.4 0.0 copy-start.4
  17.4 0.0 copy-start.5
  17.4 11.7 %all-to-all-done = f32[16,2,32,256]{3,2,1,0:T(8,128)S(1)} async-done(((f32[16,2,32,256]{3,2,1,0:T(8,128)}), f32[16,2,32,256]{3,2,1,0:T(8,128)S(1)}, u32[]{:S(2)}, u32[]{:S(2)}) %all-to-all-start) | async-done | bytes 1048608 | tf_op jit(solution)/shard_map/all_to_all | solution.py:355
  29.1 0.0 copy-start.6
  29.1 1.0 copy-done.6
  30.1 3.7 %all-to-all-start.1 = ((f32[16,2,32,256]{3,2,1,0:T(8,128)}), f32[16,2,32,256]{3,2,1,0:T(8,128)S(1)}, u32[]{:S(2)}, u32[]{:S(2)}) async-start(f32[16,2,32,256]{3,2,1,0:T(8,128)} %shard_map.139), calls=%async_computation.1 | async-start | bytes 2097152 | tf_op jit(solution)/shard_map/all_to_all | solution.py:355
  34.4 3.3 %shard_map.137.turns_hbm = f32[4,2,4,32,256]{4,3,2,1,0:T(8,128)} custom-call(s32[1]{0:T(128)S(6)} %copy.15.refs_0_, s32[1]{0:T(128)} %collective-permute-done.refs_1_, s32[1]{0:T(128)} %collective-permute-done.1.refs_2_, s32[1]{0:T(128)} %collective-permute-done.2.refs_3_), custom_call_target="tpu_custom_call" | custom-call | flops 5242880 | bytes 1048592 | tf_op jit(solution)/shard_map/pallas_call | solution.py:290
  37.8 0.0 copy-done
  37.8 0.0 copy-done.1
  37.8 0.0 copy-done.2
  37.8 0.0 copy-done.3
  37.8 0.0 copy-done.4
  37.8 0.0 copy-done.5
  37.9 0.0 copy-start.7
  37.9 1.2 %copy-done.7 = f32[16,2,32,256]{3,2,1,0:T(8,128)S(1)} copy-done((f32[16,2,32,256]{3,2,1,0:T(8,128)S(1)}, f32[16,2,32,256]{3,2,1,0:T(8,128)}, u32[]{:S(2)}) %copy-start.7) | copy-done | bytes 1048600
  39.1 2.9 %shard_map.138 = (f32[4,4,2,32,256]{4,3,2,1,0:T(8,128)}, f32[2,32,1024]{2,1,0:T(8,128)S(1)}) custom-call(f32[4,4,2,32,256]{4,3,2,1,0:T(8,128)S(1)} %bitcast.7, f32[4,2,4,32,256]{4,3,2,1,0:T(8,128)} %shard_map.137.turns_hbm, bf16[256,256]{1,0:T(8,128)(2,1)S(1)} %copy-done.5, bf16[256,256]{1,0:T(8,128)(2,1)S(1)} %copy-done.4, bf16[256,256]{1,0:T(8,128)(2,1)S(1)} %copy-done.3, ...), custom_call_target="tpu_custom_call" | custom-call | flops 603979776 | bytes 4980736 | tf_op jit(solution)/shard_map/pallas_call | solution.py:290
  42.0 4.5 %collective-permute-start.3 = (f32[2,32,1024]{2,1,0:T(8,128)S(1)}, f32[2,32,1024]{2,1,0:T(8,128)S(1)}, u32[]{:S(2)}, u32[]{:S(2)}) collective-permute-start(f32[2,32,1024]{2,1,0:T(8,128)S(1)} %get-tuple-element.21), channel_id=1, source_target_pairs={{0,16},{1,17},{2,18},{3,19},{4,20},{5,21},{6,22},{7,23},{8,24},{9,... | collective-permute-start | bytes 786440 | tf_op jit(solution)/shard_map/ppermute | solution.py:370
  46.6 3.4 %shard_map.140.turns_hbm = f32[4,2,4,32,256]{4,3,2,1,0:T(8,128)} custom-call(s32[1]{0:T(128)S(6)} %copy.15.refs_0_, s32[1]{0:T(128)} %collective-permute-done.refs_1_, s32[1]{0:T(128)} %collective-permute-done.1.refs_2_, s32[1]{0:T(128)} %collective-permute-done.2.refs_3_), custom_call_target="tpu_custom_call" | custom-call | flops 5242880 | bytes 1048592 | tf_op jit(solution)/shard_map/pallas_call | solution.py:290
  49.9 0.0 all-to-all-done.1
  49.9 3.0 %shard_map.141 = (f32[4,4,2,32,256]{4,3,2,1,0:T(8,128)}, f32[2,32,1024]{2,1,0:T(8,128)S(1)}) custom-call(f32[4,4,2,32,256]{4,3,2,1,0:T(8,128)S(1)} %bitcast.6, f32[4,2,4,32,256]{4,3,2,1,0:T(8,128)} %shard_map.140.turns_hbm, bf16[256,256]{1,0:T(8,128)(2,1)S(1)} %copy-done.5, bf16[256,256]{1,0:T(8,128)(2,1)S(1)} %copy-done.4, bf16[256,256]{1,0:T(8,128)(2,1)S(1)} %copy-done.3, ...), custom_call_target="tpu_custom_call" | custom-call | flops 603979776 | bytes 4980736 | tf_op jit(solution)/shard_map/pallas_call | solution.py:290
  52.9 0.0 collective-permute-done.3.carry
  52.9 3.4 %shard_map.143 = f32[4,4,2,32,256]{4,3,2,1,0:T(8,128)} custom-call(f32[4,4,2,32,256]{4,3,2,1,0:T(8,128)} %get-tuple-element.25.spectra_hbm, f32[2,32,1024]{2,1,0:T(8,128)S(1)} %collective-permute-done.3.carry, f32[4,2,4,32,256]{4,3,2,1,0:T(8,128)} %shard_map.137.turns_hbm, bf16[256,256]{1,0:T(8,128)(2,1)S(1)} %copy-done.5, bf16[256,256]{1,0:T(8,128)(2,1)S(1)} %copy-done.4, ...), custom_call_target="tpu_custom_call" | custom-call | flops 603979776 | bytes 4980736 | tf_op jit(solution)/shard_map/pallas_call | solution.py:290
  56.3 10.1 %all-to-all-start.3 = ((f32[16,2,32,256]{3,2,1,0:T(8,128)}), f32[16,2,32,256]{3,2,1,0:T(8,128)S(1)}, u32[]{:S(2)}, u32[]{:S(2)}) async-start(f32[16,2,32,256]{3,2,1,0:T(8,128)} %bitcast.10), calls=%async_computation.3 | async-start | bytes 2097152 | tf_op jit(solution)/shard_map/all_to_all | solution.py:408
  66.4 5.3 %collective-permute-start.4 = (f32[2,32,1024]{2,1,0:T(8,128)S(1)}, f32[2,32,1024]{2,1,0:T(8,128)S(1)}, u32[]{:S(2)}, u32[]{:S(2)}) collective-permute-start(f32[2,32,1024]{2,1,0:T(8,128)S(1)} %get-tuple-element.24), channel_id=1, source_target_pairs={{0,16},{1,17},{2,18},{3,19},{4,20},{5,21},{6,22},{7,23},{8,24},{9,... | collective-permute-start | bytes 786440 | tf_op jit(solution)/shard_map/ppermute | solution.py:370
  71.7 12.8 %collective-permute-done.4.carry = f32[2,32,1024]{2,1,0:T(8,128)S(1)} collective-permute-done((f32[2,32,1024]{2,1,0:T(8,128)S(1)}, f32[2,32,1024]{2,1,0:T(8,128)S(1)}, u32[]{:S(2)}, u32[]{:S(2)}) %collective-permute-start.4) | collective-permute-done | bytes 262176 | tf_op jit(solution)/shard_map/ppermute | solution.py:370
  84.5 3.4 %shard_map.142 = f32[4,4,2,32,256]{4,3,2,1,0:T(8,128)} custom-call(f32[4,4,2,32,256]{4,3,2,1,0:T(8,128)} %get-tuple-element.23.spectra_hbm, f32[2,32,1024]{2,1,0:T(8,128)S(1)} %collective-permute-done.4.carry, f32[4,2,4,32,256]{4,3,2,1,0:T(8,128)} %shard_map.140.turns_hbm, bf16[256,256]{1,0:T(8,128)(2,1)S(1)} %copy-done.5, bf16[256,256]{1,0:T(8,128)(2,1)S(1)} %copy-done.4, ...), custom_call_target="tpu_custom_call" | custom-call | flops 603979776 | bytes 4980736 | tf_op jit(solution)/shard_map/pallas_call | solution.py:290
  87.9 0.0 all-to-all-done.3.r_hbm
  87.9 0.0 copy-start.8
  87.9 1.0 copy-done.8
  88.9 3.7 %all-to-all-start.2 = ((f32[16,2,32,256]{3,2,1,0:T(8,128)}), f32[16,2,32,256]{3,2,1,0:T(8,128)S(1)}, u32[]{:S(2)}, u32[]{:S(2)}) async-start(f32[16,2,32,256]{3,2,1,0:T(8,128)} %bitcast.11), calls=%async_computation.2 | async-start | bytes 2097152 | tf_op jit(solution)/shard_map/all_to_all | solution.py:408
  92.6 2.7 %shard_map.144.even_hbm = f32[2,256,512]{2,1,0:T(8,128)} custom-call(f32[16,2,32,256]{3,2,1,0:T(8,128)} %copy-done.8, bf16[256,256]{1,0:T(8,128)(2,1)S(1)} %copy-done.5, bf16[256,256]{1,0:T(8,128)(2,1)S(1)} %copy-done.4, bf16[256,256]{1,0:T(8,128)(2,1)S(1)} %copy-done.3, bf16[256,256]{1,0:T(8,128)(2,1)S(1)} %copy-done.2), custom_call_target="tpu_custom_call" | custom-call | flops 402653184 | bytes 2621440 | tf_op jit(solution)/shard_map/pallas_call | solution.py:290
  95.2 13.5 %all-to-all-done.2.r_ref = f32[16,2,32,256]{3,2,1,0:T(8,128)S(1)} async-done(((f32[16,2,32,256]{3,2,1,0:T(8,128)}), f32[16,2,32,256]{3,2,1,0:T(8,128)S(1)}, u32[]{:S(2)}, u32[]{:S(2)}) %all-to-all-start.2) | async-done | bytes 1048608 | tf_op jit(solution)/shard_map/all_to_all | solution.py:408
  108.7 3.4 %shard_map.145 = f32[2,256,1024]{2,1,0:T(8,128)} custom-call(f32[16,2,32,256]{3,2,1,0:T(8,128)S(1)} %all-to-all-done.2.r_ref, f32[2,256,512]{2,1,0:T(8,128)} %shard_map.144.even_hbm, bf16[512,512]{1,0:T(8,128)(2,1)S(1)} %copy-done.1, bf16[512,512]{1,0:T(8,128)(2,1)S(1)} %copy-done), custom_call_target="tpu_custom_call" | custom-call | flops 805306368 | bytes 5242880 | tf_op jit(solution)/shard_map/pallas_call | solution.py:290
Async XLA Ops:
  0.0 9.0 %collective-permute-start.1 = (s32[1]{0:T(128)}, s32[1]{0:T(128)}, u32[]{:S(2)}, u32[]{:S(2)}) collective-permute-start(s32[1]{0:T(128)} %param.15), channel_id=1, source_target_pairs={{0,8},{4,12},{8,0},{12,4},{1,9},{5,13},{9,1},{13,5},{2,10},{6,14},... | collective-permute-start | bytes 20 | tf_op jit(solution)/shard_map/ppermute | solution.py:313
  3.1 6.0 %collective-permute-start = (s32[1]{0:T(128)}, s32[1]{0:T(128)}, u32[]{:S(2)}, u32[]{:S(2)}) collective-permute-start(s32[1]{0:T(128)} %param.15), channel_id=1, source_target_pairs={{0,4},{4,8},{8,12},{12,0},{1,5},{5,9},{9,13},{13,1},{2,6},{6,10},{... | collective-permute-start | bytes 20 | tf_op jit(solution)/shard_map/ppermute | solution.py:313
  4.6 4.5 %collective-permute-start.2 = (s32[1]{0:T(128)}, s32[1]{0:T(128)}, u32[]{:S(2)}, u32[]{:S(2)}) collective-permute-start(s32[1]{0:T(128)} %param.15), channel_id=1, source_target_pairs={{0,12},{4,0},{8,4},{12,8},{1,13},{5,1},{9,5},{13,9},{2,14},{6,2},{... | collective-permute-start | bytes 20 | tf_op jit(solution)/shard_map/ppermute | solution.py:313
  9.1 20.1 %all-to-all-start = ((f32[16,2,32,256]{3,2,1,0:T(8,128)}), f32[16,2,32,256]{3,2,1,0:T(8,128)S(1)}, u32[]{:S(2)}, u32[]{:S(2)}) async-start(f32[16,2,32,256]{3,2,1,0:T(8,128)} %shard_map.136), calls=%async_computation | async-start | bytes 2097152 | tf_op jit(solution)/shard_map/all_to_all | solution.py:355
  17.4 20.4 %copy-start = (bf16[512,512]{1,0:T(8,128)(2,1)S(1)}, bf16[512,512]{1,0:T(8,128)(2,1)}, u32[]{:S(2)}) copy-start(bf16[512,512]{1,0:T(8,128)(2,1)} %constant.17.clone.refs_5_.refs_1_) | copy-start | bytes 1572868
  17.4 20.4 %copy-start.1 = (bf16[512,512]{1,0:T(8,128)(2,1)S(1)}, bf16[512,512]{1,0:T(8,128)(2,1)}, u32[]{:S(2)}) copy-start(bf16[512,512]{1,0:T(8,128)(2,1)} %constant.16.clone.refs_4_.refs_0_) | copy-start | bytes 1572868
  17.4 20.4 %copy-start.2 = (bf16[256,256]{1,0:T(8,128)(2,1)S(1)}, bf16[256,256]{1,0:T(8,128)(2,1)}, u32[]{:S(2)}) copy-start(bf16[256,256]{1,0:T(8,128)(2,1)} %constant.15.clone.refs_3_) | copy-start | bytes 393220
  17.4 20.4 %copy-start.3 = (bf16[256,256]{1,0:T(8,128)(2,1)S(1)}, bf16[256,256]{1,0:T(8,128)(2,1)}, u32[]{:S(2)}) copy-start(bf16[256,256]{1,0:T(8,128)(2,1)} %constant.14.clone.refs_2_) | copy-start | bytes 393220
  17.4 20.4 %copy-start.4 = (bf16[256,256]{1,0:T(8,128)(2,1)S(1)}, bf16[256,256]{1,0:T(8,128)(2,1)}, u32[]{:S(2)}) copy-start(bf16[256,256]{1,0:T(8,128)(2,1)} %constant.13.clone.refs_1_) | copy-start | bytes 393220
  17.4 20.4 %copy-start.5 = (bf16[256,256]{1,0:T(8,128)(2,1)S(1)}, bf16[256,256]{1,0:T(8,128)(2,1)}, u32[]{:S(2)}) copy-start(bf16[256,256]{1,0:T(8,128)(2,1)} %constant.12.clone.refs_0_) | copy-start | bytes 393220
  29.1 1.0 copy-start.6
  30.1 19.8 %all-to-all-start.1 = ((f32[16,2,32,256]{3,2,1,0:T(8,128)}), f32[16,2,32,256]{3,2,1,0:T(8,128)S(1)}, u32[]{:S(2)}, u32[]{:S(2)}) async-start(f32[16,2,32,256]{3,2,1,0:T(8,128)} %shard_map.139), calls=%async_computation.1 | async-start | bytes 2097152 | tf_op jit(solution)/shard_map/all_to_all | solution.py:355
  37.9 1.2 %copy-start.7 = (f32[16,2,32,256]{3,2,1,0:T(8,128)S(1)}, f32[16,2,32,256]{3,2,1,0:T(8,128)}, u32[]{:S(2)}) copy-start(f32[16,2,32,256]{3,2,1,0:T(8,128)} %copy-done.6) | copy-start | bytes 3145732
  42.0 10.9 %collective-permute-start.3 = (f32[2,32,1024]{2,1,0:T(8,128)S(1)}, f32[2,32,1024]{2,1,0:T(8,128)S(1)}, u32[]{:S(2)}, u32[]{:S(2)}) collective-permute-start(f32[2,32,1024]{2,1,0:T(8,128)S(1)} %get-tuple-element.21), channel_id=1, source_target_pairs={{0,16},{1,17},{2,18},{3,19},{4,20},{5,21},{6,22},{7,23},{8,24},{9,... | collective-permute-start | bytes 786440 | tf_op jit(solution)/shard_map/ppermute | solution.py:370
  56.3 31.6 %all-to-all-start.3 = ((f32[16,2,32,256]{3,2,1,0:T(8,128)}), f32[16,2,32,256]{3,2,1,0:T(8,128)S(1)}, u32[]{:S(2)}, u32[]{:S(2)}) async-start(f32[16,2,32,256]{3,2,1,0:T(8,128)} %bitcast.10), calls=%async_computation.3 | async-start | bytes 2097152 | tf_op jit(solution)/shard_map/all_to_all | solution.py:408
  66.4 18.1 %collective-permute-start.4 = (f32[2,32,1024]{2,1,0:T(8,128)S(1)}, f32[2,32,1024]{2,1,0:T(8,128)S(1)}, u32[]{:S(2)}, u32[]{:S(2)}) collective-permute-start(f32[2,32,1024]{2,1,0:T(8,128)S(1)} %get-tuple-element.24), channel_id=1, source_target_pairs={{0,16},{1,17},{2,18},{3,19},{4,20},{5,21},{6,22},{7,23},{8,24},{9,... | collective-permute-start | bytes 786440 | tf_op jit(solution)/shard_map/ppermute | solution.py:370
  87.9 1.0 copy-start.8
  88.9 19.8 %all-to-all-start.2 = ((f32[16,2,32,256]{3,2,1,0:T(8,128)}), f32[16,2,32,256]{3,2,1,0:T(8,128)S(1)}, u32[]{:S(2)}, u32[]{:S(2)}) async-start(f32[16,2,32,256]{3,2,1,0:T(8,128)} %bitcast.11), calls=%async_computation.2 | async-start | bytes 2097152 | tf_op jit(solution)/shard_map/all_to_all | solution.py:408

commit v2 on v1

v2 whole, which is shorter than its diff:
```python
import functools
import math

import jax
import jax.numpy as jnp
import numpy as np
from jax import lax
from jax.experimental import pallas as pl
from jax.experimental.pallas import tpu as pltpu
from jax.sharding import Mesh
from jax.sharding import PartitionSpec as P


phase_rate = 0.004
f32 = jnp.float32
bf16 = jnp.bfloat16
NN = (((1,), (0,)), ((), ()))
NT = (((1,), (1,)), ((), ()))
TN = (((0,), (0,)), ((), ()))
SIN = (3.14159274, -5.1677103, 2.55007744, -0.598291218, 0.0776574388)
COS = (1.0, -4.93480206, 4.05870914, -1.335212, 0.23493728, -0.0243962663)


def cas_tables(length):
    quarter = length // 4
    m = np.arange(quarter, dtype=np.int64)
    j = np.arange(quarter, dtype=np.int64)

    def cas(k, sign=1):
        angle = sign * 2.0 * np.pi * ((k[:, None] * j[None, :]) % length) / length
        return np.cos(angle) + np.sin(angle)

    odd = np.block(
        [
            [cas(4 * m + 1), cas(4 * m + 1, -1)],
            [cas(4 * m + 3), -cas(4 * m + 3, -1)],
        ]
    )
    tables = []
    for table in (np.concatenate([cas(4 * m), cas(4 * m + 2)], axis=1), odd):
        table = table.astype(np.float32)
        high = table.astype(jnp.bfloat16)
        low = (table - high.astype(np.float32)).astype(jnp.bfloat16)
        tables.append(np.stack([high, low]))
    return tables


def split_tables(even):
    quarter = even.shape[1]
    return tuple((even[0, :, here], even[1, :, here]) for here in (slice(0, quarter), slice(quarter, 2 * quarter)))


def halves(value):
    high = value.astype(bf16)
    return high, (value - high.astype(f32)).astype(bf16)


def product(left, right, form):
    dot = functools.partial(lax.dot_general, dimension_numbers=form, preferred_element_type=f32)
    return dot(left[0], right[0]) + dot(left[0], right[1]) + dot(left[1], right[0])


def fold(parts):
    even, cross = parts[0] + parts[2], parts[1] + parts[3]
    return even + cross, even - cross


def fold_odd(parts):
    return jnp.concatenate([parts[0] - parts[2], parts[1] - parts[3]], axis=-1)


def signed_wave(indices, length):
    return jnp.where(indices < length // 2, indices, indices - length).astype(f32)


def wave_at(spot, length):
    quarter = length // 4
    block = spot // quarter
    return 4 * (spot % quarter) + jnp.where(block == 1, 2, jnp.where(block == 2, 1, block))


def modulus_at(start, start_x, shape, length_x, length_y):
    place_y = start + lax.broadcasted_iota(jnp.int32, shape, 0)
    place_x = start_x + lax.broadcasted_iota(jnp.int32, shape, 1)
    wave_y = signed_wave(wave_at(place_y, length_y), length_y)
    wave_x = signed_wave(wave_at(place_x, length_x), length_x)
    return jnp.sqrt(wave_x * wave_x + wave_y * wave_y)


def turn(angle):
    part = angle - jnp.round(angle)
    square = part * part
    sine = jnp.full_like(square, SIN[-1])
    for factor in SIN[-2::-1]:
        sine = sine * square + factor
    sine = sine * part
    cosine = jnp.full_like(square, COS[-1])
    for factor in COS[-2::-1]:
        cosine = cosine * square + factor
    return 1.0 - 2.0 * sine * sine, 2.0 * sine * cosine


def place(odd, rows, length_y):
    band = lax.axis_index("point") * lax.axis_size("space") + lax.axis_index("space")
    return odd * (length_y // 2) + band * rows


def copy_in(pairs, sems):
    copies = [pltpu.make_async_copy(source, target, sems.at[i]) for i, (source, target) in enumerate(pairs)]
    for copy in copies:
        copy.start()
    return copies


def copy_out(copies, source, target, sem):
    copies.append(pltpu.make_async_copy(source, target, sem))
    copies[-1].start()


def wait_all(copies):
    for copy in copies:
        copy.wait()


def forward_y(odd, count_ref, x_hbm, table_hbm, out_hbm, x_ref, out, table_ref, sems, out_sems):
    pairs = [(x_hbm.at[0], x_ref.at[0]), (table_hbm, table_ref), (x_hbm.at[1], x_ref.at[1])]
    copies = copy_in(pairs, sems)
    bands, height, lanes = out.shape
    slab, length_y = x_ref.shape[1:]
    quarter = length_y // 4
    rows = length_y // (2 * bands)
    tall = slab // lanes * rows
    if not odd:
        out[:, 2 * tall :] = jnp.full((bands, height - 2 * tall, lanes), count_ref[0].astype(f32))
    wait_all(copies[:-1])
    table = table_ref[...]
    stores = []

    def keep(part, first, result):
        reach = result.shape[0] // rows
        for piece in range(slab // lanes):
            start = part * tall + piece * rows
            wanted = result[:, piece * lanes : (piece + 1) * lanes]
            out[first : first + reach, start : start + rows] = wanted.reshape(reach, rows, lanes)

    for part in range(2):
        if part:
            copies[-1].wait()
        pieces = [x_ref[part, :, q * quarter : (q + 1) * quarter] for q in range(4)]
        if odd:
            keep(part, 0, product(table, halves(fold_odd(pieces)), NT))
        else:
            total, alternate = fold(pieces)
            for half, (pair, value) in enumerate(zip(split_tables(table), (total, alternate))):
                keep(part, half * bands // 2, product(pair, halves(value), NT))
        here = pl.ds(part * tall, height - tall if part else tall)
        copy_out(stores, out.at[:, here], out_hbm.at[:, here], out_sems.at[part])
    wait_all(stores)


def rotations(odd, length_x, length_y, out_hbm, out, sems):
    _, _, choices, rows, quarter = out.shape
    block = math.gcd(rows, 8)
    start = place(odd, rows, length_y)
    stores = []
    for q in range(4):

        def step(index, _):
            here = pl.ds(pl.multiple_of(index * block, block), block)
            modulus = modulus_at(start + index * block, q * quarter, (block, quarter), length_x, length_y)
            for n in range(choices):
                rate = phase_rate * (n + 1) / (2.0 * math.pi)
                out[q, 0, n, here, :], out[q, 1, n, here, :] = turn(rate * modulus)
            return 0

        lax.fori_loop(0, rows // block, step, 0)
        copy_out(stores, out.at[q], out_hbm.at[q], sems.at[q])
    wait_all(stores)


def forward_x(odd, *refs):
    refs, (turns, highs, lows, spectra, turn_sems, out_sems) = refs[:-6], refs[-6:]
    if odd:
        count_ref, r_hbm, turns_hbm, even, mixing, spectra_hbm, last, r_ref, sems = refs
        copies = copy_in([(r_hbm.at[n], r_ref.at[n]) for n in range(r_ref.shape[0])], sems)
    else:
        r_ref, turns_hbm, even, mixing, spectra_hbm, last, count_ref = refs
    turn_copies = copy_in([(turns_hbm.at[q], turns.at[q]) for q in (2, 3, 0, 1)], turn_sems)
    points, spaces, _, lanes = r_ref.shape
    _, _, rows, quarter = spectra.shape[1:]
    slab = 4 * quarter // spaces
    tall = slab // lanes * rows
    count = 2 * rows
    if not odd:
        for n in range(points):
            count_ref[n] = jnp.max(r_ref[n, 0, 2 * tall :]).astype(jnp.int32)
    for n in range(points):
        if odd:
            copies[n].wait()
        pieces = []
        for s in range(spaces):
            slices = [r_ref[n, s, start : start + rows] for start in range(0, 2 * tall, rows)]
            wide = slab // lanes
            pieces.append(
                jnp.concatenate(
                    [jnp.concatenate(slices[part * wide : (part + 1) * wide], axis=-1) for part in range(2)],
                    axis=0,
                )
            )
        if spaces != 4:
            whole = jnp.concatenate(pieces, axis=-1)
            pieces = [whole[:, q * quarter : (q + 1) * quarter] for q in range(4)]
        here = slice(n * count, (n + 1) * count)
        columns = [*fold(pieces), pieces[0] - pieces[2], pieces[1] - pieces[3]]
        for q, column in enumerate(columns):
            high, low = halves(column)
            highs[here, q * quarter : (q + 1) * quarter] = high
            lows[here, q * quarter : (q + 1) * quarter] = low
    choice = [jnp.clip(count_ref[n] - 1, 0, turns.shape[2] - 1) for n in range(points)]
    stores = []

    def finish(q, result):
        result = result.reshape(points, 2, rows, quarter)
        spectra[q] = result
        copy_out(stores, spectra.at[q], spectra_hbm.at[q], out_sems.at[q])
        turn_copies[(q + 2) % 4].wait()
        first, second = result[0, 0], result[0, 1]
        for n in range(1, points):
            cosine, sine = turns[q, 0, choice[n]], turns[q, 1, choice[n]]
            first, second = (
                cosine * first + sine * second + result[n, 0],
                cosine * second - sine * first + result[n, 1],
            )
        here = slice(q * quarter, (q + 1) * quarter)
        last[0, :, here] = first
        last[1, :, here] = second

    straight, alternate = split_tables(even[...])
    for first, wide, pair in ((2, 2, mixing[...]), (0, 1, straight), (1, 1, alternate)):
        here = slice(first * quarter, (first + wide) * quarter)
        result = product((highs[:, here], lows[:, here]), pair, NT)
        for q in range(wide):
            finish(first + q, result[:, q * quarter : (q + 1) * quarter])
    wait_all(stores)


def finish_x(scaling, count_ref, spectra, carry, turns, even, mixing, out_hbm, out, states, out_sems):
    spaces, points, _, rows, slab = out.shape
    quarter = spaces * slab // 4
    count = points * 2 * rows
    choice = [jnp.clip(count_ref[n] - 1, 0, turns.shape[2] - 1) for n in range(points)]
    for q in range(4):
        here = slice(q * quarter, (q + 1) * quarter)
        first, second = carry[0, :, here], carry[1, :, here]
        for n in range(points):
            cosine, sine = turns[q, 0, choice[n]], turns[q, 1, choice[n]]
            first, second = (
                cosine * first + sine * second + spectra[q, n, 0],
                cosine * second - sine * first + spectra[q, n, 1],
            )
            states[n, 0, :, here] = first * scaling
            states[n, 1, :, here] = second * scaling
    tables = split_tables(even[...])
    total = product(halves(states[..., :quarter].reshape(count, quarter)), tables[0], NN)
    alternate = product(halves(states[..., quarter : 2 * quarter].reshape(count, quarter)), tables[1], NN)
    mixed = product(halves(states[..., 2 * quarter :].reshape(count, 2 * quarter)), mixing[...], NN)
    plus, minus = total + alternate, total - alternate
    straight, crossed = mixed[:, :quarter], mixed[:, quarter:]
    results = [plus + straight, minus + crossed, plus - straight, minus - crossed]
    if spaces != 4:
        whole = jnp.concatenate(results, axis=-1)
        results = [whole[:, s * slab : (s + 1) * slab] for s in range(spaces)]
    stores = []
    for s in range(spaces):
        out[s] = results[s].reshape(points, 2, rows, slab)
        copy_out(stores, out.at[s], out_hbm.at[:, s], out_sems.at[s])
    wait_all(stores)


def inverse_y_even(r_hbm, table, out_hbm, _, r_ref, out, in_sems, sems):
    tables = split_tables(table[...])
    wait_all(copy_in([(r_hbm, r_ref)], in_sems))
    bands, _, rows, slab = r_ref.shape
    half = bands // 2
    stores = []
    for part in range(2):
        total = product(halves(r_ref[:half, part].reshape(half * rows, slab)), tables[0], TN)
        alternate = product(halves(r_ref[half:, part].reshape(half * rows, slab)), tables[1], TN)
        out[part] = jnp.concatenate([total + alternate, total - alternate], axis=-1)
        copy_out(stores, out.at[part], out_hbm.at[part], sems.at[part])
    wait_all(stores)


def inverse_y_odd(r_ref, even_hbm, table, out_hbm, even, out, sems, out_sems):
    bands, _, rows, slab = r_ref.shape
    width = even.shape[-1]
    copies = copy_in([(even_hbm.at[part], even.at[part]) for part in range(2)], sems)
    stores = []
    step = slab // 2
    for part in range(2):
        for piece in range(2):
            here = slice(piece * step, (piece + 1) * step)
            mixed = product(halves(r_ref[:, part, :, here].reshape(bands * rows, step)), table[...], TN)
            if not piece:
                copies[part].wait()
            out[part, here, :width] = even[part, here] + mixed
            out[part, here, width:] = even[part, here] - mixed
            there = pl.ds(piece * step, step)
            copy_out(stores, out.at[part, there], out_hbm.at[part, there], out_sems.at[2 * part + piece])
    wait_all(stores)


def call(kernel, operands, outs, flops, spaces, out_spaces, scratch=(), limit=20, aliases=None):
    shapes = [space(shape, jnp.int32 if space == pltpu.SMEM else f32) for shape, space in zip(outs, out_spaces)]
    traffic = sum(math.prod(x.shape) * x.dtype.itemsize for x in operands)
    traffic += sum(4 * math.prod(shape) for shape in outs)
    many = len(outs) > 1
    specs = [pl.BlockSpec(memory_space=space) for space in out_spaces]
    operands = [pltpu.with_memory_space_constraint(x, s) if s == pltpu.HBM else x for x, s in zip(operands, spaces)]
    return pl.pallas_call(
        kernel,
        in_specs=[pl.BlockSpec(memory_space=space) for space in spaces],
        out_specs=specs if many else specs[0],
        out_shape=shapes if many else shapes[0],
        scratch_shapes=list(scratch),
        input_output_aliases=aliases or {},
        cost_estimate=pl.CostEstimate(flops=flops, bytes_accessed=traffic, transcendentals=0),
        compiler_params=pltpu.CompilerParams(vmem_limit_bytes=limit * 2**20),
    )(*operands)


def on_device(residual, counts):
    slab, length_y = residual.shape[2:]
    blocks, points, spaces = (lax.axis_size(name) for name in ("block", "point", "space"))
    length_x = slab * spaces
    group = ("point", "space")
    bands = points * spaces
    rows = length_y // (2 * bands)
    quarter = length_x // 4
    table_x, tables_y = (cas_tables(length) for length in (length_x, length_y))
    flops_y = [3 * 4 * slab * (length_y // 2) * (length_y // wide) for wide in (4, 2)]
    flops_x = 3 * 4 * rows * points * length_x * 3 * length_x // 8
    vmem, smem, hbm, sems = pltpu.VMEM, pltpu.SMEM, pltpu.HBM, pltpu.SemaphoreType.DMA
    spectra_shape = (4, points, 2, rows, quarter)
    turns_shape = (4, 2, 4, rows, quarter)

    lanes = math.gcd(slab, 128)
    tall = slab // lanes * rows
    heights = (2 * tall + 8, 2 * tall)

    sent, turns = [], []
    for odd in range(2):
        table = tables_y[odd]
        sent.append(
            call(
                functools.partial(forward_y, odd),
                [counts, residual[0], table],
                [(bands, heights[odd], lanes)],
                flops_y[odd],
                [smem, hbm, hbm],
                [hbm],
                scratch=[
                    vmem(residual.shape[1:], f32),
                    vmem((bands, heights[odd], lanes), f32),
                    vmem(table.shape, bf16),
                    sems((3,)),
                    sems((2,)),
                ],
            )
        )
        turns.append(
            call(
                functools.partial(rotations, odd, length_x, length_y),
                [],
                [turns_shape],
                40 * 4 * rows * length_x,
                [],
                [hbm],
                scratch=[vmem(turns_shape, f32), sems((4,))],
            )
        )
    spectra, carry = [None] * 2, [None] * 2
    for odd in range(2):
        arrived = lax.all_to_all(sent[odd], group, split_axis=0, concat_axis=0, tiled=True)
        if odd:
            arrived, spectra[0], later = lax.optimization_barrier((arrived, spectra[0], turns[0]))
        arrived = arrived.reshape(points, spaces, heights[odd], lanes)
        folded = [vmem((points * 2 * rows, length_x), bf16)] * 2
        results = call(
            functools.partial(forward_x, odd),
            [near, arrived, turns[1], *table_x] if odd else [arrived, turns[0], *table_x],
            [spectra_shape, (2, rows, length_x)] + ([] if odd else [(points,)]),
            flops_x,
            ([smem, pl.ANY] if odd else [vmem]) + [hbm, vmem, vmem],
            [hbm, vmem] + ([] if odd else [smem]),
            scratch=[vmem(arrived.shape, f32), sems((points,))] * odd
            + [vmem(turns_shape, f32), *folded, vmem(spectra_shape, f32), sems((4,)), sems((4,))],
        )
        spectra[odd], last = results[:2]
        if not odd:
            near = results[2]
        carry[odd] = lax.ppermute(last, "block", [(b, b + 1) for b in range(blocks - 1)])
        if blocks > 2:
            total = jnp.sum(near).astype(f32) * (phase_rate / (2.0 * math.pi))
            span = lax.ppermute(total, "block", [(b, b + 1) for b in range(blocks - 1)])
            modulus = modulus_at(place(odd, rows, length_y), 0, (rows, length_x), length_x, length_y)
            reach = 1
            while reach < blocks - 1:
                steps = [(b, b + reach) for b in range(blocks - reach)]
                further = lax.ppermute(carry[odd], "block", steps)
                cosine, sine = turn(span * modulus)
                carry[odd] = carry[odd] + jnp.stack(
                    [
                        cosine * further[0] + sine * further[1],
                        cosine * further[1] - sine * further[0],
                    ]
                )
                span = span + lax.ppermute(span, "block", steps)
                reach *= 2
    carry[0], spectra[1] = lax.optimization_barrier((carry[0], spectra[1]))
    solved = []
    for odd in range(2):
        back = call(
            functools.partial(finish_x, 1.0 / (length_x * length_y)),
            [near, spectra[odd], carry[odd], turns[1] if odd else later, *table_x],
            [(points, spaces, 2, rows, slab)],
            flops_x,
            [smem] + [vmem] * 5,
            [hbm],
            scratch=[
                vmem((spaces, points, 2, rows, slab), f32),
                vmem((points, 2, rows, length_x), f32),
                sems((spaces,)),
            ],
        )
        back = back.reshape(bands, 2, rows, slab)
        solved.append(lax.all_to_all(back, group, split_axis=0, concat_axis=0, tiled=True))
    half = (2, slab, length_y // 2)
    even, _ = call(
        inverse_y_even,
        [solved[0], tables_y[0]],
        [half, solved[0].shape],
        flops_y[0],
        [hbm, vmem],
        [hbm, hbm],
        aliases={0: 1},
        scratch=[vmem((bands, 2, rows, slab), f32), vmem(half, f32), sems((1,)), sems((2,))],
    )
    fields = call(
        inverse_y_odd,
        [solved[1], even, tables_y[1]],
        [(2, slab, length_y)],
        flops_y[1],
        [vmem, hbm, vmem],
        [hbm],
        scratch=[vmem(half, f32), vmem((2, slab, length_y), f32), sems((2,)), sems((4,))],
    )
    return fields[None]


def solution(mesh):
    times, spaces = mesh.shape["tm"], mesh.shape["space"]
    points = 4 if times % 4 == 0 else 1
    inner = Mesh(mesh.devices.reshape(times // points, points, spaces), ("block", "point", "space"))
    when = ("block", "point")
    return jax.shard_map(
        on_device,
        mesh=inner,
        in_specs=(P(when, None, "space", None), P(when)),
        out_specs=P(when, None, "space", None),
        check_vma=False,
    )
```

time: 113 us -> 104 us (0.920)
  starting transfers between devices: 37.2 us -> 30.3 us
  waiting for transfers between devices: 37.9 us -> 43.6 us
  Pallas kernels: 32.8 us -> 27.1 us
  local copies, waits for them, and re-layouts: 3.22 us -> 1.25 us
    ppermute x3 -> x0, starting transfers between devices: 5.98 us -> none  [on_device(): lax.ppermute(counts, 'point', [(i, (i + d) % points) for i in range(point...]
    all_to_all x2, waiting for transfers between devices: 11.7 us -> 17.4 us  [on_device(): lax.all_to_all(sent[odd], group, split_axis=0, concat_axis=0, tiled=True)]
    pallas_call x10, Pallas kernels: 32.8 us -> 27.1 us  [call(): pl.pallas_call(kernel, in_specs=[pl.BlockSpec(memory_space=space) for spa...]
    all_to_all x2, starting transfers between devices: 13.8 us -> 9.84 us  [on_device(): lax.all_to_all(back, group, split_axis=0, concat_axis=0, tiled=True)]
    all_to_all x2, starting transfers between devices: 7.58 us -> 10.7 us  [on_device(): lax.all_to_all(sent[odd], group, split_axis=0, concat_axis=0, tiled=True)]
    unnamed x18 -> x12, local copies, waits for them, and re-layouts: 3.22 us -> 1.25 us
  transfers between devices with their start and end apart: 9 -> 6, of which waited for: 3 -> 4; matrix products, arithmetic and copies ran while one was open for 0% -> 0% of each run, Pallas kernels for 23% -> 19%
where the time goes in v2:
time: 104 us; the launch traced here: 103 us
  waiting for transfers between devices  43.6 us (42%)
  starting transfers between devices  30.3 us (29%)
  Pallas kernels  27.1 us (26%)
  local copies, waits for them, and re-layouts  1.25 us (1%)
    pallas_call x10, Pallas kernels, call(): pl.pallas_call(kernel, in_specs=[pl.BlockSpec(memory_space=space) for spa...  27.1 us
    all_to_all x2, waiting for transfers between devices, on_device(): lax.all_to_all(sent[odd], group, split_axis=0, concat_axis=0, tiled=True)  17.4 us
    all_to_all x2, waiting for transfers between devices, on_device(): lax.all_to_all(back, group, split_axis=0, concat_axis=0, tiled=True)  13.4 us
    ppermute x2, waiting for transfers between devices, on_device(): lax.ppermute(last, 'block', [(b, b + 1) for b in range(blocks - 1)])  12.7 us
    all_to_all x2, starting transfers between devices, on_device(): lax.all_to_all(sent[odd], group, split_axis=0, concat_axis=0, tiled=True)  10.7 us
    all_to_all x2, starting transfers between devices, on_device(): lax.all_to_all(back, group, split_axis=0, concat_axis=0, tiled=True)  9.84 us
    ppermute x2, starting transfers between devices, on_device(): lax.ppermute(last, 'block', [(b, b + 1) for b in range(blocks - 1)])  9.81 us
  transfers between devices with their start and end apart: 6, of which 4 were waited for; matrix products, arithmetic and copies ran while one was open for 0% of the time, Pallas kernels for 19%

profile of v2, /device:TPU:0, one launch (start us, length us, event | category | flops | bytes accessed | tf_op | source)
XLA Modules:
  0.0 103.2 jit_solution(17383304377702611229)
XLA Ops:
  0.7 3.1 %shard_map.64 = f32[16,136,128]{2,1,0:T(8,128)} custom-call(s32[1]{0:T(128)S(6)} %copy.9.count_ref, f32[2,256,1024]{2,1,0:T(8,128)} %bitcast.7, bf16[2,256,512]{2,1,0:T(8,128)(2,1)} %constant.4.clone.table_hbm.refs_2_.refs_3_.even.table), custom_call_target="tpu_custom_call" | custom-call | flops 402653184 | bytes 3735556 | tf_op jit(solution)/shard_map/pallas_call | solution.py:320
  3.7 6.3 %all-to-all-start = ((f32[16,136,128]{2,1,0:T(8,128)}), f32[16,136,128]{2,1,0:T(8,128)S(1)}, u32[]{:S(2)}, u32[]{:S(2)}) async-start(f32[16,136,128]{2,1,0:T(8,128)} %shard_map.64), calls=%async_computation | async-start | bytes 2228224 | tf_op jit(solution)/shard_map/all_to_all | solution.py:384
  10.1 4.4 %shard_map.67 = f32[16,128,128]{2,1,0:T(8,128)} custom-call(s32[1]{0:T(128)S(6)} %copy.9.count_ref, f32[2,256,1024]{2,1,0:T(8,128)} %bitcast.8, bf16[2,512,512]{2,1,0:T(8,128)(2,1)} %constant.5.clone.refs_3_.table_hbm.refs_4_.mixing.table), custom_call_target="tpu_custom_call" | custom-call | flops 805306368 | bytes 4194308 | tf_op jit(solution)/shard_map/pallas_call | solution.py:320
  14.5 0.0 copy-start
  14.5 0.0 copy-start.1
  14.5 12.4 %all-to-all-done = f32[16,136,128]{2,1,0:T(8,128)S(1)} async-done(((f32[16,136,128]{2,1,0:T(8,128)}), f32[16,136,128]{2,1,0:T(8,128)S(1)}, u32[]{:S(2)}, u32[]{:S(2)}) %all-to-all-start) | async-done | bytes 1114144 | tf_op jit(solution)/shard_map/all_to_all | solution.py:384
  26.9 4.3 %all-to-all-start.1 = ((f32[16,128,128]{2,1,0:T(8,128)}), f32[16,128,128]{2,1,0:T(8,128)}, u32[]{:S(2)}, u32[]{:S(2)}) async-start(f32[16,128,128]{2,1,0:T(8,128)} %shard_map.67), calls=%async_computation.1 | async-start | bytes 2097152 | tf_op jit(solution)/shard_map/all_to_all | solution.py:384
  31.3 1.7 %shard_map.65.refs_1_.turns = f32[4,2,4,32,256]{4,3,2,1,0:T(8,128)} custom-call(), custom_call_target="tpu_custom_call" | custom-call | flops 5242880 | bytes 1048576 | tf_op jit(solution)/shard_map/pallas_call | solution.py:320
  32.9 0.0 copy-done
  32.9 0.0 copy-done.1
  33.0 3.2 %shard_map.66 = (f32[4,4,2,32,256]{4,3,2,1,0:T(8,128)}, f32[2,32,1024]{2,1,0:T(8,128)S(1)}, s32[4]{0:T(128)S(4)}) custom-call(f32[4,4,136,128]{3,2,1,0:T(8,128)S(1)} %bitcast.6, f32[4,2,4,32,256]{4,3,2,1,0:T(8,128)} %shard_map.65.refs_1_.turns, bf16[2,256,512]{2,1,0:T(8,128)(2,1)S(1)} %copy-done.1, bf16[2,512,512]{2,1,0:T(8,128)(2,1)S(1)} %copy-done), custom_call_target="tpu_custom_call" | custom-call | flops 603979776 | bytes 5046288 | tf_op jit(solution)/shard_map/pallas_call | solution.py:320
  36.2 4.5 %collective-permute-start = (f32[2,32,1024]{2,1,0:T(8,128)S(1)}, f32[2,32,1024]{2,1,0:T(8,128)S(1)}, u32[]{:S(2)}, u32[]{:S(2)}) collective-permute-start(f32[2,32,1024]{2,1,0:T(8,128)S(1)} %get-tuple-element.17), channel_id=1, source_target_pairs={{0,16},{1,17},{2,18},{3,19},{4,20},{5,21},{6,22},{7,23},{8,24},{9,... | collective-permute-start | bytes 786440 | tf_op jit(solution)/shard_map/ppermute | solution.py:402
  40.7 1.7 %shard_map.68.refs_2_.turns = f32[4,2,4,32,256]{4,3,2,1,0:T(8,128)} custom-call(), custom_call_target="tpu_custom_call" | custom-call | flops 5242880 | bytes 1048576 | tf_op jit(solution)/shard_map/pallas_call | solution.py:320
  42.4 0.0 copy-start.2
  42.4 5.0 %all-to-all-done.1 = f32[16,128,128]{2,1,0:T(8,128)} async-done(((f32[16,128,128]{2,1,0:T(8,128)}), f32[16,128,128]{2,1,0:T(8,128)}, u32[]{:S(2)}, u32[]{:S(2)}) %all-to-all-start.1) | async-done | bytes 1048608 | tf_op jit(solution)/shard_map/all_to_all | solution.py:384
  47.4 0.0 copy-start.5
  47.4 3.8 %shard_map.69 = (f32[4,4,2,32,256]{4,3,2,1,0:T(8,128)}, f32[2,32,1024]{2,1,0:T(8,128)S(1)}) custom-call(s32[4]{0:T(128)S(4)} %get-tuple-element.16.refs_0_.count_ref, f32[4,4,128,128]{3,2,1,0:T(8,128)} %bitcast.2.refs_1_, f32[4,2,4,32,256]{4,3,2,1,0:T(8,128)} %shard_map.68.refs_2_.turns, bf16[2,256,512]{2,1,0:T(8,128)(2,1)S(1)} %copy-done.1, ...), custom_call_target="tpu_custom_call" | custom-call | flops 603979776 | bytes 4980752 | tf_op jit(solution)/shard_map/pallas_call | solution.py:320
  51.2 0.0 collective-permute-done.carry
  51.2 0.0 copy-done.2
  51.2 0.0 copy-done.5
  51.2 1.9 %shard_map.71 = f32[4,4,2,32,256]{4,3,2,1,0:T(8,128)} custom-call(s32[4]{0:T(128)S(4)} %get-tuple-element.16.refs_0_.count_ref, f32[4,4,2,32,256]{4,3,2,1,0:T(8,128)S(1)} %copy-done.5, f32[2,32,1024]{2,1,0:T(8,128)S(1)} %collective-permute-done.carry, f32[4,2,4,32,256]{4,3,2,1,0:T(8,128)S(1)} %copy-done.2, bf16[2,256,512]{2,1,0:T(8,128)(2,1)S(1)} %copy-done.1, ...), custom_call_target="tpu_custom_call" | custom-call | flops 603979776 | bytes 4980752 | tf_op jit(solution)/shard_map/pallas_call | solution.py:320
  53.1 0.0 copy-start.3
  53.1 6.1 %all-to-all-start.3 = ((f32[16,2,32,256]{3,2,1,0:T(8,128)}), f32[16,2,32,256]{3,2,1,0:T(8,128)}, u32[]{:S(2)}, u32[]{:S(2)}) async-start(f32[16,2,32,256]{3,2,1,0:T(8,128)} %bitcast.9), calls=%async_computation.3 | async-start | bytes 2097152 | tf_op jit(solution)/shard_map/all_to_all | solution.py:437
  59.3 5.3 %collective-permute-start.1 = (f32[2,32,1024]{2,1,0:T(8,128)S(1)}, f32[2,32,1024]{2,1,0:T(8,128)S(1)}, u32[]{:S(2)}, u32[]{:S(2)}) collective-permute-start(f32[2,32,1024]{2,1,0:T(8,128)S(1)} %get-tuple-element.22), channel_id=1, source_target_pairs={{0,16},{1,17},{2,18},{3,19},{4,20},{5,21},{6,22},{7,23},{8,24},{9,... | collective-permute-start | bytes 786440 | tf_op jit(solution)/shard_map/ppermute | solution.py:402
  64.6 12.7 %collective-permute-done.1.carry = f32[2,32,1024]{2,1,0:T(8,128)S(1)} collective-permute-done((f32[2,32,1024]{2,1,0:T(8,128)S(1)}, f32[2,32,1024]{2,1,0:T(8,128)S(1)}, u32[]{:S(2)}, u32[]{:S(2)}) %collective-permute-start.1) | collective-permute-done | bytes 262176 | tf_op jit(solution)/shard_map/ppermute | solution.py:402
  77.3 0.0 copy-done.3
  77.3 0.0 copy-start.4
  77.3 1.2 %copy-done.4 = f32[4,4,2,32,256]{4,3,2,1,0:T(8,128)S(1)} copy-done((f32[4,4,2,32,256]{4,3,2,1,0:T(8,128)S(1)}, f32[4,4,2,32,256]{4,3,2,1,0:T(8,128)}, u32[]{:S(2)}) %copy-start.4) | copy-done | bytes 1048600
  78.5 1.8 %shard_map.70 = f32[4,4,2,32,256]{4,3,2,1,0:T(8,128)} custom-call(s32[4]{0:T(128)S(4)} %get-tuple-element.16.refs_0_.count_ref, f32[4,4,2,32,256]{4,3,2,1,0:T(8,128)S(1)} %copy-done.4, f32[2,32,1024]{2,1,0:T(8,128)S(1)} %collective-permute-done.1.carry, f32[4,2,4,32,256]{4,3,2,1,0:T(8,128)S(1)} %copy-done.3, bf16[2,256,512]{2,1,0:T(8,128)(2,1)S(1)} %copy-done.1, ...), custom_call_target="tpu_custom_call" | custom-call | flops 603979776 | bytes 4980752 | tf_op jit(solution)/shard_map/pallas_call | solution.py:320
  80.3 0.0 all-to-all-done.3.r_hbm
  80.3 3.7 %all-to-all-start.2 = ((f32[16,2,32,256]{3,2,1,0:T(8,128)}), f32[16,2,32,256]{3,2,1,0:T(8,128)S(1)}, u32[]{:S(2)}, u32[]{:S(2)}) async-start(f32[16,2,32,256]{3,2,1,0:T(8,128)} %bitcast.10), calls=%async_computation.2 | async-start | bytes 2097152 | tf_op jit(solution)/shard_map/all_to_all | solution.py:437
  84.0 2.7 %shard_map.72 = (f32[2,256,512]{2,1,0:T(8,128)}, f32[16,2,32,256]{3,2,1,0:T(8,128)}) custom-call(f32[16,2,32,256]{3,2,1,0:T(8,128)} %all-to-all-done.3.r_hbm, bf16[2,256,512]{2,1,0:T(8,128)(2,1)S(1)} %copy-done.1), custom_call_target="tpu_custom_call", output_to_operand_aliasing={{1}: (0, {})} | custom-call | flops 402653184 | bytes 3670016 | tf_op jit(solution)/shard_map/pallas_call | solution.py:320
  86.7 13.4 %all-to-all-done.2.r_ref = f32[16,2,32,256]{3,2,1,0:T(8,128)S(1)} async-done(((f32[16,2,32,256]{3,2,1,0:T(8,128)}), f32[16,2,32,256]{3,2,1,0:T(8,128)S(1)}, u32[]{:S(2)}, u32[]{:S(2)}) %all-to-all-start.2) | async-done | bytes 1048608 | tf_op jit(solution)/shard_map/all_to_all | solution.py:437
  100.2 3.0 %shard_map.73 = f32[2,256,1024]{2,1,0:T(8,128)} custom-call(f32[16,2,32,256]{3,2,1,0:T(8,128)S(1)} %all-to-all-done.2.r_ref, f32[2,256,512]{2,1,0:T(8,128)} %get-tuple-element.26.even_hbm, bf16[2,512,512]{2,1,0:T(8,128)(2,1)S(1)} %copy-done), custom_call_target="tpu_custom_call" | custom-call | flops 805306368 | bytes 5242880 | tf_op jit(solution)/shard_map/pallas_call | solution.py:320
Async XLA Ops:
  3.7 23.2 %all-to-all-start = ((f32[16,136,128]{2,1,0:T(8,128)}), f32[16,136,128]{2,1,0:T(8,128)S(1)}, u32[]{:S(2)}, u32[]{:S(2)}) async-start(f32[16,136,128]{2,1,0:T(8,128)} %shard_map.64), calls=%async_computation | async-start | bytes 2228224 | tf_op jit(solution)/shard_map/all_to_all | solution.py:384
  14.5 18.4 %copy-start = (bf16[2,512,512]{2,1,0:T(8,128)(2,1)S(1)}, bf16[2,512,512]{2,1,0:T(8,128)(2,1)}, u32[]{:S(2)}) copy-start(bf16[2,512,512]{2,1,0:T(8,128)(2,1)} %constant.5.clone.refs_3_.table_hbm.refs_4_.mixing.table) | copy-start | bytes 3145732
  14.5 18.4 %copy-start.1 = (bf16[2,256,512]{2,1,0:T(8,128)(2,1)S(1)}, bf16[2,256,512]{2,1,0:T(8,128)(2,1)}, u32[]{:S(2)}) copy-start(bf16[2,256,512]{2,1,0:T(8,128)(2,1)} %constant.4.clone.table_hbm.refs_2_.refs_3_.even.table) | copy-start | bytes 1572868
  26.9 20.5 %all-to-all-start.1 = ((f32[16,128,128]{2,1,0:T(8,128)}), f32[16,128,128]{2,1,0:T(8,128)}, u32[]{:S(2)}, u32[]{:S(2)}) async-start(f32[16,128,128]{2,1,0:T(8,128)} %shard_map.67), calls=%async_computation.1 | async-start | bytes 2097152 | tf_op jit(solution)/shard_map/all_to_all | solution.py:384
  36.2 15.0 %collective-permute-start = (f32[2,32,1024]{2,1,0:T(8,128)S(1)}, f32[2,32,1024]{2,1,0:T(8,128)S(1)}, u32[]{:S(2)}, u32[]{:S(2)}) collective-permute-start(f32[2,32,1024]{2,1,0:T(8,128)S(1)} %get-tuple-element.17), channel_id=1, source_target_pairs={{0,16},{1,17},{2,18},{3,19},{4,20},{5,21},{6,22},{7,23},{8,24},{9,... | collective-permute-start | bytes 786440 | tf_op jit(solution)/shard_map/ppermute | solution.py:402
  42.4 8.9 %copy-start.2 = (f32[4,2,4,32,256]{4,3,2,1,0:T(8,128)S(1)}, f32[4,2,4,32,256]{4,3,2,1,0:T(8,128)}, u32[]{:S(2)}) copy-start(f32[4,2,4,32,256]{4,3,2,1,0:T(8,128)} %shard_map.65.refs_1_.turns) | copy-start | bytes 3145732
  47.4 3.8 %copy-start.5 = (f32[4,4,2,32,256]{4,3,2,1,0:T(8,128)S(1)}, f32[4,4,2,32,256]{4,3,2,1,0:T(8,128)}, u32[]{:S(2)}) copy-start(f32[4,4,2,32,256]{4,3,2,1,0:T(8,128)} %get-tuple-element.23.spectra) | copy-start | bytes 3145732
  53.1 24.2 %copy-start.3 = (f32[4,2,4,32,256]{4,3,2,1,0:T(8,128)S(1)}, f32[4,2,4,32,256]{4,3,2,1,0:T(8,128)}, u32[]{:S(2)}) copy-start(f32[4,2,4,32,256]{4,3,2,1,0:T(8,128)} %shard_map.68.refs_2_.turns) | copy-start | bytes 3145732
  53.1 27.2 %all-to-all-start.3 = ((f32[16,2,32,256]{3,2,1,0:T(8,128)}), f32[16,2,32,256]{3,2,1,0:T(8,128)}, u32[]{:S(2)}, u32[]{:S(2)}) async-start(f32[16,2,32,256]{3,2,1,0:T(8,128)} %bitcast.9), calls=%async_computation.3 | async-start | bytes 2097152 | tf_op jit(solution)/shard_map/all_to_all | solution.py:437
  59.3 18.0 %collective-permute-start.1 = (f32[2,32,1024]{2,1,0:T(8,128)S(1)}, f32[2,32,1024]{2,1,0:T(8,128)S(1)}, u32[]{:S(2)}, u32[]{:S(2)}) collective-permute-start(f32[2,32,1024]{2,1,0:T(8,128)S(1)} %get-tuple-element.22), channel_id=1, source_target_pairs={{0,16},{1,17},{2,18},{3,19},{4,20},{5,21},{6,22},{7,23},{8,24},{9,... | collective-permute-start | bytes 786440 | tf_op jit(solution)/shard_map/ppermute | solution.py:402
  77.3 1.2 %copy-start.4 = (f32[4,4,2,32,256]{4,3,2,1,0:T(8,128)S(1)}, f32[4,4,2,32,256]{4,3,2,1,0:T(8,128)}, u32[]{:S(2)}) copy-start(f32[4,4,2,32,256]{4,3,2,1,0:T(8,128)} %get-tuple-element.21.spectra) | copy-start | bytes 3145732
  80.3 19.8 %all-to-all-start.2 = ((f32[16,2,32,256]{3,2,1,0:T(8,128)}), f32[16,2,32,256]{3,2,1,0:T(8,128)S(1)}, u32[]{:S(2)}, u32[]{:S(2)}) async-start(f32[16,2,32,256]{3,2,1,0:T(8,128)} %bitcast.10), calls=%async_computation.2 | async-start | bytes 2097152 | tf_op jit(solution)/shard_map/all_to_all | solution.py:437

commit v3 on v2

--- a/solution.py
+++ b/solution.py
@@ -22,32 +22,19 @@
 
 
 def cas_tables(length):
-    quarter = length // 4
-    m = np.arange(quarter, dtype=np.int64)
-    j = np.arange(quarter, dtype=np.int64)
-
-    def cas(k, sign=1):
-        angle = sign * 2.0 * np.pi * ((k[:, None] * j[None, :]) % length) / length
+    steps = np.arange(length // 4, dtype=np.int64)
+
+    def cas(k):
+        angle = 2.0 * np.pi * ((k[:, None] * steps[None, :]) % length) / length
         return np.cos(angle) + np.sin(angle)
 
-    odd = np.block(
-        [
-            [cas(4 * m + 1), cas(4 * m + 1, -1)],
-            [cas(4 * m + 3), -cas(4 * m + 3, -1)],
-        ]
-    )
     tables = []
-    for table in (np.concatenate([cas(4 * m), cas(4 * m + 2)], axis=1), odd):
-        table = table.astype(np.float32)
+    for pair in ((4 * steps, 4 * steps + 2), (4 * steps + 1, -4 * steps - 1)):
+        table = np.stack([cas(k) for k in pair]).astype(np.float32)
         high = table.astype(jnp.bfloat16)
         low = (table - high.astype(np.float32)).astype(jnp.bfloat16)
-        tables.append(np.stack([high, low]))
+        tables.append(np.stack([high, low], axis=1))
     return tables
-
-
-def split_tables(even):
-    quarter = even.shape[1]
-    return tuple((even[0, :, here], even[1, :, here]) for here in (slice(0, quarter), slice(quarter, 2 * quarter)))
 
 
 def halves(value):
@@ -65,8 +52,12 @@
     return even + cross, even - cross
 
 
-def fold_odd(parts):
-    return jnp.concatenate([parts[0] - parts[2], parts[1] - parts[3]], axis=-1)
+def mix(first, second, table, form):
+    plain, turned = table[0], table[1]
+    return (
+        product(first, plain, form) + product(second, turned, form),
+        product(first, turned, form) - product(second, plain, form),
+    )
 
 
 def signed_wave(indices, length):
@@ -76,7 +67,8 @@
 def wave_at(spot, length):
     quarter = length // 4
     block = spot // quarter
-    return 4 * (spot % quarter) + jnp.where(block == 1, 2, jnp.where(block == 2, 1, block))
+    wave = 4 * (spot % quarter) + jnp.where(block == 1, 2, jnp.where(block == 0, 0, 1))
+    return jnp.where(block == 3, length - wave, wave)
 
 
 def modulus_at(start, start_x, shape, length_x, length_y):
@@ -130,9 +122,9 @@
     quarter = length_y // 4
     rows = length_y // (2 * bands)
     tall = slab // lanes * rows
+    wait_all(copies[:-1])
     if not odd:
         out[:, 2 * tall :] = jnp.full((bands, height - 2 * tall, lanes), count_ref[0].astype(f32))
-    wait_all(copies[:-1])
     table = table_ref[...]
     stores = []
 
@@ -148,11 +140,13 @@
             copies[-1].wait()
         pieces = [x_ref[part, :, q * quarter : (q + 1) * quarter] for q in range(4)]
         if odd:
-            keep(part, 0, product(table, halves(fold_odd(pieces)), NT))
+            first, second = halves(pieces[0] - pieces[2]), halves(pieces[1] - pieces[3])
+            plain, turned = table[0], table[1]
+            keep(part, 0, product(plain, first, NT) + product(turned, second, NT))
+            keep(part, bands // 2, product(turned, first, NT) - product(plain, second, NT))
         else:
-            total, alternate = fold(pieces)
-            for half, (pair, value) in enumerate(zip(split_tables(table), (total, alternate))):
-                keep(part, half * bands // 2, product(pair, halves(value), NT))
+            for half, value in enumerate(fold(pieces)):
+                keep(part, half * bands // 2, product(table[half], halves(value), NT))
         here = pl.ds(part * tall, height - tall if part else tall)
         copy_out(stores, out.at[:, here], out_hbm.at[:, here], out_sems.at[part])
     wait_all(stores)
@@ -163,7 +157,7 @@
     block = math.gcd(rows, 8)
     start = place(odd, rows, length_y)
     stores = []
-    for q in range(4):
+    for q in range(3):
 
         def step(index, _):
             here = pl.ds(pl.multiple_of(index * block, block), block)
@@ -179,93 +173,88 @@
 
 
 def forward_x(odd, *refs):
-    refs, (turns, highs, lows, spectra, turn_sems, out_sems) = refs[:-6], refs[-6:]
+    refs, (turns, highs, lows, spectra, turn_sem, out_sems) = refs[:-6], refs[-6:]
     if odd:
-        count_ref, r_hbm, turns_hbm, even, mixing, spectra_hbm, last, r_ref, sems = refs
-        copies = copy_in([(r_hbm.at[n], r_ref.at[n]) for n in range(r_ref.shape[0])], sems)
+        count_ref, r_ref, turns_hbm, even, mixing, spectra_hbm, last = refs
     else:
         r_ref, turns_hbm, even, mixing, spectra_hbm, last, count_ref = refs
-    turn_copies = copy_in([(turns_hbm.at[q], turns.at[q]) for q in (2, 3, 0, 1)], turn_sems)
     points, spaces, _, lanes = r_ref.shape
     _, _, rows, quarter = spectra.shape[1:]
     slab = 4 * quarter // spaces
-    tall = slab // lanes * rows
+    wide = slab // lanes
+    tall = wide * rows
     count = 2 * rows
+    turn_copy = pltpu.make_async_copy(turns_hbm, turns, turn_sem.at[0])
+    turn_copy.start()
     if not odd:
         for n in range(points):
             count_ref[n] = jnp.max(r_ref[n, 0, 2 * tall :]).astype(jnp.int32)
-    for n in range(points):
-        if odd:
-            copies[n].wait()
+
+    def gather(n, _):
         pieces = []
         for s in range(spaces):
             slices = [r_ref[n, s, start : start + rows] for start in range(0, 2 * tall, rows)]
-            wide = slab // lanes
-            pieces.append(
-                jnp.concatenate(
-                    [jnp.concatenate(slices[part * wide : (part + 1) * wide], axis=-1) for part in range(2)],
-                    axis=0,
-                )
-            )
+            parts = [jnp.concatenate(slices[part * wide : (part + 1) * wide], axis=-1) for part in range(2)]
+            pieces.append(jnp.concatenate(parts, axis=0))
         if spaces != 4:
             whole = jnp.concatenate(pieces, axis=-1)
             pieces = [whole[:, q * quarter : (q + 1) * quarter] for q in range(4)]
-        here = slice(n * count, (n + 1) * count)
+        here = pl.ds(pl.multiple_of(n * count, count), count)
         columns = [*fold(pieces), pieces[0] - pieces[2], pieces[1] - pieces[3]]
         for q, column in enumerate(columns):
-            high, low = halves(column)
-            highs[here, q * quarter : (q + 1) * quarter] = high
-            lows[here, q * quarter : (q + 1) * quarter] = low
+            highs[q, here], lows[q, here] = halves(column)
+        return 0
+
+    lax.fori_loop(0, points, gather, 0)
+    folded = [(highs[q], lows[q]) for q in range(4)]
     choice = [jnp.clip(count_ref[n] - 1, 0, turns.shape[2] - 1) for n in range(points)]
     stores = []
 
-    def finish(q, result):
-        result = result.reshape(points, 2, rows, quarter)
-        spectra[q] = result
+    def keep(q, result):
+        spectra[q] = result.reshape(points, 2, rows, quarter)
         copy_out(stores, spectra.at[q], spectra_hbm.at[q], out_sems.at[q])
-        turn_copies[(q + 2) % 4].wait()
-        first, second = result[0, 0], result[0, 1]
+
+    for q, result in zip((2, 3), mix(*folded[2:], mixing, NT)):
+        keep(q, result)
+    for q in range(2):
+        keep(q, product(folded[q], even[q], NT))
+    turn_copy.wait()
+    for q in (2, 3, 0, 1):
+        first, second = spectra[q, 0, 0], spectra[q, 0, 1]
         for n in range(1, points):
-            cosine, sine = turns[q, 0, choice[n]], turns[q, 1, choice[n]]
+            cosine, sine = turns[min(q, 2), 0, choice[n]], turns[min(q, 2), 1, choice[n]]
             first, second = (
-                cosine * first + sine * second + result[n, 0],
-                cosine * second - sine * first + result[n, 1],
+                cosine * first + sine * second + spectra[q, n, 0],
+                cosine * second - sine * first + spectra[q, n, 1],
             )
         here = slice(q * quarter, (q + 1) * quarter)
         last[0, :, here] = first
         last[1, :, here] = second
-
-    straight, alternate = split_tables(even[...])
-    for first, wide, pair in ((2, 2, mixing[...]), (0, 1, straight), (1, 1, alternate)):
-        here = slice(first * quarter, (first + wide) * quarter)
-        result = product((highs[:, here], lows[:, here]), pair, NT)
-        for q in range(wide):
-            finish(first + q, result[:, q * quarter : (q + 1) * quarter])
     wait_all(stores)
 
 
-def finish_x(scaling, count_ref, spectra, carry, turns, even, mixing, out_hbm, out, states, out_sems):
+def finish_x(scaling, count_ref, spectra, carry, turns, even, mixing, out_hbm, out, states, out_sems, *scratch):
+    if scratch:
+        spectra_hbm, turns_hbm, (spectra, turns, sems) = spectra, turns, scratch
+        wait_all(copy_in([(turns_hbm, turns), (spectra_hbm, spectra)], sems))
     spaces, points, _, rows, slab = out.shape
     quarter = spaces * slab // 4
     count = points * 2 * rows
     choice = [jnp.clip(count_ref[n] - 1, 0, turns.shape[2] - 1) for n in range(points)]
     for q in range(4):
-        here = slice(q * quarter, (q + 1) * quarter)
-        first, second = carry[0, :, here], carry[1, :, here]
+        first, second = (carry[part, :, q * quarter : (q + 1) * quarter] for part in range(2))
         for n in range(points):
-            cosine, sine = turns[q, 0, choice[n]], turns[q, 1, choice[n]]
+            cosine, sine = turns[min(q, 2), 0, choice[n]], turns[min(q, 2), 1, choice[n]]
             first, second = (
                 cosine * first + sine * second + spectra[q, n, 0],
                 cosine * second - sine * first + spectra[q, n, 1],
             )
-            states[n, 0, :, here] = first * scaling
-            states[n, 1, :, here] = second * scaling
-    tables = split_tables(even[...])
-    total = product(halves(states[..., :quarter].reshape(count, quarter)), tables[0], NN)
-    alternate = product(halves(states[..., quarter : 2 * quarter].reshape(count, quarter)), tables[1], NN)
-    mixed = product(halves(states[..., 2 * quarter :].reshape(count, 2 * quarter)), mixing[...], NN)
+            states[q, n, 0] = first * scaling
+            states[q, n, 1] = second * scaling
+    waves = [halves(states[q].reshape(count, quarter)) for q in range(4)]
+    total, alternate = product(waves[0], even[0], NN), product(waves[1], even[1], NN)
     plus, minus = total + alternate, total - alternate
-    straight, crossed = mixed[:, :quarter], mixed[:, quarter:]
+    straight, crossed = mix(waves[2], waves[3], mixing, NN)
     results = [plus + straight, minus + crossed, plus - straight, minus - crossed]
     if spaces != 4:
         whole = jnp.concatenate(results, axis=-1)
@@ -278,14 +267,13 @@
 
 
 def inverse_y_even(r_hbm, table, out_hbm, _, r_ref, out, in_sems, sems):
-    tables = split_tables(table[...])
     wait_all(copy_in([(r_hbm, r_ref)], in_sems))
     bands, _, rows, slab = r_ref.shape
     half = bands // 2
     stores = []
     for part in range(2):
-        total = product(halves(r_ref[:half, part].reshape(half * rows, slab)), tables[0], TN)
-        alternate = product(halves(r_ref[half:, part].reshape(half * rows, slab)), tables[1], TN)
+        total = product(halves(r_ref[:half, part].reshape(half * rows, slab)), table[0], TN)
+        alternate = product(halves(r_ref[half:, part].reshape(half * rows, slab)), table[1], TN)
         out[part] = jnp.concatenate([total + alternate, total - alternate], axis=-1)
         copy_out(stores, out.at[part], out_hbm.at[part], sems.at[part])
     wait_all(stores)
@@ -293,21 +281,36 @@
 
 def inverse_y_odd(r_ref, even_hbm, table, out_hbm, even, out, sems, out_sems):
     bands, _, rows, slab = r_ref.shape
-    width = even.shape[-1]
-    copies = copy_in([(even_hbm.at[part], even.at[part]) for part in range(2)], sems)
-    stores = []
-    step = slab // 2
-    for part in range(2):
-        for piece in range(2):
-            here = slice(piece * step, (piece + 1) * step)
-            mixed = product(halves(r_ref[:, part, :, here].reshape(bands * rows, step)), table[...], TN)
-            if not piece:
-                copies[part].wait()
-            out[part, here, :width] = even[part, here] + mixed
-            out[part, here, width:] = even[part, here] - mixed
-            there = pl.ds(piece * step, step)
-            copy_out(stores, out.at[part, there], out_hbm.at[part, there], out_sems.at[2 * part + piece])
-    wait_all(stores)
+    half = bands // 2
+    quarter = even.shape[-1] // 2
+    pieces = slab // math.gcd(slab, 128)
+    step = slab // pieces
+    copies = copy_in([(even_hbm, even)], sems)
+
+    def place_out(index):
+        here = (index // pieces, pl.ds(pl.multiple_of(index % pieces * step, step), step))
+        return pltpu.make_async_copy(out.at[here], out_hbm.at[here], out_sems.at[index])
+
+    def work(index, _):
+        part = index // pieces
+        here = pl.ds(pl.multiple_of(index % pieces * step, step), step)
+        first = halves(r_ref[:half, part, :, here].reshape(half * rows, step))
+        second = halves(r_ref[half:, part, :, here].reshape(half * rows, step))
+
+        @pl.when(index == 0)
+        def _():
+            wait_all(copies)
+
+        for q, result in enumerate(mix(first, second, table, TN)):
+            base = even[part, here, q * quarter : (q + 1) * quarter]
+            out[part, here, q * quarter : (q + 1) * quarter] = base + result
+            out[part, here, (q + 2) * quarter : (q + 3) * quarter] = base - result
+        place_out(index).start()
+        return 0
+
+    lax.fori_loop(0, 2 * pieces, work, 0)
+    for index in range(2 * pieces):
+        place_out(index).wait()
 
 
 def call(kernel, operands, outs, flops, spaces, out_spaces, scratch=(), limit=20, aliases=None):
@@ -342,7 +345,7 @@
     flops_x = 3 * 4 * rows * points * length_x * 3 * length_x // 8
     vmem, smem, hbm, sems = pltpu.VMEM, pltpu.SMEM, pltpu.HBM, pltpu.SemaphoreType.DMA
     spectra_shape = (4, points, 2, rows, quarter)
-    turns_shape = (4, 2, 4, rows, quarter)
+    turns_shape = (3, 2, 4, rows, quarter)
 
     lanes = math.gcd(slab, 128)
     tall = slab // lanes * rows
@@ -376,7 +379,7 @@
                 40 * 4 * rows * length_x,
                 [],
                 [hbm],
-                scratch=[vmem(turns_shape, f32), sems((4,))],
+                scratch=[vmem(turns_shape, f32), sems((3,))],
             )
         )
     spectra, carry = [None] * 2, [None] * 2
@@ -385,16 +388,15 @@
         if odd:
             arrived, spectra[0], later = lax.optimization_barrier((arrived, spectra[0], turns[0]))
         arrived = arrived.reshape(points, spaces, heights[odd], lanes)
-        folded = [vmem((points * 2 * rows, length_x), bf16)] * 2
+        folded = [vmem((4, points * 2 * rows, quarter), bf16)] * 2
         results = call(
             functools.partial(forward_x, odd),
             [near, arrived, turns[1], *table_x] if odd else [arrived, turns[0], *table_x],
             [spectra_shape, (2, rows, length_x)] + ([] if odd else [(points,)]),
             flops_x,
-            ([smem, pl.ANY] if odd else [vmem]) + [hbm, vmem, vmem],
+            [smem] * odd + [vmem, hbm, vmem, vmem],
             [hbm, vmem] + ([] if odd else [smem]),
-            scratch=[vmem(arrived.shape, f32), sems((points,))] * odd
-            + [vmem(turns_shape, f32), *folded, vmem(spectra_shape, f32), sems((4,)), sems((4,))],
+            scratch=[vmem(turns_shape, f32), *folded, vmem(spectra_shape, f32), sems((1,)), sems((4,))],
         )
         spectra[odd], last = results[:2]
         if not odd:
@@ -425,13 +427,14 @@
             [near, spectra[odd], carry[odd], turns[1] if odd else later, *table_x],
             [(points, spaces, 2, rows, slab)],
             flops_x,
-            [smem] + [vmem] * 5,
+            [smem, hbm, vmem, hbm, vmem, vmem] if odd else [smem] + [vmem] * 5,
             [hbm],
             scratch=[
                 vmem((spaces, points, 2, rows, slab), f32),
-                vmem((points, 2, rows, length_x), f32),
+                vmem(spectra_shape, f32),
                 sems((spaces,)),
-            ],
+            ]
+            + [vmem(spectra_shape, f32), vmem(turns_shape, f32), sems((2,))] * odd,
         )
         back = back.reshape(bands, 2, rows, slab)
         solved.append(lax.all_to_all(back, group, split_axis=0, concat_axis=0, tiled=True))
@@ -453,7 +456,7 @@
         flops_y[1],
         [vmem, hbm, vmem],
         [hbm],
-        scratch=[vmem(half, f32), vmem((2, slab, length_y), f32), sems((2,)), sems((4,))],
+        scratch=[vmem(half, f32), vmem((2, slab, length_y), f32), sems((1,)), sems((2 * slab // lanes,))],
     )
     return fields[None]
 

time: 104 us -> 105 us (level)
  waiting for transfers between devices: 43.6 us -> 45.4 us
  Pallas kernels: 27.1 us -> 25.6 us
    all_to_all x2, waiting for transfers between devices: 17.4 us -> 19.1 us  [on_device(): lax.all_to_all(sent[odd], group, split_axis=0, concat_axis=0, tiled=True)]
    all_to_all x2, starting transfers between devices: 9.84 us -> 11.4 us  [on_device(): lax.all_to_all(back, group, split_axis=0, concat_axis=0, tiled=True)]
    pallas_call x10, Pallas kernels: 27.1 us -> 25.6 us  [call(): pl.pallas_call(kernel, in_specs=[pl.BlockSpec(memory_space=space) for spa...]
  transfers between devices with their start and end apart: 6 -> 6, of which waited for: 4 -> 4; matrix products, arithmetic and copies ran while one was open for 0% -> 0% of each run, Pallas kernels for 19% -> 16%
where the time goes in v3:
time: 105 us; the launch traced here: 104 us
  waiting for transfers between devices  45.4 us (43%)
  starting transfers between devices  31.2 us (30%)
  Pallas kernels  25.6 us (24%)
    pallas_call x10, Pallas kernels, call(): pl.pallas_call(kernel, in_specs=[pl.BlockSpec(memory_space=space) for spa...  25.6 us
    all_to_all x2, waiting for transfers between devices, on_device(): lax.all_to_all(sent[odd], group, split_axis=0, concat_axis=0, tiled=True)  19.1 us
    all_to_all x2, waiting for transfers between devices, on_device(): lax.all_to_all(back, group, split_axis=0, concat_axis=0, tiled=True)  13.4 us
    ppermute x2, waiting for transfers between devices, on_device(): lax.ppermute(last, 'block', [(b, b + 1) for b in range(blocks - 1)])  12.9 us
    all_to_all x2, starting transfers between devices, on_device(): lax.all_to_all(back, group, split_axis=0, concat_axis=0, tiled=True)  11.4 us
    all_to_all x2, starting transfers between devices, on_device(): lax.all_to_all(sent[odd], group, split_axis=0, concat_axis=0, tiled=True)  9.98 us
    ppermute x2, starting transfers between devices, on_device(): lax.ppermute(last, 'block', [(b, b + 1) for b in range(blocks - 1)])  9.84 us
  transfers between devices with their start and end apart: 6, of which 4 were waited for; matrix products, arithmetic and copies ran while one was open for 0% of the time, Pallas kernels for 16%

profile of v3, /device:TPU:0, one launch (start us, length us, event | category | flops | bytes accessed | tf_op | source)
XLA Modules:
  0.0 104.2 jit_solution(1283250418505505836)
XLA Ops:
  0.7 3.1 %shard_map.64 = f32[16,136,128]{2,1,0:T(8,128)} custom-call(s32[1]{0:T(128)S(6)} %copy.9.count_ref, f32[2,256,1024]{2,1,0:T(8,128)} %bitcast.8, bf16[2,2,256,256]{3,2,1,0:T(8,128)(2,1)} %constant.4.clone.table_hbm.refs_2_.refs_3_.even.table), custom_call_target="tpu_custom_call" | custom-call | flops 402653184 | bytes 3735556 | tf_op jit(solution)/shard_map/pallas_call | solution.py:323
  3.7 6.3 %all-to-all-start = ((f32[16,136,128]{2,1,0:T(8,128)}), f32[16,136,128]{2,1,0:T(8,128)S(1)}, u32[]{:S(2)}, u32[]{:S(2)}) async-start(f32[16,136,128]{2,1,0:T(8,128)} %shard_map.64), calls=%async_computation | async-start | bytes 2228224 | tf_op jit(solution)/shard_map/all_to_all | solution.py:387
  10.1 3.4 %shard_map.67 = f32[16,128,128]{2,1,0:T(8,128)} custom-call(s32[1]{0:T(128)S(6)} %copy.9.count_ref, f32[2,256,1024]{2,1,0:T(8,128)} %bitcast.9, bf16[2,2,256,256]{3,2,1,0:T(8,128)(2,1)} %constant.5.clone.refs_3_.table_hbm.refs_4_.mixing.table), custom_call_target="tpu_custom_call" | custom-call | flops 805306368 | bytes 3670020 | tf_op jit(solution)/shard_map/pallas_call | solution.py:323
  13.5 0.0 copy-start
  13.5 0.0 copy-start.1
  13.5 13.4 %all-to-all-done = f32[16,136,128]{2,1,0:T(8,128)S(1)} async-done(((f32[16,136,128]{2,1,0:T(8,128)}), f32[16,136,128]{2,1,0:T(8,128)S(1)}, u32[]{:S(2)}, u32[]{:S(2)}) %all-to-all-start) | async-done | bytes 1114144 | tf_op jit(solution)/shard_map/all_to_all | solution.py:387
  26.9 3.7 %all-to-all-start.1 = ((f32[16,128,128]{2,1,0:T(8,128)}), f32[16,128,128]{2,1,0:T(8,128)S(1)}, u32[]{:S(2)}, u32[]{:S(2)}) async-start(f32[16,128,128]{2,1,0:T(8,128)} %shard_map.67), calls=%async_computation.1 | async-start | bytes 2097152 | tf_op jit(solution)/shard_map/all_to_all | solution.py:387
  30.6 1.4 %shard_map.65.refs_1_.turns = f32[3,2,4,32,256]{4,3,2,1,0:T(8,128)} custom-call(), custom_call_target="tpu_custom_call" | custom-call | flops 5242880 | bytes 786432 | tf_op jit(solution)/shard_map/pallas_call | solution.py:323
  32.0 0.0 copy-done
  32.0 0.0 copy-done.1
  32.0 2.7 %shard_map.66 = (f32[4,4,2,32,256]{4,3,2,1,0:T(8,128)}, f32[2,32,1024]{2,1,0:T(8,128)}, s32[4]{0:T(128)S(4)}) custom-call(f32[4,4,136,128]{3,2,1,0:T(8,128)S(1)} %bitcast.6, f32[3,2,4,32,256]{4,3,2,1,0:T(8,128)} %shard_map.65.refs_1_.turns, bf16[2,2,256,256]{3,2,1,0:T(8,128)(2,1)S(1)} %copy-done.1, bf16[2,2,256,256]{3,2,1,0:T(8,128)(2,1)S(1)} %copy-done), custom_call_target="tpu_custom_call" | custom-call | flops 603979776 | bytes 4259856 | tf_op jit(solution)/shard_map/pallas_call | solution.py:323
  34.8 0.0 copy-start.2
  34.8 4.6 %collective-permute-start = (f32[2,32,1024]{2,1,0:T(8,128)}, f32[2,32,1024]{2,1,0:T(8,128)S(1)}, u32[]{:S(2)}, u32[]{:S(2)}) collective-permute-start(f32[2,32,1024]{2,1,0:T(8,128)} %get-tuple-element.17), channel_id=1, source_target_pairs={{0,16},{1,17},{2,18},{3,19},{4,20},{5,21},{6,22},{7,23},{8,24},{9,... | collective-permute-start | bytes 786440 | tf_op jit(solution)/shard_map/ppermute | solution.py:404
  39.4 1.5 %shard_map.68.refs_2_.turns = f32[3,2,4,32,256]{4,3,2,1,0:T(8,128)} custom-call(), custom_call_target="tpu_custom_call" | custom-call | flops 5242880 | bytes 786432 | tf_op jit(solution)/shard_map/pallas_call | solution.py:323
  40.9 5.8 %all-to-all-done.1 = f32[16,128,128]{2,1,0:T(8,128)S(1)} async-done(((f32[16,128,128]{2,1,0:T(8,128)}), f32[16,128,128]{2,1,0:T(8,128)S(1)}, u32[]{:S(2)}, u32[]{:S(2)}) %all-to-all-start.1) | async-done | bytes 1048608 | tf_op jit(solution)/shard_map/all_to_all | solution.py:387
  46.7 0.0 copy-start.3
  46.7 1.9 %shard_map.69 = (f32[4,4,2,32,256]{4,3,2,1,0:T(8,128)}, f32[2,32,1024]{2,1,0:T(8,128)S(1)}) custom-call(s32[4]{0:T(128)S(4)} %get-tuple-element.16.refs_0_.count_ref, f32[4,4,128,128]{3,2,1,0:T(8,128)S(1)} %bitcast.7, f32[3,2,4,32,256]{4,3,2,1,0:T(8,128)} %shard_map.68.refs_2_.turns, bf16[2,2,256,256]{3,2,1,0:T(8,128)(2,1)S(1)} %copy-done.1, ...), custom_call_target="tpu_custom_call" | custom-call | flops 603979776 | bytes 4194320 | tf_op jit(solution)/shard_map/pallas_call | solution.py:323
  48.6 0.0 collective-permute-done.carry
  48.6 0.0 copy-done.2
  48.6 0.0 copy-done.3
  48.6 1.8 %shard_map.71 = f32[4,4,2,32,256]{4,3,2,1,0:T(8,128)} custom-call(s32[4]{0:T(128)S(4)} %get-tuple-element.16.refs_0_.count_ref, f32[4,4,2,32,256]{4,3,2,1,0:T(8,128)S(1)} %copy-done.3, f32[2,32,1024]{2,1,0:T(8,128)S(1)} %collective-permute-done.carry, f32[3,2,4,32,256]{4,3,2,1,0:T(8,128)S(1)} %copy-done.2, bf16[2,2,256,256]{3,2,1,0:T(8,128)(2,1)S(1)} %copy-done.1, ...), custom_call_target="tpu_custom_call" | custom-call | flops 603979776 | bytes 4194320 | tf_op jit(solution)/shard_map/pallas_call | solution.py:323
  50.4 7.7 %all-to-all-start.3 = ((f32[16,2,32,256]{3,2,1,0:T(8,128)}), f32[16,2,32,256]{3,2,1,0:T(8,128)S(1)}, u32[]{:S(2)}, u32[]{:S(2)}) async-start(f32[16,2,32,256]{3,2,1,0:T(8,128)} %bitcast.10), calls=%async_computation.3 | async-start | bytes 2097152 | tf_op jit(solution)/shard_map/all_to_all | solution.py:440
  58.2 5.2 %collective-permute-start.1 = (f32[2,32,1024]{2,1,0:T(8,128)S(1)}, f32[2,32,1024]{2,1,0:T(8,128)S(1)}, u32[]{:S(2)}, u32[]{:S(2)}) collective-permute-start(f32[2,32,1024]{2,1,0:T(8,128)S(1)} %get-tuple-element.22), channel_id=1, source_target_pairs={{0,16},{1,17},{2,18},{3,19},{4,20},{5,21},{6,22},{7,23},{8,24},{9,... | collective-permute-start | bytes 786440 | tf_op jit(solution)/shard_map/ppermute | solution.py:404
  63.4 12.9 %collective-permute-done.1.carry = f32[2,32,1024]{2,1,0:T(8,128)S(1)} collective-permute-done((f32[2,32,1024]{2,1,0:T(8,128)S(1)}, f32[2,32,1024]{2,1,0:T(8,128)S(1)}, u32[]{:S(2)}, u32[]{:S(2)}) %collective-permute-start.1) | collective-permute-done | bytes 262176 | tf_op jit(solution)/shard_map/ppermute | solution.py:404
  76.3 3.3 %shard_map.70 = f32[4,4,2,32,256]{4,3,2,1,0:T(8,128)} custom-call(s32[4]{0:T(128)S(4)} %get-tuple-element.16.refs_0_.count_ref, f32[4,4,2,32,256]{4,3,2,1,0:T(8,128)} %get-tuple-element.21.spectra, f32[2,32,1024]{2,1,0:T(8,128)S(1)} %collective-permute-done.1.carry, f32[3,2,4,32,256]{4,3,2,1,0:T(8,128)} %shard_map.68.refs_2_.turns, ...), custom_call_target="tpu_custom_call" | custom-call | flops 603979776 | bytes 4194320 | tf_op jit(solution)/shard_map/pallas_call | solution.py:323
  79.5 0.0 all-to-all-done.3.r_hbm
  79.6 0.0 copy-start.4
  79.6 1.0 copy-done.4
  80.5 3.7 %all-to-all-start.2 = ((f32[16,2,32,256]{3,2,1,0:T(8,128)}), f32[16,2,32,256]{3,2,1,0:T(8,128)S(1)}, u32[]{:S(2)}, u32[]{:S(2)}) async-start(f32[16,2,32,256]{3,2,1,0:T(8,128)} %bitcast.11), calls=%async_computation.2 | async-start | bytes 2097152 | tf_op jit(solution)/shard_map/all_to_all | solution.py:440
  84.2 2.7 %shard_map.72 = (f32[2,256,512]{2,1,0:T(8,128)}, f32[16,2,32,256]{3,2,1,0:T(8,128)}) custom-call(f32[16,2,32,256]{3,2,1,0:T(8,128)} %copy-done.4, bf16[2,2,256,256]{3,2,1,0:T(8,128)(2,1)S(1)} %copy-done.1), custom_call_target="tpu_custom_call", output_to_operand_aliasing={{1}: (0, {})} | custom-call | flops 402653184 | bytes 3670016 | tf_op jit(solution)/shard_map/pallas_call | solution.py:323
  86.9 13.4 %all-to-all-done.2.r_ref = f32[16,2,32,256]{3,2,1,0:T(8,128)S(1)} async-done(((f32[16,2,32,256]{3,2,1,0:T(8,128)}), f32[16,2,32,256]{3,2,1,0:T(8,128)S(1)}, u32[]{:S(2)}, u32[]{:S(2)}) %all-to-all-start.2) | async-done | bytes 1048608 | tf_op jit(solution)/shard_map/all_to_all | solution.py:440
  100.4 3.8 %shard_map.73 = f32[2,256,1024]{2,1,0:T(8,128)} custom-call(f32[16,2,32,256]{3,2,1,0:T(8,128)S(1)} %all-to-all-done.2.r_ref, f32[2,256,512]{2,1,0:T(8,128)} %get-tuple-element.26.even_hbm, bf16[2,2,256,256]{3,2,1,0:T(8,128)(2,1)S(1)} %copy-done), custom_call_target="tpu_custom_call" | custom-call | flops 805306368 | bytes 4718592 | tf_op jit(solution)/shard_map/pallas_call | solution.py:323
Async XLA Ops:
  3.7 23.2 %all-to-all-start = ((f32[16,136,128]{2,1,0:T(8,128)}), f32[16,136,128]{2,1,0:T(8,128)S(1)}, u32[]{:S(2)}, u32[]{:S(2)}) async-start(f32[16,136,128]{2,1,0:T(8,128)} %shard_map.64), calls=%async_computation | async-start | bytes 2228224 | tf_op jit(solution)/shard_map/all_to_all | solution.py:387
  13.5 18.5 %copy-start = (bf16[2,2,256,256]{3,2,1,0:T(8,128)(2,1)S(1)}, bf16[2,2,256,256]{3,2,1,0:T(8,128)(2,1)}, u32[]{:S(2)}) copy-start(bf16[2,2,256,256]{3,2,1,0:T(8,128)(2,1)} %constant.5.clone.refs_3_.table_hbm.refs_4_.mixing.table) | copy-start | bytes 1572868
  13.5 18.5 %copy-start.1 = (bf16[2,2,256,256]{3,2,1,0:T(8,128)(2,1)S(1)}, bf16[2,2,256,256]{3,2,1,0:T(8,128)(2,1)}, u32[]{:S(2)}) copy-start(bf16[2,2,256,256]{3,2,1,0:T(8,128)(2,1)} %constant.4.clone.table_hbm.refs_2_.refs_3_.even.table) | copy-start | bytes 1572868
  26.9 19.8 %all-to-all-start.1 = ((f32[16,128,128]{2,1,0:T(8,128)}), f32[16,128,128]{2,1,0:T(8,128)S(1)}, u32[]{:S(2)}, u32[]{:S(2)}) async-start(f32[16,128,128]{2,1,0:T(8,128)} %shard_map.67), calls=%async_computation.1 | async-start | bytes 2097152 | tf_op jit(solution)/shard_map/all_to_all | solution.py:387
  34.8 13.8 %copy-start.2 = (f32[3,2,4,32,256]{4,3,2,1,0:T(8,128)S(1)}, f32[3,2,4,32,256]{4,3,2,1,0:T(8,128)}, u32[]{:S(2)}) copy-start(f32[3,2,4,32,256]{4,3,2,1,0:T(8,128)} %shard_map.65.refs_1_.turns) | copy-start | bytes 2359300
  34.8 13.8 %collective-permute-start = (f32[2,32,1024]{2,1,0:T(8,128)}, f32[2,32,1024]{2,1,0:T(8,128)S(1)}, u32[]{:S(2)}, u32[]{:S(2)}) collective-permute-start(f32[2,32,1024]{2,1,0:T(8,128)} %get-tuple-element.17), channel_id=1, source_target_pairs={{0,16},{1,17},{2,18},{3,19},{4,20},{5,21},{6,22},{7,23},{8,24},{9,... | collective-permute-start | bytes 786440 | tf_op jit(solution)/shard_map/ppermute | solution.py:404
  46.7 1.9 %copy-start.3 = (f32[4,4,2,32,256]{4,3,2,1,0:T(8,128)S(1)}, f32[4,4,2,32,256]{4,3,2,1,0:T(8,128)}, u32[]{:S(2)}) copy-start(f32[4,4,2,32,256]{4,3,2,1,0:T(8,128)} %get-tuple-element.23.spectra) | copy-start | bytes 3145732
  50.4 29.1 %all-to-all-start.3 = ((f32[16,2,32,256]{3,2,1,0:T(8,128)}), f32[16,2,32,256]{3,2,1,0:T(8,128)S(1)}, u32[]{:S(2)}, u32[]{:S(2)}) async-start(f32[16,2,32,256]{3,2,1,0:T(8,128)} %bitcast.10), calls=%async_computation.3 | async-start | bytes 2097152 | tf_op jit(solution)/shard_map/all_to_all | solution.py:440
  58.2 18.1 %collective-permute-start.1 = (f32[2,32,1024]{2,1,0:T(8,128)S(1)}, f32[2,32,1024]{2,1,0:T(8,128)S(1)}, u32[]{:S(2)}, u32[]{:S(2)}) collective-permute-start(f32[2,32,1024]{2,1,0:T(8,128)S(1)} %get-tuple-element.22), channel_id=1, source_target_pairs={{0,16},{1,17},{2,18},{3,19},{4,20},{5,21},{6,22},{7,23},{8,24},{9,... | collective-permute-start | bytes 786440 | tf_op jit(solution)/shard_map/ppermute | solution.py:404
  79.6 1.0 copy-start.4
  80.5 19.8 %all-to-all-start.2 = ((f32[16,2,32,256]{3,2,1,0:T(8,128)}), f32[16,2,32,256]{3,2,1,0:T(8,128)S(1)}, u32[]{:S(2)}, u32[]{:S(2)}) async-start(f32[16,2,32,256]{3,2,1,0:T(8,128)} %bitcast.11), calls=%async_computation.2 | async-start | bytes 2097152 | tf_op jit(solution)/shard_map/all_to_all | solution.py:440

commit v4 on v3

--- a/solution.py
+++ b/solution.py
@@ -71,8 +71,8 @@
     return jnp.where(block == 3, length - wave, wave)
 
 
-def modulus_at(start, start_x, shape, length_x, length_y):
-    place_y = start + lax.broadcasted_iota(jnp.int32, shape, 0)
+def modulus_at(kind, start, start_x, shape, length_x, length_y):
+    place_y = kind * (length_y // 4) + start + lax.broadcasted_iota(jnp.int32, shape, 0)
     place_x = start_x + lax.broadcasted_iota(jnp.int32, shape, 1)
     wave_y = signed_wave(wave_at(place_y, length_y), length_y)
     wave_x = signed_wave(wave_at(place_x, length_x), length_x)
@@ -92,9 +92,8 @@
     return 1.0 - 2.0 * sine * sine, 2.0 * sine * cosine
 
 
-def place(odd, rows, length_y):
-    band = lax.axis_index("point") * lax.axis_size("space") + lax.axis_index("space")
-    return odd * (length_y // 2) + band * rows
+def own_band():
+    return lax.axis_index("point") * lax.axis_size("space") + lax.axis_index("space")
 
 
 def copy_in(pairs, sems):
@@ -114,54 +113,48 @@
         copy.wait()
 
 
-def forward_y(odd, count_ref, x_hbm, table_hbm, out_hbm, x_ref, out, table_ref, sems, out_sems):
-    pairs = [(x_hbm.at[0], x_ref.at[0]), (table_hbm, table_ref), (x_hbm.at[1], x_ref.at[1])]
+def forward_y(count_ref, x_hbm, even_hbm, odd_hbm, out_hbm, x_ref, out, even, mixing, sems, out_sems):
+    pairs = [(x_hbm.at[0], x_ref.at[0]), (even_hbm, even), (odd_hbm, mixing), (x_hbm.at[1], x_ref.at[1])]
     copies = copy_in(pairs, sems)
     bands, height, lanes = out.shape
     slab, length_y = x_ref.shape[1:]
     quarter = length_y // 4
-    rows = length_y // (2 * bands)
-    tall = slab // lanes * rows
+    small = quarter // bands
+    tall = slab // lanes * 4 * small
+    out[:, 2 * tall :] = jnp.full((bands, height - 2 * tall, lanes), count_ref[0].astype(f32))
     wait_all(copies[:-1])
-    if not odd:
-        out[:, 2 * tall :] = jnp.full((bands, height - 2 * tall, lanes), count_ref[0].astype(f32))
-    table = table_ref[...]
-    stores = []
-
-    def keep(part, first, result):
-        reach = result.shape[0] // rows
-        for piece in range(slab // lanes):
-            start = part * tall + piece * rows
-            wanted = result[:, piece * lanes : (piece + 1) * lanes]
-            out[first : first + reach, start : start + rows] = wanted.reshape(reach, rows, lanes)
-
+    stores = []
     for part in range(2):
         if part:
             copies[-1].wait()
         pieces = [x_ref[part, :, q * quarter : (q + 1) * quarter] for q in range(4)]
-        if odd:
-            first, second = halves(pieces[0] - pieces[2]), halves(pieces[1] - pieces[3])
-            plain, turned = table[0], table[1]
-            keep(part, 0, product(plain, first, NT) + product(turned, second, NT))
-            keep(part, bands // 2, product(turned, first, NT) - product(plain, second, NT))
-        else:
-            for half, value in enumerate(fold(pieces)):
-                keep(part, half * bands // 2, product(table[half], halves(value), NT))
+        first, second = halves(pieces[0] - pieces[2]), halves(pieces[1] - pieces[3])
+        plain, turned = mixing[0], mixing[1]
+        results = [product(even[half], halves(value), NT) for half, value in enumerate(fold(pieces))]
+        results.append(product(plain, first, NT) + product(turned, second, NT))
+        results.append(product(turned, first, NT) - product(plain, second, NT))
+        for kind, result in enumerate(results):
+            for piece in range(slab // lanes):
+                start = part * tall + (piece * 4 + kind) * small
+                wanted = result[:, piece * lanes : (piece + 1) * lanes]
+                out[:, start : start + small] = wanted.reshape(bands, small, lanes)
         here = pl.ds(part * tall, height - tall if part else tall)
         copy_out(stores, out.at[:, here], out_hbm.at[:, here], out_sems.at[part])
     wait_all(stores)
 
 
-def rotations(odd, length_x, length_y, out_hbm, out, sems):
+def rotations(kinds, length_x, length_y, out_hbm, out, sems):
     _, _, choices, rows, quarter = out.shape
-    block = math.gcd(rows, 8)
-    start = place(odd, rows, length_y)
+    small = rows // len(kinds)
+    block = math.gcd(small, 8)
+    start = own_band() * small
     stores = []
     for q in range(3):
 
         def step(index, _):
             here = pl.ds(pl.multiple_of(index * block, block), block)
-            modulus = modulus_at(start + index * block, q * quarter, (block, quarter), length_x, length_y)
+            kind, within = kinds[0] + index * block // small, index * block % small
+            modulus = modulus_at(kind, start + within, q * quarter, (block, quarter), length_x, length_y)
             for n in range(choices):
                 rate = phase_rate * (n + 1) / (2.0 * math.pi)
                 out[q, 0, n, here, :], out[q, 1, n, here, :] = turn(rate * modulus)
@@ -172,9 +165,10 @@
     wait_all(stores)
 
 
-def forward_x(odd, *refs):
+def forward_x(kinds, *refs):
     refs, (turns, highs, lows, spectra, turn_sem, out_sems) = refs[:-6], refs[-6:]
-    if odd:
+    late = kinds[0] > 0
+    if late:
         count_ref, r_ref, turns_hbm, even, mixing, spectra_hbm, last = refs
     else:
         r_ref, turns_hbm, even, mixing, spectra_hbm, last, count_ref = refs
@@ -182,18 +176,20 @@
     _, _, rows, quarter = spectra.shape[1:]
     slab = 4 * quarter // spaces
     wide = slab // lanes
-    tall = wide * rows
+    small = rows // len(kinds)
+    stride, offset = 4 * small, kinds[0] * small
+    tall = wide * stride
     count = 2 * rows
     turn_copy = pltpu.make_async_copy(turns_hbm, turns, turn_sem.at[0])
     turn_copy.start()
-    if not odd:
+    if not late:
         for n in range(points):
             count_ref[n] = jnp.max(r_ref[n, 0, 2 * tall :]).astype(jnp.int32)
 
     def gather(n, _):
         pieces = []
         for s in range(spaces):
-            slices = [r_ref[n, s, start : start + rows] for start in range(0, 2 * tall, rows)]
+            slices = [r_ref[n, s, start : start + rows] for start in range(offset, 2 * tall, stride)]
             parts = [jnp.concatenate(slices[part * wide : (part + 1) * wide], axis=-1) for part in range(2)]
             pieces.append(jnp.concatenate(parts, axis=0))
         if spaces != 4:
@@ -266,51 +262,41 @@
     wait_all(stores)
 
 
-def inverse_y_even(r_hbm, table, out_hbm, _, r_ref, out, in_sems, sems):
+def inverse_y_first(r_hbm, even, out_hbm, _, r_ref, out, in_sems, sems):
     wait_all(copy_in([(r_hbm, r_ref)], in_sems))
     bands, _, rows, slab = r_ref.shape
-    half = bands // 2
     stores = []
     for part in range(2):
-        total = product(halves(r_ref[:half, part].reshape(half * rows, slab)), table[0], TN)
-        alternate = product(halves(r_ref[half:, part].reshape(half * rows, slab)), table[1], TN)
-        out[part] = jnp.concatenate([total + alternate, total - alternate], axis=-1)
+        out[part] = product(halves(r_ref[:, part].reshape(bands * rows, slab)), even[0], TN)
         copy_out(stores, out.at[part], out_hbm.at[part], sems.at[part])
     wait_all(stores)
 
 
-def inverse_y_odd(r_ref, even_hbm, table, out_hbm, even, out, sems, out_sems):
+def inverse_y_rest(r_ref, first_hbm, even, mixing, out_hbm, total, out, sems, out_sems):
     bands, _, rows, slab = r_ref.shape
-    half = bands // 2
-    quarter = even.shape[-1] // 2
+    small = rows // 3
+    quarter = total.shape[-1]
     pieces = slab // math.gcd(slab, 128)
     step = slab // pieces
-    copies = copy_in([(even_hbm, even)], sems)
-
-    def place_out(index):
-        here = (index // pieces, pl.ds(pl.multiple_of(index % pieces * step, step), step))
-        return pltpu.make_async_copy(out.at[here], out_hbm.at[here], out_sems.at[index])
-
-    def work(index, _):
-        part = index // pieces
-        here = pl.ds(pl.multiple_of(index % pieces * step, step), step)
-        first = halves(r_ref[:half, part, :, here].reshape(half * rows, step))
-        second = halves(r_ref[half:, part, :, here].reshape(half * rows, step))
-
-        @pl.when(index == 0)
-        def _():
-            wait_all(copies)
-
-        for q, result in enumerate(mix(first, second, table, TN)):
-            base = even[part, here, q * quarter : (q + 1) * quarter]
-            out[part, here, q * quarter : (q + 1) * quarter] = base + result
-            out[part, here, (q + 2) * quarter : (q + 3) * quarter] = base - result
-        place_out(index).start()
-        return 0
-
-    lax.fori_loop(0, 2 * pieces, work, 0)
-    for index in range(2 * pieces):
-        place_out(index).wait()
+    copies = copy_in([(first_hbm, total)], sems)
+    stores = []
+    for part in range(2):
+        for piece in range(pieces):
+            here = slice(piece * step, (piece + 1) * step)
+            waves = [
+                halves(r_ref[:, part, kind * small : (kind + 1) * small, here].reshape(bands * small, step))
+                for kind in range(3)
+            ]
+            alternate = product(waves[0], even[1], TN)
+            straight, crossed = mix(waves[1], waves[2], mixing, TN)
+            if not stores:
+                wait_all(copies)
+            plus, minus = total[part, here] + alternate, total[part, here] - alternate
+            for q, result in enumerate((plus + straight, minus + crossed, plus - straight, minus - crossed)):
+                out[part, here, q * quarter : (q + 1) * quarter] = result
+            there = pl.ds(piece * step, step)
+            copy_out(stores, out.at[part, there], out_hbm.at[part, there], out_sems.at[part * pieces + piece])
+    wait_all(stores)
 
 
 def call(kernel, operands, outs, flops, spaces, out_spaces, scratch=(), limit=20, aliases=None):
@@ -338,42 +324,43 @@
     length_x = slab * spaces
     group = ("point", "space")
     bands = points * spaces
-    rows = length_y // (2 * bands)
+    small = length_y // (4 * bands)
     quarter = length_x // 4
-    table_x, tables_y = (cas_tables(length) for length in (length_x, length_y))
-    flops_y = [3 * 4 * slab * (length_y // 2) * (length_y // wide) for wide in (4, 2)]
-    flops_x = 3 * 4 * rows * points * length_x * 3 * length_x // 8
+    table_x, table_y = cas_tables(length_x), cas_tables(length_y)
     vmem, smem, hbm, sems = pltpu.VMEM, pltpu.SMEM, pltpu.HBM, pltpu.SemaphoreType.DMA
-    spectra_shape = (4, points, 2, rows, quarter)
-    turns_shape = (3, 2, 4, rows, quarter)
-
     lanes = math.gcd(slab, 128)
-    tall = slab // lanes * rows
-    heights = (2 * tall + 8, 2 * tall)
-
-    sent, turns = [], []
-    for odd in range(2):
-        table = tables_y[odd]
-        sent.append(
-            call(
-                functools.partial(forward_y, odd),
-                [counts, residual[0], table],
-                [(bands, heights[odd], lanes)],
-                flops_y[odd],
-                [smem, hbm, hbm],
-                [hbm],
-                scratch=[
-                    vmem(residual.shape[1:], f32),
-                    vmem((bands, heights[odd], lanes), f32),
-                    vmem(table.shape, bf16),
-                    sems((3,)),
-                    sems((2,)),
-                ],
-            )
-        )
+    height = 8 * (slab // lanes) * small + 8
+
+    def flops_y(parts):
+        return 3 * 4 * slab * parts * (length_y // 4) ** 2
+
+    sent = call(
+        forward_y,
+        [counts, residual[0], *table_y],
+        [(bands, height, lanes)],
+        flops_y(6),
+        [smem, hbm, hbm, hbm],
+        [hbm],
+        scratch=[
+            vmem(residual.shape[1:], f32),
+            vmem((bands, height, lanes), f32),
+            *[vmem(table.shape, bf16) for table in table_y],
+            sems((4,)),
+            sems((2,)),
+        ],
+    )
+    arrived = lax.all_to_all(sent, group, split_axis=0, concat_axis=0, tiled=True)
+    arrived = arrived.reshape(points, spaces, height, lanes)
+    turns, spectra, carry = [], [], []
+    shapes = []
+    for chunk, kinds in enumerate(CHUNKS):
+        rows = len(kinds) * small
+        shapes.append(((4, points, 2, rows, quarter), (3, 2, 4, rows, quarter)))
+        spectra_shape, turns_shape = shapes[-1]
+        flops_x = 3 * 4 * rows * points * 6 * quarter * quarter
         turns.append(
             call(
-                functools.partial(rotations, odd, length_x, length_y),
+                functools.partial(rotations, kinds, length_x, length_y),
                 [],
                 [turns_shape],
                 40 * 4 * rows * length_x,
@@ -382,36 +369,33 @@
                 scratch=[vmem(turns_shape, f32), sems((3,))],
             )
         )
-    spectra, carry = [None] * 2, [None] * 2
-    for odd in range(2):
-        arrived = lax.all_to_all(sent[odd], group, split_axis=0, concat_axis=0, tiled=True)
-        if odd:
-            arrived, spectra[0], later = lax.optimization_barrier((arrived, spectra[0], turns[0]))
-        arrived = arrived.reshape(points, spaces, heights[odd], lanes)
         folded = [vmem((4, points * 2 * rows, quarter), bf16)] * 2
         results = call(
-            functools.partial(forward_x, odd),
-            [near, arrived, turns[1], *table_x] if odd else [arrived, turns[0], *table_x],
-            [spectra_shape, (2, rows, length_x)] + ([] if odd else [(points,)]),
+            functools.partial(forward_x, kinds),
+            ([near] if chunk else []) + [arrived, turns[chunk], *table_x],
+            [spectra_shape, (2, rows, length_x)] + ([] if chunk else [(points,)]),
             flops_x,
-            [smem] * odd + [vmem, hbm, vmem, vmem],
-            [hbm, vmem] + ([] if odd else [smem]),
+            [smem] * chunk + [vmem, hbm, vmem, vmem],
+            [hbm, vmem] + ([] if chunk else [smem]),
             scratch=[vmem(turns_shape, f32), *folded, vmem(spectra_shape, f32), sems((1,)), sems((4,))],
         )
-        spectra[odd], last = results[:2]
-        if not odd:
+        spectra.append(results[0])
+        last = results[1]
+        if not chunk:
             near = results[2]
-        carry[odd] = lax.ppermute(last, "block", [(b, b + 1) for b in range(blocks - 1)])
+        carry.append(lax.ppermute(last, "block", [(b, b + 1) for b in range(blocks - 1)]))
         if blocks > 2:
-            total = jnp.sum(near).astype(f32) * (phase_rate / (2.0 * math.pi))
-            span = lax.ppermute(total, "block", [(b, b + 1) for b in range(blocks - 1)])
-            modulus = modulus_at(place(odd, rows, length_y), 0, (rows, length_x), length_x, length_y)
+            whole = jnp.sum(near).astype(f32) * (phase_rate / (2.0 * math.pi))
+            span = lax.ppermute(whole, "block", [(b, b + 1) for b in range(blocks - 1)])
+            start = own_band() * small
+            modulus = [modulus_at(kind, start, 0, (small, length_x), length_x, length_y) for kind in kinds]
+            modulus = jnp.concatenate(modulus, axis=0)
             reach = 1
             while reach < blocks - 1:
                 steps = [(b, b + reach) for b in range(blocks - reach)]
-                further = lax.ppermute(carry[odd], "block", steps)
+                further = lax.ppermute(carry[chunk], "block", steps)
                 cosine, sine = turn(span * modulus)
-                carry[odd] = carry[odd] + jnp.stack(
+                carry[chunk] = carry[chunk] + jnp.stack(
                     [
                         cosine * further[0] + sine * further[1],
                         cosine * further[1] - sine * further[0],
@@ -421,44 +405,54 @@
                 reach *= 2
     carry[0], spectra[1] = lax.optimization_barrier((carry[0], spectra[1]))
     solved = []
-    for odd in range(2):
+    for chunk, kinds in enumerate(CHUNKS):
+        rows = len(kinds) * small
+        spectra_shape, turns_shape = shapes[chunk]
         back = call(
             functools.partial(finish_x, 1.0 / (length_x * length_y)),
-            [near, spectra[odd], carry[odd], turns[1] if odd else later, *table_x],
+            [near, spectra[chunk], carry[chunk], turns[chunk], *table_x],
             [(points, spaces, 2, rows, slab)],
-            flops_x,
-            [smem, hbm, vmem, hbm, vmem, vmem] if odd else [smem] + [vmem] * 5,
+            3 * 4 * rows * points * 6 * quarter * quarter,
+            [smem, hbm, vmem, hbm, vmem, vmem] if chunk else [smem] + [vmem] * 5,
             [hbm],
             scratch=[
                 vmem((spaces, points, 2, rows, slab), f32),
                 vmem(spectra_shape, f32),
                 sems((spaces,)),
             ]
-            + [vmem(spectra_shape, f32), vmem(turns_shape, f32), sems((2,))] * odd,
+            + [vmem(spectra_shape, f32), vmem(turns_shape, f32), sems((2,))] * chunk,
         )
         back = back.reshape(bands, 2, rows, slab)
         solved.append(lax.all_to_all(back, group, split_axis=0, concat_axis=0, tiled=True))
-    half = (2, slab, length_y // 2)
-    even, _ = call(
-        inverse_y_even,
-        [solved[0], tables_y[0]],
-        [half, solved[0].shape],
-        flops_y[0],
+    part_shape = (2, slab, length_y // 4)
+    first, _ = call(
+        inverse_y_first,
+        [solved[0], table_y[0]],
+        [part_shape, solved[0].shape],
+        flops_y(1),
         [hbm, vmem],
         [hbm, hbm],
         aliases={0: 1},
-        scratch=[vmem((bands, 2, rows, slab), f32), vmem(half, f32), sems((1,)), sems((2,))],
+        scratch=[vmem(solved[0].shape, f32), vmem(part_shape, f32), sems((1,)), sems((2,))],
     )
     fields = call(
-        inverse_y_odd,
-        [solved[1], even, tables_y[1]],
+        inverse_y_rest,
+        [solved[1], first, *table_y],
         [(2, slab, length_y)],
-        flops_y[1],
-        [vmem, hbm, vmem],
+        flops_y(5),
+        [vmem, hbm, vmem, vmem],
         [hbm],
-        scratch=[vmem(half, f32), vmem((2, slab, length_y), f32), sems((1,)), sems((2 * slab // lanes,))],
+        scratch=[
+            vmem(part_shape, f32),
+            vmem((2, slab, length_y), f32),
+            sems((1,)),
+            sems((2 * slab // lanes,)),
+        ],
     )
     return fields[None]
+
+
+CHUNKS = ((0,), (1, 2, 3))
 
 
 def solution(mesh):

time: 105 us -> 118 us (1.12)
  waiting for transfers between devices: 45.4 us -> 58.9 us
  starting transfers between devices: 31.2 us -> 35.5 us
  Pallas kernels: 25.6 us -> 22.3 us
    all_to_all x2 -> x1, waiting for transfers between devices: 19.1 us -> 28.8 us  [on_device(): lax.all_to_all(sent, group, split_axis=0, concat_axis=0, tiled=True)]
    all_to_all x2, starting transfers between devices: 11.4 us -> 19.2 us  [on_device(): lax.all_to_all(back, group, split_axis=0, concat_axis=0, tiled=True)]
    all_to_all x2, waiting for transfers between devices: 13.4 us -> 20.2 us  [on_device(): lax.all_to_all(back, group, split_axis=0, concat_axis=0, tiled=True)]
    all_to_all x2 -> x1, starting transfers between devices: 9.98 us -> 6.46 us  [on_device(): lax.all_to_all(sent, group, split_axis=0, concat_axis=0, tiled=True)]
    pallas_call x10 -> x9, Pallas kernels: 25.6 us -> 22.3 us  [call(): pl.pallas_call(kernel, in_specs=[pl.BlockSpec(memory_space=space) for spa...]
    ppermute x2, waiting for transfers between devices: 12.9 us -> 9.89 us  [on_device(): lax.ppermute(last, 'block', [(b, b + 1) for b in range(blocks - 1)])]
  transfers between devices with their start and end apart: 6 -> 5, of which waited for: 4 -> 3; matrix products, arithmetic and copies ran while one was open for 0% -> 0% of each run, Pallas kernels for 16% -> 10%
where the time goes in v4:
time: 118 us
  waiting for transfers between devices  58.9 us (50%)
  starting transfers between devices  35.5 us (30%)
  Pallas kernels  22.3 us (19%)
    all_to_all x1, waiting for transfers between devices, on_device(): lax.all_to_all(sent, group, split_axis=0, concat_axis=0, tiled=True)  28.8 us
    pallas_call x9, Pallas kernels, call(): pl.pallas_call(kernel, in_specs=[pl.BlockSpec(memory_space=space) for spa...  22.3 us
    all_to_all x2, waiting for transfers between devices, on_device(): lax.all_to_all(back, group, split_axis=0, concat_axis=0, tiled=True)  20.2 us
    all_to_all x2, starting transfers between devices, on_device(): lax.all_to_all(back, group, split_axis=0, concat_axis=0, tiled=True)  19.2 us
    ppermute x2, waiting for transfers between devices, on_device(): lax.ppermute(last, 'block', [(b, b + 1) for b in range(blocks - 1)])  9.89 us
    ppermute x2, starting transfers between devices, on_device(): lax.ppermute(last, 'block', [(b, b + 1) for b in range(blocks - 1)])  9.81 us
    all_to_all x1, starting transfers between devices, on_device(): lax.all_to_all(sent, group, split_axis=0, concat_axis=0, tiled=True)  6.46 us
  transfers between devices with their start and end apart: 5, of which 3 were waited for; matrix products, arithmetic and copies ran while one was open for 0% of the time, Pallas kernels for 10%

profile of v4, /device:TPU:0, one launch (start us, length us, event | category | flops | bytes accessed | tf_op | source)
XLA Modules:
  0.0 117.5 jit_solution(7790160159086695082)
XLA Ops:
  0.7 4.3 %shard_map.64 = f32[16,264,128]{2,1,0:T(8,128)} custom-call(s32[1]{0:T(128)S(6)} %copy.9.count_ref, f32[2,256,1024]{2,1,0:T(8,128)} %bitcast.8, bf16[2,2,256,256]{3,2,1,0:T(8,128)(2,1)} %constant.4.clone.even_hbm.refs_2_.refs_3_.even, bf16[2,2,256,256]{3,2,1,0:T(8,128)(2,1)} %constant.5.clone.odd_hbm.refs_3_.refs_4_.mixing), custom_call_target="tpu_custom_call" | custom-call | flops 1207959552 | bytes 5308420 | tf_op jit(solution)/shard_map/pallas_call | solution.py:309
  4.9 0.0 copy-start
  5.0 0.0 copy-start.1
  5.0 6.5 %all-to-all-start = ((f32[16,264,128]{2,1,0:T(8,128)}), f32[16,264,128]{2,1,0:T(8,128)S(1)}, u32[]{:S(2)}, u32[]{:S(2)}) async-start(f32[16,264,128]{2,1,0:T(8,128)} %shard_map.64), calls=%async_computation | async-start | bytes 4325376 | tf_op jit(solution)/shard_map/all_to_all | solution.py:352
  11.4 1.1 shard_map.65.refs_1_.turns
  12.5 28.8 %all-to-all-done = f32[16,264,128]{2,1,0:T(8,128)S(1)} async-done(((f32[16,264,128]{2,1,0:T(8,128)}), f32[16,264,128]{2,1,0:T(8,128)S(1)}, u32[]{:S(2)}, u32[]{:S(2)}) %all-to-all-start) | async-done | bytes 2162720 | tf_op jit(solution)/shard_map/all_to_all | solution.py:352
  41.3 0.0 copy-done
  41.3 0.0 copy-done.1
  41.3 1.9 %shard_map.66 = (f32[4,4,2,16,256]{4,3,2,1,0:T(8,128)}, f32[2,16,1024]{2,1,0:T(8,128)S(1)}, s32[4]{0:T(128)S(4)}) custom-call(f32[4,4,264,128]{3,2,1,0:T(8,128)S(1)} %bitcast.5, f32[3,2,4,16,256]{4,3,2,1,0:T(8,128)} %shard_map.65.refs_1_.turns, bf16[2,2,256,256]{3,2,1,0:T(8,128)(2,1)S(1)} %copy-done, bf16[2,2,256,256]{3,2,1,0:T(8,128)(2,1)S(1)} %copy-done.1), custom_call_target="tpu_custom_call" | custom-call | flops 301989888 | bytes 4259856 | tf_op jit(solution)/shard_map/pallas_call | solution.py:309
  43.2 4.5 %collective-permute-start = (f32[2,16,1024]{2,1,0:T(8,128)S(1)}, f32[2,16,1024]{2,1,0:T(8,128)S(1)}, u32[]{:S(2)}, u32[]{:S(2)}) collective-permute-start(f32[2,16,1024]{2,1,0:T(8,128)S(1)} %get-tuple-element.14), channel_id=1, source_target_pairs={{0,16},{1,17},{2,18},{3,19},{4,20},{5,21},{6,22},{7,23},{8,24},{9,... | collective-permute-start | bytes 393224 | tf_op jit(solution)/shard_map/ppermute | solution.py:386
  47.7 2.0 %shard_map.67.refs_2_.turns = f32[3,2,4,48,256]{4,3,2,1,0:T(8,128)} custom-call(), custom_call_target="tpu_custom_call" | custom-call | flops 7864320 | bytes 1179648 | tf_op jit(solution)/shard_map/pallas_call | solution.py:309
  49.6 0.0 copy-start.2
  49.6 0.0 copy-start.3
  49.7 2.4 %shard_map.68 = (f32[4,4,2,48,256]{4,3,2,1,0:T(8,128)}, f32[2,48,1024]{2,1,0:T(8,128)S(1)}) custom-call(s32[4]{0:T(128)S(4)} %get-tuple-element.13.refs_0_.count_ref, f32[4,4,264,128]{3,2,1,0:T(8,128)S(1)} %bitcast.6, f32[3,2,4,48,256]{4,3,2,1,0:T(8,128)} %shard_map.67.refs_2_.turns, bf16[2,2,256,256]{3,2,1,0:T(8,128)(2,1)S(1)} %copy-done, ...), custom_call_target="tpu_custom_call" | custom-call | flops 905969664 | bytes 6357008 | tf_op jit(solution)/shard_map/pallas_call | solution.py:309
  52.1 0.0 copy-start.4
  52.1 0.0 collective-permute-done.carry
  52.1 0.0 copy-done.2
  52.1 0.0 copy-done.3
  52.1 1.3 %shard_map.70 = f32[4,4,2,16,256]{4,3,2,1,0:T(8,128)} custom-call(s32[4]{0:T(128)S(4)} %get-tuple-element.13.refs_0_.count_ref, f32[4,4,2,16,256]{4,3,2,1,0:T(8,128)S(1)} %copy-done.3, f32[2,16,1024]{2,1,0:T(8,128)S(1)} %collective-permute-done.carry, f32[3,2,4,16,256]{4,3,2,1,0:T(8,128)S(1)} %copy-done.2, bf16[2,2,256,256]{3,2,1,0:T(8,128)(2,1)S(1)} %copy-done, ...), custom_call_target="tpu_custom_call" | custom-call | flops 301989888 | bytes 2621456 | tf_op jit(solution)/shard_map/pallas_call | solution.py:309
  53.4 0.0 copy-done.4
  53.5 6.7 %all-to-all-start.2 = ((f32[16,2,16,256]{3,2,1,0:T(8,128)}), f32[16,2,16,256]{3,2,1,0:T(8,128)S(1)}, u32[]{:S(2)}, u32[]{:S(2)}) async-start(f32[16,2,16,256]{3,2,1,0:T(8,128)} %bitcast.9), calls=%async_computation.2 | async-start | bytes 1048576 | tf_op jit(solution)/shard_map/all_to_all | solution.py:426
  60.1 5.3 %collective-permute-start.1 = (f32[2,48,1024]{2,1,0:T(8,128)}, f32[2,48,1024]{2,1,0:T(8,128)S(1)}, u32[]{:S(2)}, u32[]{:S(2)}) collective-permute-start(f32[2,48,1024]{2,1,0:T(8,128)} %copy-done.4), channel_id=1, source_target_pairs={{0,16},{1,17},{2,18},{3,19},{4,20},{5,21},{6,22},{7,23},{8,24},{9,... | collective-permute-start | bytes 1179656 | tf_op jit(solution)/shard_map/ppermute | solution.py:386
  65.5 9.9 %collective-permute-done.1.carry = f32[2,48,1024]{2,1,0:T(8,128)S(1)} collective-permute-done((f32[2,48,1024]{2,1,0:T(8,128)}, f32[2,48,1024]{2,1,0:T(8,128)S(1)}, u32[]{:S(2)}, u32[]{:S(2)}) %collective-permute-start.1) | collective-permute-done | bytes 393248 | tf_op jit(solution)/shard_map/ppermute | solution.py:386
  75.3 4.1 %shard_map.69 = f32[4,4,2,48,256]{4,3,2,1,0:T(8,128)} custom-call(s32[4]{0:T(128)S(4)} %get-tuple-element.13.refs_0_.count_ref, f32[4,4,2,48,256]{4,3,2,1,0:T(8,128)} %get-tuple-element.16.spectra, f32[2,48,1024]{2,1,0:T(8,128)S(1)} %collective-permute-done.1.carry, f32[3,2,4,48,256]{4,3,2,1,0:T(8,128)} %shard_map.67.refs_2_.turns, ...), custom_call_target="tpu_custom_call" | custom-call | flops 905969664 | bytes 5767184 | tf_op jit(solution)/shard_map/pallas_call | solution.py:309
  79.5 0.0 all-to-all-done.2.r_hbm
  79.5 0.0 copy-start.5
  79.5 12.6 %all-to-all-start.1 = ((f32[16,2,48,256]{3,2,1,0:T(8,128)}), f32[16,2,48,256]{3,2,1,0:T(8,128)S(1)}, u32[]{:S(2)}, u32[]{:S(2)}) async-start(f32[16,2,48,256]{3,2,1,0:T(8,128)} %bitcast.7), calls=%async_computation.1 | async-start | bytes 3145728 | tf_op jit(solution)/shard_map/all_to_all | solution.py:426
  92.1 0.0 copy-done.5
  92.1 2.3 %shard_map.71 = (f32[2,256,256]{2,1,0:T(8,128)}, f32[16,2,16,256]{3,2,1,0:T(8,128)}) custom-call(f32[16,2,16,256]{3,2,1,0:T(8,128)} %copy-done.5, bf16[2,2,256,256]{3,2,1,0:T(8,128)(2,1)S(1)} %copy-done), custom_call_target="tpu_custom_call", output_to_operand_aliasing={{1}: (0, {})} | custom-call | flops 201326592 | bytes 2097152 | tf_op jit(solution)/shard_map/pallas_call | solution.py:309
  94.4 20.2 %all-to-all-done.1.r_ref = f32[16,2,48,256]{3,2,1,0:T(8,128)S(1)} async-done(((f32[16,2,48,256]{3,2,1,0:T(8,128)}), f32[16,2,48,256]{3,2,1,0:T(8,128)S(1)}, u32[]{:S(2)}, u32[]{:S(2)}) %all-to-all-start.1) | async-done | bytes 1572896 | tf_op jit(solution)/shard_map/all_to_all | solution.py:426
  114.6 2.9 %shard_map.72 = f32[2,256,1024]{2,1,0:T(8,128)} custom-call(f32[16,2,48,256]{3,2,1,0:T(8,128)S(1)} %all-to-all-done.1.r_ref, f32[2,256,256]{2,1,0:T(8,128)} %get-tuple-element.20.first_hbm, bf16[2,2,256,256]{3,2,1,0:T(8,128)(2,1)S(1)} %copy-done, bf16[2,2,256,256]{3,2,1,0:T(8,128)(2,1)S(1)} %copy-done.1), custom_call_target="tpu_custom_call" | custom-call | flops 1006632960 | bytes 5242880 | tf_op jit(solution)/shard_map/pallas_call | solution.py:309
Async XLA Ops:
  4.9 36.4 %copy-start = (bf16[2,2,256,256]{3,2,1,0:T(8,128)(2,1)S(1)}, bf16[2,2,256,256]{3,2,1,0:T(8,128)(2,1)}, u32[]{:S(2)}) copy-start(bf16[2,2,256,256]{3,2,1,0:T(8,128)(2,1)} %constant.4.clone.even_hbm.refs_2_.refs_3_.even) | copy-start | bytes 1572868
  5.0 36.3 %copy-start.1 = (bf16[2,2,256,256]{3,2,1,0:T(8,128)(2,1)S(1)}, bf16[2,2,256,256]{3,2,1,0:T(8,128)(2,1)}, u32[]{:S(2)}) copy-start(bf16[2,2,256,256]{3,2,1,0:T(8,128)(2,1)} %constant.5.clone.odd_hbm.refs_3_.refs_4_.mixing) | copy-start | bytes 1572868
  5.0 36.3 %all-to-all-start = ((f32[16,264,128]{2,1,0:T(8,128)}), f32[16,264,128]{2,1,0:T(8,128)S(1)}, u32[]{:S(2)}, u32[]{:S(2)}) async-start(f32[16,264,128]{2,1,0:T(8,128)} %shard_map.64), calls=%async_computation | async-start | bytes 4325376 | tf_op jit(solution)/shard_map/all_to_all | solution.py:352
  43.2 8.9 %collective-permute-start = (f32[2,16,1024]{2,1,0:T(8,128)S(1)}, f32[2,16,1024]{2,1,0:T(8,128)S(1)}, u32[]{:S(2)}, u32[]{:S(2)}) collective-permute-start(f32[2,16,1024]{2,1,0:T(8,128)S(1)} %get-tuple-element.14), channel_id=1, source_target_pairs={{0,16},{1,17},{2,18},{3,19},{4,20},{5,21},{6,22},{7,23},{8,24},{9,... | collective-permute-start | bytes 393224 | tf_op jit(solution)/shard_map/ppermute | solution.py:386
  49.6 2.5 %copy-start.2 = (f32[3,2,4,16,256]{4,3,2,1,0:T(8,128)S(1)}, f32[3,2,4,16,256]{4,3,2,1,0:T(8,128)}, u32[]{:S(2)}) copy-start(f32[3,2,4,16,256]{4,3,2,1,0:T(8,128)} %shard_map.65.refs_1_.turns) | copy-start | bytes 1179652
  49.6 2.5 %copy-start.3 = (f32[4,4,2,16,256]{4,3,2,1,0:T(8,128)S(1)}, f32[4,4,2,16,256]{4,3,2,1,0:T(8,128)}, u32[]{:S(2)}) copy-start(f32[4,4,2,16,256]{4,3,2,1,0:T(8,128)} %get-tuple-element.18.spectra) | copy-start | bytes 1572868
  52.1 1.4 %copy-start.4 = (f32[2,48,1024]{2,1,0:T(8,128)}, f32[2,48,1024]{2,1,0:T(8,128)S(1)}, u32[]{:S(2)}) copy-start(f32[2,48,1024]{2,1,0:T(8,128)S(1)} %get-tuple-element.17) | copy-start | bytes 1179652
  53.5 26.0 %all-to-all-start.2 = ((f32[16,2,16,256]{3,2,1,0:T(8,128)}), f32[16,2,16,256]{3,2,1,0:T(8,128)S(1)}, u32[]{:S(2)}, u32[]{:S(2)}) async-start(f32[16,2,16,256]{3,2,1,0:T(8,128)} %bitcast.9), calls=%async_computation.2 | async-start | bytes 1048576 | tf_op jit(solution)/shard_map/all_to_all | solution.py:426
  60.1 15.2 %collective-permute-start.1 = (f32[2,48,1024]{2,1,0:T(8,128)}, f32[2,48,1024]{2,1,0:T(8,128)S(1)}, u32[]{:S(2)}, u32[]{:S(2)}) collective-permute-start(f32[2,48,1024]{2,1,0:T(8,128)} %copy-done.4), channel_id=1, source_target_pairs={{0,16},{1,17},{2,18},{3,19},{4,20},{5,21},{6,22},{7,23},{8,24},{9,... | collective-permute-start | bytes 1179656 | tf_op jit(solution)/shard_map/ppermute | solution.py:386
  79.5 12.6 %copy-start.5 = (f32[16,2,16,256]{3,2,1,0:T(8,128)}, f32[16,2,16,256]{3,2,1,0:T(8,128)S(1)}, u32[]{:S(2)}) copy-start(f32[16,2,16,256]{3,2,1,0:T(8,128)S(1)} %all-to-all-done.2.r_hbm) | copy-start | bytes 1572868
  79.5 35.1 %all-to-all-start.1 = ((f32[16,2,48,256]{3,2,1,0:T(8,128)}), f32[16,2,48,256]{3,2,1,0:T(8,128)S(1)}, u32[]{:S(2)}, u32[]{:S(2)}) async-start(f32[16,2,48,256]{3,2,1,0:T(8,128)} %bitcast.7), calls=%async_computation.1 | async-start | bytes 3145728 | tf_op jit(solution)/shard_map/all_to_all | solution.py:426

commit v5 on v4

--- a/solution.py
+++ b/solution.py
@@ -113,30 +113,37 @@
         copy.wait()
 
 
-def forward_y(count_ref, x_hbm, even_hbm, odd_hbm, out_hbm, x_ref, out, even, mixing, sems, out_sems):
-    pairs = [(x_hbm.at[0], x_ref.at[0]), (even_hbm, even), (odd_hbm, mixing), (x_hbm.at[1], x_ref.at[1])]
+def forward_y(kinds, late, count_ref, x_hbm, even_hbm, odd_hbm, out_hbm, x_ref, out, even, mixing, sems, out_sems):
+    pairs = [(x_hbm.at[0], x_ref.at[0]), (even_hbm, even), (x_hbm.at[1], x_ref.at[1])]
+    if kinds[-1] > 1:
+        pairs.insert(1, (odd_hbm, mixing))
     copies = copy_in(pairs, sems)
     bands, height, lanes = out.shape
     slab, length_y = x_ref.shape[1:]
     quarter = length_y // 4
     small = quarter // bands
-    tall = slab // lanes * 4 * small
-    out[:, 2 * tall :] = jnp.full((bands, height - 2 * tall, lanes), count_ref[0].astype(f32))
+    tall = slab // lanes * len(kinds) * small
+    if not late:
+        out[:, 2 * tall :] = jnp.full((bands, height - 2 * tall, lanes), count_ref[0].astype(f32))
     wait_all(copies[:-1])
     stores = []
     for part in range(2):
         if part:
             copies[-1].wait()
         pieces = [x_ref[part, :, q * quarter : (q + 1) * quarter] for q in range(4)]
-        first, second = halves(pieces[0] - pieces[2]), halves(pieces[1] - pieces[3])
-        plain, turned = mixing[0], mixing[1]
-        results = [product(even[half], halves(value), NT) for half, value in enumerate(fold(pieces))]
-        results.append(product(plain, first, NT) + product(turned, second, NT))
-        results.append(product(turned, first, NT) - product(plain, second, NT))
-        for kind, result in enumerate(results):
+        results = {}
+        for kind, value in enumerate(fold(pieces)):
+            if kind in kinds:
+                results[kind] = product(even[kind], halves(value), NT)
+        if kinds[-1] > 1:
+            first, second = halves(pieces[0] - pieces[2]), halves(pieces[1] - pieces[3])
+            plain, turned = mixing[0], mixing[1]
+            results[2] = product(plain, first, NT) + product(turned, second, NT)
+            results[3] = product(turned, first, NT) - product(plain, second, NT)
+        for index, kind in enumerate(kinds):
             for piece in range(slab // lanes):
-                start = part * tall + (piece * 4 + kind) * small
-                wanted = result[:, piece * lanes : (piece + 1) * lanes]
+                start = part * tall + (piece * len(kinds) + index) * small
+                wanted = results[kind][:, piece * lanes : (piece + 1) * lanes]
                 out[:, start : start + small] = wanted.reshape(bands, small, lanes)
         here = pl.ds(part * tall, height - tall if part else tall)
         copy_out(stores, out.at[:, here], out_hbm.at[:, here], out_sems.at[part])
@@ -165,9 +172,8 @@
     wait_all(stores)
 
 
-def forward_x(kinds, *refs):
+def forward_x(late, *refs):
     refs, (turns, highs, lows, spectra, turn_sem, out_sems) = refs[:-6], refs[-6:]
-    late = kinds[0] > 0
     if late:
         count_ref, r_ref, turns_hbm, even, mixing, spectra_hbm, last = refs
     else:
@@ -176,9 +182,7 @@
     _, _, rows, quarter = spectra.shape[1:]
     slab = 4 * quarter // spaces
     wide = slab // lanes
-    small = rows // len(kinds)
-    stride, offset = 4 * small, kinds[0] * small
-    tall = wide * stride
+    tall = wide * rows
     count = 2 * rows
     turn_copy = pltpu.make_async_copy(turns_hbm, turns, turn_sem.at[0])
     turn_copy.start()
@@ -189,7 +193,7 @@
     def gather(n, _):
         pieces = []
         for s in range(spaces):
-            slices = [r_ref[n, s, start : start + rows] for start in range(offset, 2 * tall, stride)]
+            slices = [r_ref[n, s, start : start + rows] for start in range(0, 2 * tall, rows)]
             parts = [jnp.concatenate(slices[part * wide : (part + 1) * wide], axis=-1) for part in range(2)]
             pieces.append(jnp.concatenate(parts, axis=0))
         if spaces != 4:
@@ -229,10 +233,8 @@
     wait_all(stores)
 
 
-def finish_x(scaling, count_ref, spectra, carry, turns, even, mixing, out_hbm, out, states, out_sems, *scratch):
-    if scratch:
-        spectra_hbm, turns_hbm, (spectra, turns, sems) = spectra, turns, scratch
-        wait_all(copy_in([(turns_hbm, turns), (spectra_hbm, spectra)], sems))
+def finish_x(scaling, first_row, count_ref, spectra, carry, turns, even, mixing, *refs):
+    out_hbm, out, states, out_sems = refs[-4:]
     spaces, points, _, rows, slab = out.shape
     quarter = spaces * slab // 4
     count = points * 2 * rows
@@ -258,40 +260,28 @@
     stores = []
     for s in range(spaces):
         out[s] = results[s].reshape(points, 2, rows, slab)
-        copy_out(stores, out.at[s], out_hbm.at[:, s], out_sems.at[s])
+        there = (slice(None), s, slice(None), pl.ds(first_row, rows))
+        copy_out(stores, out.at[s], out_hbm.at[there], out_sems.at[s])
     wait_all(stores)
 
 
-def inverse_y_first(r_hbm, even, out_hbm, _, r_ref, out, in_sems, sems):
-    wait_all(copy_in([(r_hbm, r_ref)], in_sems))
+def inverse_y(r_ref, even, mixing, out_hbm, out, out_sems):
     bands, _, rows, slab = r_ref.shape
-    stores = []
-    for part in range(2):
-        out[part] = product(halves(r_ref[:, part].reshape(bands * rows, slab)), even[0], TN)
-        copy_out(stores, out.at[part], out_hbm.at[part], sems.at[part])
-    wait_all(stores)
-
-
-def inverse_y_rest(r_ref, first_hbm, even, mixing, out_hbm, total, out, sems, out_sems):
-    bands, _, rows, slab = r_ref.shape
-    small = rows // 3
-    quarter = total.shape[-1]
+    small = rows // 4
+    quarter = out.shape[-1] // 4
     pieces = slab // math.gcd(slab, 128)
     step = slab // pieces
-    copies = copy_in([(first_hbm, total)], sems)
     stores = []
     for part in range(2):
         for piece in range(pieces):
             here = slice(piece * step, (piece + 1) * step)
             waves = [
-                halves(r_ref[:, part, kind * small : (kind + 1) * small, here].reshape(bands * small, step))
-                for kind in range(3)
+                halves(r_ref[:, part, index * small : (index + 1) * small, here].reshape(bands * small, step))
+                for index in range(4)
             ]
-            alternate = product(waves[0], even[1], TN)
+            alternate, total = product(waves[0], even[1], TN), product(waves[3], even[0], TN)
             straight, crossed = mix(waves[1], waves[2], mixing, TN)
-            if not stores:
-                wait_all(copies)
-            plus, minus = total[part, here] + alternate, total[part, here] - alternate
+            plus, minus = total + alternate, total - alternate
             for q, result in enumerate((plus + straight, minus + crossed, plus - straight, minus - crossed)):
                 out[part, here, q * quarter : (q + 1) * quarter] = result
             there = pl.ds(piece * step, step)
@@ -329,28 +319,30 @@
     table_x, table_y = cas_tables(length_x), cas_tables(length_y)
     vmem, smem, hbm, sems = pltpu.VMEM, pltpu.SMEM, pltpu.HBM, pltpu.SemaphoreType.DMA
     lanes = math.gcd(slab, 128)
-    height = 8 * (slab // lanes) * small + 8
 
     def flops_y(parts):
         return 3 * 4 * slab * parts * (length_y // 4) ** 2
 
-    sent = call(
-        forward_y,
-        [counts, residual[0], *table_y],
-        [(bands, height, lanes)],
-        flops_y(6),
-        [smem, hbm, hbm, hbm],
-        [hbm],
-        scratch=[
-            vmem(residual.shape[1:], f32),
-            vmem((bands, height, lanes), f32),
-            *[vmem(table.shape, bf16) for table in table_y],
-            sems((4,)),
-            sems((2,)),
-        ],
-    )
-    arrived = lax.all_to_all(sent, group, split_axis=0, concat_axis=0, tiled=True)
-    arrived = arrived.reshape(points, spaces, height, lanes)
+    sent = []
+    for chunk, kinds in enumerate(CHUNKS):
+        height = 2 * (slab // lanes) * len(kinds) * small + 8 * (1 - chunk)
+        sent.append(
+            call(
+                functools.partial(forward_y, kinds, chunk),
+                [counts, residual[0], *table_y],
+                [(bands, height, lanes)],
+                flops_y(1 if chunk else 5),
+                [smem, hbm, hbm, hbm],
+                [hbm],
+                scratch=[
+                    vmem(residual.shape[1:], f32),
+                    vmem((bands, height, lanes), f32),
+                    *[vmem(table.shape, bf16) for table in table_y],
+                    sems((4,)),
+                    sems((2,)),
+                ],
+            )
+        )
     turns, spectra, carry = [], [], []
     shapes = []
     for chunk, kinds in enumerate(CHUNKS):
@@ -370,8 +362,10 @@
             )
         )
         folded = [vmem((4, points * 2 * rows, quarter), bf16)] * 2
+        arrived = lax.all_to_all(sent[chunk], group, split_axis=0, concat_axis=0, tiled=True)
+        arrived = arrived.reshape(points, spaces, arrived.shape[1], lanes)
         results = call(
-            functools.partial(forward_x, kinds),
+            functools.partial(forward_x, chunk),
             ([near] if chunk else []) + [arrived, turns[chunk], *table_x],
             [spectra_shape, (2, rows, length_x)] + ([] if chunk else [(points,)]),
             flops_x,
@@ -403,56 +397,39 @@
                 )
                 span = span + lax.ppermute(span, "block", steps)
                 reach *= 2
-    carry[0], spectra[1] = lax.optimization_barrier((carry[0], spectra[1]))
-    solved = []
+    back = None
     for chunk, kinds in enumerate(CHUNKS):
         rows = len(kinds) * small
         spectra_shape, turns_shape = shapes[chunk]
         back = call(
-            functools.partial(finish_x, 1.0 / (length_x * length_y)),
-            [near, spectra[chunk], carry[chunk], turns[chunk], *table_x],
-            [(points, spaces, 2, rows, slab)],
+            functools.partial(finish_x, 1.0 / (length_x * length_y), 0 if not chunk else 4 * small - rows),
+            [near, spectra[chunk], carry[chunk], turns[chunk], *table_x] + [back] * chunk,
+            [(points, spaces, 2, 4 * small, slab)],
             3 * 4 * rows * points * 6 * quarter * quarter,
-            [smem, hbm, vmem, hbm, vmem, vmem] if chunk else [smem] + [vmem] * 5,
+            [smem] + [vmem] * 5 + [hbm] * chunk,
             [hbm],
+            aliases={6: 0} if chunk else None,
             scratch=[
                 vmem((spaces, points, 2, rows, slab), f32),
                 vmem(spectra_shape, f32),
                 sems((spaces,)),
-            ]
-            + [vmem(spectra_shape, f32), vmem(turns_shape, f32), sems((2,))] * chunk,
+            ],
         )
-        back = back.reshape(bands, 2, rows, slab)
-        solved.append(lax.all_to_all(back, group, split_axis=0, concat_axis=0, tiled=True))
-    part_shape = (2, slab, length_y // 4)
-    first, _ = call(
-        inverse_y_first,
-        [solved[0], table_y[0]],
-        [part_shape, solved[0].shape],
-        flops_y(1),
-        [hbm, vmem],
-        [hbm, hbm],
-        aliases={0: 1},
-        scratch=[vmem(solved[0].shape, f32), vmem(part_shape, f32), sems((1,)), sems((2,))],
-    )
+    back = back.reshape(bands, 2, 4 * small, slab)
+    solved = lax.all_to_all(back, group, split_axis=0, concat_axis=0, tiled=True)
     fields = call(
-        inverse_y_rest,
-        [solved[1], first, *table_y],
+        inverse_y,
+        [solved, *table_y],
         [(2, slab, length_y)],
-        flops_y(5),
-        [vmem, hbm, vmem, vmem],
+        flops_y(6),
+        [vmem, vmem, vmem],
         [hbm],
-        scratch=[
-            vmem(part_shape, f32),
-            vmem((2, slab, length_y), f32),
-            sems((1,)),
-            sems((2 * slab // lanes,)),
-        ],
+        scratch=[vmem((2, slab, length_y), f32), sems((2 * slab // lanes,))],
     )
     return fields[None]
 
 
-CHUNKS = ((0,), (1, 2, 3))
+CHUNKS = ((1, 2, 3), (0,))
 
 
 def solution(mesh):

time: 118 us -> 109 us (0.924)
  blocking collectives: 0 us -> 42.9 us
  waiting for transfers between devices: 58.9 us -> 23.1 us
  starting transfers between devices: 35.5 us -> 18.9 us
  local copies, waits for them, and re-layouts: 0.03 us -> 1.43 us
    all_to_all x0 -> x1, blocking collectives: none -> 42.9 us  [on_device(): lax.all_to_all(back, group, split_axis=0, concat_axis=0, tiled=True)]
    all_to_all x3 -> x2, waiting for transfers between devices: 49 us -> 20.1 us  [on_device(): lax.all_to_all(sent[chunk], group, split_axis=0, concat_axis=0, tiled=True)]
    all_to_all x3 -> x2, starting transfers between devices: 25.7 us -> 10.3 us  [on_device(): lax.all_to_all(sent[chunk], group, split_axis=0, concat_axis=0, tiled=True)]
    ppermute x2, waiting for transfers between devices: 9.89 us -> 3 us  [on_device(): lax.ppermute(last, 'block', [(b, b + 1) for b in range(blocks - 1)])]
    unnamed x12, local copies, waits for them, and re-layouts: 0.03 us -> 1.43 us
    ppermute x2, starting transfers between devices: 9.81 us -> 8.62 us  [on_device(): lax.ppermute(last, 'block', [(b, b + 1) for b in range(blocks - 1)])]
  transfers between devices with their start and end apart: 5 -> 4, of which waited for: 3 -> 2; matrix products, arithmetic and copies ran while one was open for 0% -> 0% of each run, Pallas kernels for 10% -> 13%
where the time goes in v5:
time: 109 us; the launch traced here: 108 us
  blocking collectives  42.9 us (39%)
  waiting for transfers between devices  23.1 us (21%)
  Pallas kernels  21.3 us (20%)
  starting transfers between devices  18.9 us (17%)
  local copies, waits for them, and re-layouts  1.43 us (1%)
    all_to_all x1, blocking collectives, on_device(): lax.all_to_all(back, group, split_axis=0, concat_axis=0, tiled=True)  42.9 us
    pallas_call x9, Pallas kernels, call(): pl.pallas_call(kernel, in_specs=[pl.BlockSpec(memory_space=space) for spa...  21.3 us
    all_to_all x2, waiting for transfers between devices, on_device(): lax.all_to_all(sent[chunk], group, split_axis=0, concat_axis=0, tiled=True)  20.1 us
    all_to_all x2, starting transfers between devices, on_device(): lax.all_to_all(sent[chunk], group, split_axis=0, concat_axis=0, tiled=True)  10.3 us
    ppermute x2, starting transfers between devices, on_device(): lax.ppermute(last, 'block', [(b, b + 1) for b in range(blocks - 1)])  8.62 us
    ppermute x2, waiting for transfers between devices, on_device(): lax.ppermute(last, 'block', [(b, b + 1) for b in range(blocks - 1)])  3 us
  transfers between devices with their start and end apart: 4, of which 2 were waited for; matrix products, arithmetic and copies ran while one was open for 0% of the time, Pallas kernels for 13%

profile of v5, /device:TPU:0, one launch (start us, length us, event | category | flops | bytes accessed | tf_op | source)
XLA Modules:
  0.0 108.5 jit_solution(17422289013374536375)
XLA Ops:
  0.7 4.2 %shard_map.64 = f32[16,200,128]{2,1,0:T(8,128)} custom-call(s32[1]{0:T(128)S(6)} %copy.9.count_ref, f32[2,256,1024]{2,1,0:T(8,128)} %bitcast.8, bf16[2,2,256,256]{3,2,1,0:T(8,128)(2,1)} %constant.4.clone.even_hbm.refs_2_.refs_3_.even, bf16[2,2,256,256]{3,2,1,0:T(8,128)(2,1)} %constant.5.clone.odd_hbm.refs_3_.refs_4_.mixing), custom_call_target="tpu_custom_call" | custom-call | flops 1006632960 | bytes 4784132 | tf_op jit(solution)/shard_map/pallas_call | solution.py:299
  4.8 6.3 %all-to-all-start = ((f32[16,200,128]{2,1,0:T(8,128)}), f32[16,200,128]{2,1,0:T(8,128)S(1)}, u32[]{:S(2)}, u32[]{:S(2)}) async-start(f32[16,200,128]{2,1,0:T(8,128)} %shard_map.64), calls=%async_computation | async-start | bytes 3276800 | tf_op jit(solution)/shard_map/all_to_all | solution.py:365
  11.1 0.0 copy-start
  11.2 0.0 copy-start.1
  11.2 3.2 %shard_map.67 = f32[16,64,128]{2,1,0:T(8,128)} custom-call(s32[1]{0:T(128)S(6)} %copy.9.count_ref, f32[2,256,1024]{2,1,0:T(8,128)} %bitcast.9, bf16[2,2,256,256]{3,2,1,0:T(8,128)(2,1)} %constant.4.clone.even_hbm.refs_2_.refs_3_.even, bf16[2,2,256,256]{3,2,1,0:T(8,128)(2,1)} %constant.5.clone.odd_hbm.refs_3_.refs_4_.mixing), custom_call_target="tpu_custom_call" | custom-call | flops 201326592 | bytes 3670020 | tf_op jit(solution)/shard_map/pallas_call | solution.py:299
  14.4 20.1 %all-to-all-done = f32[16,200,128]{2,1,0:T(8,128)S(1)} async-done(((f32[16,200,128]{2,1,0:T(8,128)}), f32[16,200,128]{2,1,0:T(8,128)S(1)}, u32[]{:S(2)}, u32[]{:S(2)}) %all-to-all-start) | async-done | bytes 1638432 | tf_op jit(solution)/shard_map/all_to_all | solution.py:365
  34.5 4.0 %all-to-all-start.1 = ((f32[16,64,128]{2,1,0:T(8,128)}), f32[16,64,128]{2,1,0:T(8,128)S(1)}, u32[]{:S(2)}, u32[]{:S(2)}) async-start(f32[16,64,128]{2,1,0:T(8,128)} %shard_map.67), calls=%async_computation.1 | async-start | bytes 1048576 | tf_op jit(solution)/shard_map/all_to_all | solution.py:365
  38.5 2.0 %shard_map.65.refs_1_.turns = f32[3,2,4,48,256]{4,3,2,1,0:T(8,128)} custom-call(), custom_call_target="tpu_custom_call" | custom-call | flops 7864320 | bytes 1179648 | tf_op jit(solution)/shard_map/pallas_call | solution.py:299
  40.4 0.0 copy-done
  40.5 0.0 copy-done.1
  40.5 3.3 %shard_map.66 = (f32[4,4,2,48,256]{4,3,2,1,0:T(8,128)}, f32[2,48,1024]{2,1,0:T(8,128)}, s32[4]{0:T(128)S(4)}) custom-call(f32[4,4,200,128]{3,2,1,0:T(8,128)S(1)} %bitcast.5, f32[3,2,4,48,256]{4,3,2,1,0:T(8,128)} %shard_map.65.refs_1_.turns, bf16[2,2,256,256]{3,2,1,0:T(8,128)(2,1)S(1)} %copy-done, bf16[2,2,256,256]{3,2,1,0:T(8,128)(2,1)S(1)} %copy-done.1), custom_call_target="tpu_custom_call" | custom-call | flops 905969664 | bytes 5832720 | tf_op jit(solution)/shard_map/pallas_call | solution.py:299
  43.8 0.0 copy-start.2
  43.8 4.7 %collective-permute-start.1 = (f32[2,48,1024]{2,1,0:T(8,128)}, f32[2,48,1024]{2,1,0:T(8,128)S(1)}, u32[]{:S(2)}, u32[]{:S(2)}) collective-permute-start(f32[2,48,1024]{2,1,0:T(8,128)} %get-tuple-element.14), channel_id=1, source_target_pairs={{0,16},{1,17},{2,18},{3,19},{4,20},{5,21},{6,22},{7,23},{8,24},{9,... | collective-permute-start | bytes 1179656 | tf_op jit(solution)/shard_map/ppermute | solution.py:380
  48.4 1.1 shard_map.68.refs_2_.turns
  49.5 0.0 all-to-all-done.1
  49.5 1.7 %shard_map.69 = (f32[4,4,2,16,256]{4,3,2,1,0:T(8,128)}, f32[2,16,1024]{2,1,0:T(8,128)S(1)}) custom-call(s32[4]{0:T(128)S(4)} %get-tuple-element.10.refs_0_.count_ref, f32[4,4,64,128]{3,2,1,0:T(8,128)S(1)} %bitcast.6, f32[3,2,4,16,256]{4,3,2,1,0:T(8,128)} %shard_map.68.refs_2_.turns, bf16[2,2,256,256]{3,2,1,0:T(8,128)(2,1)S(1)} %copy-done, ...), custom_call_target="tpu_custom_call" | custom-call | flops 301989888 | bytes 2621456 | tf_op jit(solution)/shard_map/pallas_call | solution.py:299
  51.3 4.0 %collective-permute-start = (f32[2,16,1024]{2,1,0:T(8,128)S(1)}, f32[2,16,1024]{2,1,0:T(8,128)S(1)}, u32[]{:S(2)}, u32[]{:S(2)}) collective-permute-start(f32[2,16,1024]{2,1,0:T(8,128)S(1)} %get-tuple-element.12), channel_id=1, source_target_pairs={{0,16},{1,17},{2,18},{3,19},{4,20},{5,21},{6,22},{7,23},{8,24},{9,... | collective-permute-start | bytes 393224 | tf_op jit(solution)/shard_map/ppermute | solution.py:380
  55.2 3.0 %collective-permute-done.1.carry = f32[2,48,1024]{2,1,0:T(8,128)S(1)} collective-permute-done((f32[2,48,1024]{2,1,0:T(8,128)}, f32[2,48,1024]{2,1,0:T(8,128)S(1)}, u32[]{:S(2)}, u32[]{:S(2)}) %collective-permute-start.1) | collective-permute-done | bytes 393248 | tf_op jit(solution)/shard_map/ppermute | solution.py:380
  58.2 0.0 copy-done.2
  58.2 0.0 copy-start.4
  58.3 1.4 %copy-done.4 = f32[4,4,2,48,256]{4,3,2,1,0:T(8,128)S(1)} copy-done((f32[4,4,2,48,256]{4,3,2,1,0:T(8,128)S(1)}, f32[4,4,2,48,256]{4,3,2,1,0:T(8,128)}, u32[]{:S(2)}) %copy-start.4) | copy-done | bytes 1572888
  59.7 0.0 copy-start.3
  59.7 0.0 copy-start.5
  59.7 2.3 %shard_map.70.refs_0_ = f32[4,4,2,64,256]{4,3,2,1,0:T(8,128)} custom-call(s32[4]{0:T(128)S(4)} %get-tuple-element.10.refs_0_.count_ref, f32[4,4,2,48,256]{4,3,2,1,0:T(8,128)S(1)} %copy-done.4, f32[2,48,1024]{2,1,0:T(8,128)S(1)} %collective-permute-done.1.carry, f32[3,2,4,48,256]{4,3,2,1,0:T(8,128)S(1)} %copy-done.2, bf16[2,2,256,256]{3,2,1,0:T(8,128)(2,1)S(1)} %copy-done, ...), custom_call_target="tpu_custom_call" | custom-call | flops 905969664 | bytes 6291472 | tf_op jit(solution)/shard_map/pallas_call | solution.py:299
  62.0 0.0 collective-permute-done.carry
  62.0 0.0 copy-done.3
  62.0 0.0 copy-done.5
  62.0 1.3 %shard_map.71 = f32[4,4,2,64,256]{4,3,2,1,0:T(8,128)} custom-call(s32[4]{0:T(128)S(4)} %get-tuple-element.10.refs_0_.count_ref, f32[4,4,2,16,256]{4,3,2,1,0:T(8,128)S(1)} %copy-done.5, f32[2,16,1024]{2,1,0:T(8,128)S(1)} %collective-permute-done.carry, f32[3,2,4,16,256]{4,3,2,1,0:T(8,128)S(1)} %copy-done.3, ...), custom_call_target="tpu_custom_call", output_to_operand_aliasing={{}: (6, {})} | custom-call | flops 301989888 | bytes 6291472 | tf_op jit(solution)/shard_map/pallas_call | solution.py:299
  63.3 42.9 %all_to_all.15.r_ref = f32[16,2,64,256]{3,2,1,0:T(8,128)S(1)} all-to-all(f32[16,2,64,256]{3,2,1,0:T(8,128)} %bitcast.7), channel_id=1, replica_groups=mesh['block'=2,'point'=4,'space'=4] {'point','space'}, dimensions={0} | all-to-all | bytes 4194304 | tf_op jit(solution)/shard_map/all_to_all | solution.py:419
  106.2 2.3 %shard_map.72 = f32[2,256,1024]{2,1,0:T(8,128)} custom-call(f32[16,2,64,256]{3,2,1,0:T(8,128)S(1)} %all_to_all.15.r_ref, bf16[2,2,256,256]{3,2,1,0:T(8,128)(2,1)S(1)} %copy-done, bf16[2,2,256,256]{3,2,1,0:T(8,128)(2,1)S(1)} %copy-done.1), custom_call_target="tpu_custom_call" | custom-call | flops 1207959552 | bytes 5242880 | tf_op jit(solution)/shard_map/pallas_call | solution.py:299
Async XLA Ops:
  4.8 29.7 %all-to-all-start = ((f32[16,200,128]{2,1,0:T(8,128)}), f32[16,200,128]{2,1,0:T(8,128)S(1)}, u32[]{:S(2)}, u32[]{:S(2)}) async-start(f32[16,200,128]{2,1,0:T(8,128)} %shard_map.64), calls=%async_computation | async-start | bytes 3276800 | tf_op jit(solution)/shard_map/all_to_all | solution.py:365
  11.1 29.3 %copy-start = (bf16[2,2,256,256]{3,2,1,0:T(8,128)(2,1)S(1)}, bf16[2,2,256,256]{3,2,1,0:T(8,128)(2,1)}, u32[]{:S(2)}) copy-start(bf16[2,2,256,256]{3,2,1,0:T(8,128)(2,1)} %constant.4.clone.even_hbm.refs_2_.refs_3_.even) | copy-start | bytes 1572868
  11.2 29.3 %copy-start.1 = (bf16[2,2,256,256]{3,2,1,0:T(8,128)(2,1)S(1)}, bf16[2,2,256,256]{3,2,1,0:T(8,128)(2,1)}, u32[]{:S(2)}) copy-start(bf16[2,2,256,256]{3,2,1,0:T(8,128)(2,1)} %constant.5.clone.odd_hbm.refs_3_.refs_4_.mixing) | copy-start | bytes 1572868
  34.5 15.0 %all-to-all-start.1 = ((f32[16,64,128]{2,1,0:T(8,128)}), f32[16,64,128]{2,1,0:T(8,128)S(1)}, u32[]{:S(2)}, u32[]{:S(2)}) async-start(f32[16,64,128]{2,1,0:T(8,128)} %shard_map.67), calls=%async_computation.1 | async-start | bytes 1048576 | tf_op jit(solution)/shard_map/all_to_all | solution.py:365
  43.8 14.5 %copy-start.2 = (f32[3,2,4,48,256]{4,3,2,1,0:T(8,128)S(1)}, f32[3,2,4,48,256]{4,3,2,1,0:T(8,128)}, u32[]{:S(2)}) copy-start(f32[3,2,4,48,256]{4,3,2,1,0:T(8,128)} %shard_map.65.refs_1_.turns) | copy-start | bytes 3538948
  43.8 14.5 %collective-permute-start.1 = (f32[2,48,1024]{2,1,0:T(8,128)}, f32[2,48,1024]{2,1,0:T(8,128)S(1)}, u32[]{:S(2)}, u32[]{:S(2)}) collective-permute-start(f32[2,48,1024]{2,1,0:T(8,128)} %get-tuple-element.14), channel_id=1, source_target_pairs={{0,16},{1,17},{2,18},{3,19},{4,20},{5,21},{6,22},{7,23},{8,24},{9,... | collective-permute-start | bytes 1179656 | tf_op jit(solution)/shard_map/ppermute | solution.py:380
  51.3 10.7 %collective-permute-start = (f32[2,16,1024]{2,1,0:T(8,128)S(1)}, f32[2,16,1024]{2,1,0:T(8,128)S(1)}, u32[]{:S(2)}, u32[]{:S(2)}) collective-permute-start(f32[2,16,1024]{2,1,0:T(8,128)S(1)} %get-tuple-element.12), channel_id=1, source_target_pairs={{0,16},{1,17},{2,18},{3,19},{4,20},{5,21},{6,22},{7,23},{8,24},{9,... | collective-permute-start | bytes 393224 | tf_op jit(solution)/shard_map/ppermute | solution.py:380
  58.2 1.4 %copy-start.4 = (f32[4,4,2,48,256]{4,3,2,1,0:T(8,128)S(1)}, f32[4,4,2,48,256]{4,3,2,1,0:T(8,128)}, u32[]{:S(2)}) copy-start(f32[4,4,2,48,256]{4,3,2,1,0:T(8,128)} %get-tuple-element.13.spectra) | copy-start | bytes 4718596
  59.7 2.3 %copy-start.3 = (f32[3,2,4,16,256]{4,3,2,1,0:T(8,128)S(1)}, f32[3,2,4,16,256]{4,3,2,1,0:T(8,128)}, u32[]{:S(2)}) copy-start(f32[3,2,4,16,256]{4,3,2,1,0:T(8,128)} %shard_map.68.refs_2_.turns) | copy-start | bytes 1179652
  59.7 2.3 %copy-start.5 = (f32[4,4,2,16,256]{4,3,2,1,0:T(8,128)S(1)}, f32[4,4,2,16,256]{4,3,2,1,0:T(8,128)}, u32[]{:S(2)}) copy-start(f32[4,4,2,16,256]{4,3,2,1,0:T(8,128)} %get-tuple-element.11.spectra) | copy-start | bytes 1572868

commit v6 on v3

--- a/solution.py
+++ b/solution.py
@@ -134,6 +134,8 @@
             start = part * tall + piece * rows
             wanted = result[:, piece * lanes : (piece + 1) * lanes]
             out[first : first + reach, start : start + rows] = wanted.reshape(reach, rows, lanes)
+        here = (pl.ds(first, reach), pl.ds(part * tall, height - tall if part else tall))
+        copy_out(stores, out.at[here], out_hbm.at[here], out_sems.at[2 * part + first // reach])
 
     for part in range(2):
         if part:
@@ -147,8 +149,6 @@
         else:
             for half, value in enumerate(fold(pieces)):
                 keep(part, half * bands // 2, product(table[half], halves(value), NT))
-        here = pl.ds(part * tall, height - tall if part else tall)
-        copy_out(stores, out.at[:, here], out_hbm.at[:, here], out_sems.at[part])
     wait_all(stores)
 
 
@@ -175,7 +175,7 @@
 def forward_x(odd, *refs):
     refs, (turns, highs, lows, spectra, turn_sem, out_sems) = refs[:-6], refs[-6:]
     if odd:
-        count_ref, r_ref, turns_hbm, even, mixing, spectra_hbm, last = refs
+        count_ref, r_ref, turns_hbm, even, mixing, spectra_hbm, last_hbm, last, last_sems = refs
     else:
         r_ref, turns_hbm, even, mixing, spectra_hbm, last, count_ref = refs
     points, spaces, _, lanes = r_ref.shape
@@ -230,6 +230,9 @@
         here = slice(q * quarter, (q + 1) * quarter)
         last[0, :, here] = first
         last[1, :, here] = second
+        if odd:
+            there = (slice(None), slice(None), pl.ds(q * quarter, quarter))
+            copy_out(stores, last.at[there], last_hbm.at[there], last_sems.at[q])
     wait_all(stores)
 
 
@@ -285,32 +288,23 @@
     quarter = even.shape[-1] // 2
     pieces = slab // math.gcd(slab, 128)
     step = slab // pieces
-    copies = copy_in([(even_hbm, even)], sems)
-
-    def place_out(index):
-        here = (index // pieces, pl.ds(pl.multiple_of(index % pieces * step, step), step))
-        return pltpu.make_async_copy(out.at[here], out_hbm.at[here], out_sems.at[index])
-
-    def work(index, _):
-        part = index // pieces
-        here = pl.ds(pl.multiple_of(index % pieces * step, step), step)
-        first = halves(r_ref[:half, part, :, here].reshape(half * rows, step))
-        second = halves(r_ref[half:, part, :, here].reshape(half * rows, step))
-
-        @pl.when(index == 0)
-        def _():
-            wait_all(copies)
-
-        for q, result in enumerate(mix(first, second, table, TN)):
-            base = even[part, here, q * quarter : (q + 1) * quarter]
-            out[part, here, q * quarter : (q + 1) * quarter] = base + result
-            out[part, here, (q + 2) * quarter : (q + 3) * quarter] = base - result
-        place_out(index).start()
-        return 0
-
-    lax.fori_loop(0, 2 * pieces, work, 0)
-    for index in range(2 * pieces):
-        place_out(index).wait()
+    spots = [(part, pl.ds(piece * step, step)) for part in range(2) for piece in range(pieces)]
+    copies = copy_in([(even_hbm.at[spot], even.at[spot]) for spot in spots], sems)
+    stores = []
+    for part in range(2):
+        for piece in range(pieces):
+            here = slice(piece * step, (piece + 1) * step)
+            first = halves(r_ref[:half, part, :, here].reshape(half * rows, step))
+            second = halves(r_ref[half:, part, :, here].reshape(half * rows, step))
+            results = mix(first, second, table, TN)
+            copies[part * pieces + piece].wait()
+            for q, result in enumerate(results):
+                base = even[part, here, q * quarter : (q + 1) * quarter]
+                out[part, here, q * quarter : (q + 1) * quarter] = base + result
+                out[part, here, (q + 2) * quarter : (q + 3) * quarter] = base - result
+            there = pl.ds(piece * step, step)
+            copy_out(stores, out.at[part, there], out_hbm.at[part, there], out_sems.at[part * pieces + piece])
+    wait_all(stores)
 
 
 def call(kernel, operands, outs, flops, spaces, out_spaces, scratch=(), limit=20, aliases=None):
@@ -367,7 +361,7 @@
                     vmem((bands, heights[odd], lanes), f32),
                     vmem(table.shape, bf16),
                     sems((3,)),
-                    sems((2,)),
+                    sems((4,)),
                 ],
             )
         )
@@ -395,8 +389,9 @@
             [spectra_shape, (2, rows, length_x)] + ([] if odd else [(points,)]),
             flops_x,
             [smem] * odd + [vmem, hbm, vmem, vmem],
-            [hbm, vmem] + ([] if odd else [smem]),
-            scratch=[vmem(turns_shape, f32), *folded, vmem(spectra_shape, f32), sems((1,)), sems((4,))],
+            [hbm, hbm] if odd else [hbm, vmem, smem],
+            scratch=[vmem((2, rows, length_x), f32), sems((4,))] * odd
+            + [vmem(turns_shape, f32), *folded, vmem(spectra_shape, f32), sems((1,)), sems((4,))],
         )
         spectra[odd], last = results[:2]
         if not odd:
@@ -456,7 +451,7 @@
         flops_y[1],
         [vmem, hbm, vmem],
         [hbm],
-        scratch=[vmem(half, f32), vmem((2, slab, length_y), f32), sems((1,)), sems((2 * slab // lanes,))],
+        scratch=[vmem(half, f32), vmem((2, slab, length_y), f32), sems((2 * slab // lanes,)), sems((2 * slab // lanes,))],
     )
     return fields[None]
 

time: 105 us -> 102 us (0.971)
  Pallas kernels: 25.6 us -> 24.5 us
    pallas_call x10, Pallas kernels: 25.6 us -> 24.5 us  [call(): pl.pallas_call(kernel, in_specs=[pl.BlockSpec(memory_space=space) for spa...]
    all_to_all x2, starting transfers between devices: 11.4 us -> 10.3 us  [on_device(): lax.all_to_all(back, group, split_axis=0, concat_axis=0, tiled=True)]
where the time goes in v6:
time: 102 us
  waiting for transfers between devices  46 us (45%)
  starting transfers between devices  30.3 us (30%)
  Pallas kernels  24.5 us (24%)
    pallas_call x10, Pallas kernels, call(): pl.pallas_call(kernel, in_specs=[pl.BlockSpec(memory_space=space) for spa...  24.5 us
    all_to_all x2, waiting for transfers between devices, on_device(): lax.all_to_all(sent[odd], group, split_axis=0, concat_axis=0, tiled=True)  19.8 us
    all_to_all x2, waiting for transfers between devices, on_device(): lax.all_to_all(back, group, split_axis=0, concat_axis=0, tiled=True)  13.4 us
    ppermute x2, waiting for transfers between devices, on_device(): lax.ppermute(last, 'block', [(b, b + 1) for b in range(blocks - 1)])  12.8 us
    all_to_all x2, starting transfers between devices, on_device(): lax.all_to_all(back, group, split_axis=0, concat_axis=0, tiled=True)  10.3 us
    all_to_all x2, starting transfers between devices, on_device(): lax.all_to_all(sent[odd], group, split_axis=0, concat_axis=0, tiled=True)  9.98 us
    ppermute x2, starting transfers between devices, on_device(): lax.ppermute(last, 'block', [(b, b + 1) for b in range(blocks - 1)])  9.94 us
  transfers between devices with their start and end apart: 6, of which 4 were waited for; matrix products, arithmetic and copies ran while one was open for 0% of the time, Pallas kernels for 16%

profile of v6, /device:TPU:0, one launch (start us, length us, event | category | flops | bytes accessed | tf_op | source)
XLA Modules:
  0.0 101.6 jit_solution(9251624795835361913)
XLA Ops:
  0.7 3.1 %shard_map.64 = f32[16,136,128]{2,1,0:T(8,128)} custom-call(s32[1]{0:T(128)S(6)} %copy.9.count_ref, f32[2,256,1024]{2,1,0:T(8,128)} %bitcast.8, bf16[2,2,256,256]{3,2,1,0:T(8,128)(2,1)} %constant.4.clone.table_hbm.refs_2_.refs_3_.even.table), custom_call_target="tpu_custom_call" | custom-call | flops 402653184 | bytes 3735556 | tf_op jit(solution)/shard_map/pallas_call | solution.py:317
  3.8 6.3 %all-to-all-start = ((f32[16,136,128]{2,1,0:T(8,128)}), f32[16,136,128]{2,1,0:T(8,128)S(1)}, u32[]{:S(2)}, u32[]{:S(2)}) async-start(f32[16,136,128]{2,1,0:T(8,128)} %shard_map.64), calls=%async_computation | async-start | bytes 2228224 | tf_op jit(solution)/shard_map/all_to_all | solution.py:381
  10.1 3.5 %shard_map.67 = f32[16,128,128]{2,1,0:T(8,128)} custom-call(s32[1]{0:T(128)S(6)} %copy.9.count_ref, f32[2,256,1024]{2,1,0:T(8,128)} %bitcast.9, bf16[2,2,256,256]{3,2,1,0:T(8,128)(2,1)} %constant.5.clone.refs_3_.table_hbm.refs_4_.mixing.table), custom_call_target="tpu_custom_call" | custom-call | flops 805306368 | bytes 3670020 | tf_op jit(solution)/shard_map/pallas_call | solution.py:317
  13.6 0.0 copy-start
  13.6 0.0 copy-start.1
  13.6 13.3 %all-to-all-done = f32[16,136,128]{2,1,0:T(8,128)S(1)} async-done(((f32[16,136,128]{2,1,0:T(8,128)}), f32[16,136,128]{2,1,0:T(8,128)S(1)}, u32[]{:S(2)}, u32[]{:S(2)}) %all-to-all-start) | async-done | bytes 1114144 | tf_op jit(solution)/shard_map/all_to_all | solution.py:381
  26.9 3.7 %all-to-all-start.1 = ((f32[16,128,128]{2,1,0:T(8,128)}), f32[16,128,128]{2,1,0:T(8,128)S(1)}, u32[]{:S(2)}, u32[]{:S(2)}) async-start(f32[16,128,128]{2,1,0:T(8,128)} %shard_map.67), calls=%async_computation.1 | async-start | bytes 2097152 | tf_op jit(solution)/shard_map/all_to_all | solution.py:381
  30.6 1.4 %shard_map.65.refs_1_.turns = f32[3,2,4,32,256]{4,3,2,1,0:T(8,128)} custom-call(), custom_call_target="tpu_custom_call" | custom-call | flops 5242880 | bytes 786432 | tf_op jit(solution)/shard_map/pallas_call | solution.py:317
  32.0 0.0 copy-done
  32.1 0.0 copy-done.1
  32.1 2.0 %shard_map.66 = (f32[4,4,2,32,256]{4,3,2,1,0:T(8,128)}, f32[2,32,1024]{2,1,0:T(8,128)S(1)}, s32[4]{0:T(128)S(4)}) custom-call(f32[4,4,136,128]{3,2,1,0:T(8,128)S(1)} %bitcast.6, f32[3,2,4,32,256]{4,3,2,1,0:T(8,128)} %shard_map.65.refs_1_.turns, bf16[2,2,256,256]{3,2,1,0:T(8,128)(2,1)S(1)} %copy-done.1, bf16[2,2,256,256]{3,2,1,0:T(8,128)(2,1)S(1)} %copy-done), custom_call_target="tpu_custom_call" | custom-call | flops 603979776 | bytes 4259856 | tf_op jit(solution)/shard_map/pallas_call | solution.py:317
  34.1 0.0 copy-start.2
  34.1 4.6 %collective-permute-start = (f32[2,32,1024]{2,1,0:T(8,128)S(1)}, f32[2,32,1024]{2,1,0:T(8,128)S(1)}, u32[]{:S(2)}, u32[]{:S(2)}) collective-permute-start(f32[2,32,1024]{2,1,0:T(8,128)S(1)} %get-tuple-element.17), channel_id=1, source_target_pairs={{0,16},{1,17},{2,18},{3,19},{4,20},{5,21},{6,22},{7,23},{8,24},{9,... | collective-permute-start | bytes 786440 | tf_op jit(solution)/shard_map/ppermute | solution.py:399
  38.7 1.5 %shard_map.68.refs_2_.turns = f32[3,2,4,32,256]{4,3,2,1,0:T(8,128)} custom-call(), custom_call_target="tpu_custom_call" | custom-call | flops 5242880 | bytes 786432 | tf_op jit(solution)/shard_map/pallas_call | solution.py:317
  40.2 6.5 %all-to-all-done.1 = f32[16,128,128]{2,1,0:T(8,128)S(1)} async-done(((f32[16,128,128]{2,1,0:T(8,128)}), f32[16,128,128]{2,1,0:T(8,128)S(1)}, u32[]{:S(2)}, u32[]{:S(2)}) %all-to-all-start.1) | async-done | bytes 1048608 | tf_op jit(solution)/shard_map/all_to_all | solution.py:381
  46.7 0.0 copy-start.3
  46.7 2.0 %shard_map.69 = (f32[4,4,2,32,256]{4,3,2,1,0:T(8,128)}, f32[2,32,1024]{2,1,0:T(8,128)}) custom-call(s32[4]{0:T(128)S(4)} %get-tuple-element.16.refs_0_.count_ref, f32[4,4,128,128]{3,2,1,0:T(8,128)S(1)} %bitcast.7, f32[3,2,4,32,256]{4,3,2,1,0:T(8,128)} %shard_map.68.refs_2_.turns, bf16[2,2,256,256]{3,2,1,0:T(8,128)(2,1)S(1)} %copy-done.1, ...), custom_call_target="tpu_custom_call" | custom-call | flops 603979776 | bytes 4194320 | tf_op jit(solution)/shard_map/pallas_call | solution.py:317
  48.8 0.0 collective-permute-done.carry
  48.8 0.0 copy-done.2
  48.8 0.0 copy-done.3
  48.8 1.8 %shard_map.71 = f32[4,4,2,32,256]{4,3,2,1,0:T(8,128)} custom-call(s32[4]{0:T(128)S(4)} %get-tuple-element.16.refs_0_.count_ref, f32[4,4,2,32,256]{4,3,2,1,0:T(8,128)S(1)} %copy-done.3, f32[2,32,1024]{2,1,0:T(8,128)S(1)} %collective-permute-done.carry, f32[3,2,4,32,256]{4,3,2,1,0:T(8,128)S(1)} %copy-done.2, bf16[2,2,256,256]{3,2,1,0:T(8,128)(2,1)S(1)} %copy-done.1, ...), custom_call_target="tpu_custom_call" | custom-call | flops 603979776 | bytes 4194320 | tf_op jit(solution)/shard_map/pallas_call | solution.py:317
  50.6 0.0 copy-start.5
  50.6 6.6 %all-to-all-start.3 = ((f32[16,2,32,256]{3,2,1,0:T(8,128)}), f32[16,2,32,256]{3,2,1,0:T(8,128)S(1)}, u32[]{:S(2)}, u32[]{:S(2)}) async-start(f32[16,2,32,256]{3,2,1,0:T(8,128)} %bitcast.10), calls=%async_computation.3 | async-start | bytes 2097152 | tf_op jit(solution)/shard_map/all_to_all | solution.py:435
  57.3 0.0 copy-done.5
  57.3 5.3 %collective-permute-start.1 = (f32[2,32,1024]{2,1,0:T(8,128)S(1)}, f32[2,32,1024]{2,1,0:T(8,128)S(1)}, u32[]{:S(2)}, u32[]{:S(2)}) collective-permute-start(f32[2,32,1024]{2,1,0:T(8,128)S(1)} %copy-done.5), channel_id=1, source_target_pairs={{0,16},{1,17},{2,18},{3,19},{4,20},{5,21},{6,22},{7,23},{8,24},{9,... | collective-permute-start | bytes 786440 | tf_op jit(solution)/shard_map/ppermute | solution.py:399
  62.6 12.8 %collective-permute-done.1.carry = f32[2,32,1024]{2,1,0:T(8,128)S(1)} collective-permute-done((f32[2,32,1024]{2,1,0:T(8,128)S(1)}, f32[2,32,1024]{2,1,0:T(8,128)S(1)}, u32[]{:S(2)}, u32[]{:S(2)}) %collective-permute-start.1) | collective-permute-done | bytes 262176 | tf_op jit(solution)/shard_map/ppermute | solution.py:399
  75.4 3.3 %shard_map.70 = f32[4,4,2,32,256]{4,3,2,1,0:T(8,128)} custom-call(s32[4]{0:T(128)S(4)} %get-tuple-element.16.refs_0_.count_ref, f32[4,4,2,32,256]{4,3,2,1,0:T(8,128)} %get-tuple-element.21.spectra, f32[2,32,1024]{2,1,0:T(8,128)S(1)} %collective-permute-done.1.carry, f32[3,2,4,32,256]{4,3,2,1,0:T(8,128)} %shard_map.68.refs_2_.turns, ...), custom_call_target="tpu_custom_call" | custom-call | flops 603979776 | bytes 4194320 | tf_op jit(solution)/shard_map/pallas_call | solution.py:317
  78.7 0.0 all-to-all-done.3.r_hbm
  78.7 0.0 copy-start.4
  78.7 3.7 %all-to-all-start.2 = ((f32[16,2,32,256]{3,2,1,0:T(8,128)}), f32[16,2,32,256]{3,2,1,0:T(8,128)S(1)}, u32[]{:S(2)}, u32[]{:S(2)}) async-start(f32[16,2,32,256]{3,2,1,0:T(8,128)} %bitcast.11), calls=%async_computation.2 | async-start | bytes 2097152 | tf_op jit(solution)/shard_map/all_to_all | solution.py:435
  82.4 0.0 copy-done.4
  82.4 2.7 %shard_map.72 = (f32[2,256,512]{2,1,0:T(8,128)}, f32[16,2,32,256]{3,2,1,0:T(8,128)}) custom-call(f32[16,2,32,256]{3,2,1,0:T(8,128)} %copy-done.4, bf16[2,2,256,256]{3,2,1,0:T(8,128)(2,1)S(1)} %copy-done.1), custom_call_target="tpu_custom_call", output_to_operand_aliasing={{1}: (0, {})} | custom-call | flops 402653184 | bytes 3670016 | tf_op jit(solution)/shard_map/pallas_call | solution.py:317
  85.1 13.4 %all-to-all-done.2.r_ref = f32[16,2,32,256]{3,2,1,0:T(8,128)S(1)} async-done(((f32[16,2,32,256]{3,2,1,0:T(8,128)}), f32[16,2,32,256]{3,2,1,0:T(8,128)S(1)}, u32[]{:S(2)}, u32[]{:S(2)}) %all-to-all-start.2) | async-done | bytes 1048608 | tf_op jit(solution)/shard_map/all_to_all | solution.py:435
  98.5 3.1 %shard_map.73 = f32[2,256,1024]{2,1,0:T(8,128)} custom-call(f32[16,2,32,256]{3,2,1,0:T(8,128)S(1)} %all-to-all-done.2.r_ref, f32[2,256,512]{2,1,0:T(8,128)} %get-tuple-element.26.even_hbm, bf16[2,2,256,256]{3,2,1,0:T(8,128)(2,1)S(1)} %copy-done), custom_call_target="tpu_custom_call" | custom-call | flops 805306368 | bytes 4718592 | tf_op jit(solution)/shard_map/pallas_call | solution.py:317
Async XLA Ops:
  3.8 23.2 %all-to-all-start = ((f32[16,136,128]{2,1,0:T(8,128)}), f32[16,136,128]{2,1,0:T(8,128)S(1)}, u32[]{:S(2)}, u32[]{:S(2)}) async-start(f32[16,136,128]{2,1,0:T(8,128)} %shard_map.64), calls=%async_computation | async-start | bytes 2228224 | tf_op jit(solution)/shard_map/all_to_all | solution.py:381
  13.6 18.5 %copy-start = (bf16[2,2,256,256]{3,2,1,0:T(8,128)(2,1)S(1)}, bf16[2,2,256,256]{3,2,1,0:T(8,128)(2,1)}, u32[]{:S(2)}) copy-start(bf16[2,2,256,256]{3,2,1,0:T(8,128)(2,1)} %constant.5.clone.refs_3_.table_hbm.refs_4_.mixing.table) | copy-start | bytes 1572868
  13.6 18.5 %copy-start.1 = (bf16[2,2,256,256]{3,2,1,0:T(8,128)(2,1)S(1)}, bf16[2,2,256,256]{3,2,1,0:T(8,128)(2,1)}, u32[]{:S(2)}) copy-start(bf16[2,2,256,256]{3,2,1,0:T(8,128)(2,1)} %constant.4.clone.table_hbm.refs_2_.refs_3_.even.table) | copy-start | bytes 1572868
  26.9 19.8 %all-to-all-start.1 = ((f32[16,128,128]{2,1,0:T(8,128)}), f32[16,128,128]{2,1,0:T(8,128)S(1)}, u32[]{:S(2)}, u32[]{:S(2)}) async-start(f32[16,128,128]{2,1,0:T(8,128)} %shard_map.67), calls=%async_computation.1 | async-start | bytes 2097152 | tf_op jit(solution)/shard_map/all_to_all | solution.py:381
  34.1 14.7 %copy-start.2 = (f32[3,2,4,32,256]{4,3,2,1,0:T(8,128)S(1)}, f32[3,2,4,32,256]{4,3,2,1,0:T(8,128)}, u32[]{:S(2)}) copy-start(f32[3,2,4,32,256]{4,3,2,1,0:T(8,128)} %shard_map.65.refs_1_.turns) | copy-start | bytes 2359300
  34.1 14.7 %collective-permute-start = (f32[2,32,1024]{2,1,0:T(8,128)S(1)}, f32[2,32,1024]{2,1,0:T(8,128)S(1)}, u32[]{:S(2)}, u32[]{:S(2)}) collective-permute-start(f32[2,32,1024]{2,1,0:T(8,128)S(1)} %get-tuple-element.17), channel_id=1, source_target_pairs={{0,16},{1,17},{2,18},{3,19},{4,20},{5,21},{6,22},{7,23},{8,24},{9,... | collective-permute-start | bytes 786440 | tf_op jit(solution)/shard_map/ppermute | solution.py:399
  46.7 2.1 %copy-start.3 = (f32[4,4,2,32,256]{4,3,2,1,0:T(8,128)S(1)}, f32[4,4,2,32,256]{4,3,2,1,0:T(8,128)}, u32[]{:S(2)}) copy-start(f32[4,4,2,32,256]{4,3,2,1,0:T(8,128)} %get-tuple-element.23.spectra) | copy-start | bytes 3145732
  50.6 6.7 %copy-start.5 = (f32[2,32,1024]{2,1,0:T(8,128)S(1)}, f32[2,32,1024]{2,1,0:T(8,128)}, u32[]{:S(2)}) copy-start(f32[2,32,1024]{2,1,0:T(8,128)} %get-tuple-element.22) | copy-start | bytes 786436
  50.6 28.0 %all-to-all-start.3 = ((f32[16,2,32,256]{3,2,1,0:T(8,128)}), f32[16,2,32,256]{3,2,1,0:T(8,128)S(1)}, u32[]{:S(2)}, u32[]{:S(2)}) async-start(f32[16,2,32,256]{3,2,1,0:T(8,128)} %bitcast.10), calls=%async_computation.3 | async-start | bytes 2097152 | tf_op jit(solution)/shard_map/all_to_all | solution.py:435
  57.3 18.1 %collective-permute-start.1 = (f32[2,32,1024]{2,1,0:T(8,128)S(1)}, f32[2,32,1024]{2,1,0:T(8,128)S(1)}, u32[]{:S(2)}, u32[]{:S(2)}) collective-permute-start(f32[2,32,1024]{2,1,0:T(8,128)S(1)} %copy-done.5), channel_id=1, source_target_pairs={{0,16},{1,17},{2,18},{3,19},{4,20},{5,21},{6,22},{7,23},{8,24},{9,... | collective-permute-start | bytes 786440 | tf_op jit(solution)/shard_map/ppermute | solution.py:399
  78.7 3.7 %copy-start.4 = (f32[16,2,32,256]{3,2,1,0:T(8,128)}, f32[16,2,32,256]{3,2,1,0:T(8,128)S(1)}, u32[]{:S(2)}) copy-start(f32[16,2,32,256]{3,2,1,0:T(8,128)S(1)} %all-to-all-done.3.r_hbm) | copy-start | bytes 3145732
  78.7 19.8 %all-to-all-start.2 = ((f32[16,2,32,256]{3,2,1,0:T(8,128)}), f32[16,2,32,256]{3,2,1,0:T(8,128)S(1)}, u32[]{:S(2)}, u32[]{:S(2)}) async-start(f32[16,2,32,256]{3,2,1,0:T(8,128)} %bitcast.11), calls=%async_computation.2 | async-start | bytes 2097152 | tf_op jit(solution)/shard_map/all_to_all | solution.py:435

commit v7 on v6

--- a/solution.py
+++ b/solution.py
@@ -134,8 +134,6 @@
             start = part * tall + piece * rows
             wanted = result[:, piece * lanes : (piece + 1) * lanes]
             out[first : first + reach, start : start + rows] = wanted.reshape(reach, rows, lanes)
-        here = (pl.ds(first, reach), pl.ds(part * tall, height - tall if part else tall))
-        copy_out(stores, out.at[here], out_hbm.at[here], out_sems.at[2 * part + first // reach])
 
     for part in range(2):
         if part:
@@ -149,6 +147,8 @@
         else:
             for half, value in enumerate(fold(pieces)):
                 keep(part, half * bands // 2, product(table[half], halves(value), NT))
+        here = pl.ds(part * tall, height - tall if part else tall)
+        copy_out(stores, out.at[:, here], out_hbm.at[:, here], out_sems.at[part])
     wait_all(stores)
 
 
@@ -288,8 +288,7 @@
     quarter = even.shape[-1] // 2
     pieces = slab // math.gcd(slab, 128)
     step = slab // pieces
-    spots = [(part, pl.ds(piece * step, step)) for part in range(2) for piece in range(pieces)]
-    copies = copy_in([(even_hbm.at[spot], even.at[spot]) for spot in spots], sems)
+    copies = copy_in([(even_hbm, even)], sems)
     stores = []
     for part in range(2):
         for piece in range(pieces):
@@ -297,7 +296,8 @@
             first = halves(r_ref[:half, part, :, here].reshape(half * rows, step))
             second = halves(r_ref[half:, part, :, here].reshape(half * rows, step))
             results = mix(first, second, table, TN)
-            copies[part * pieces + piece].wait()
+            if not stores:
+                wait_all(copies)
             for q, result in enumerate(results):
                 base = even[part, here, q * quarter : (q + 1) * quarter]
                 out[part, here, q * quarter : (q + 1) * quarter] = base + result
@@ -361,7 +361,7 @@
                     vmem((bands, heights[odd], lanes), f32),
                     vmem(table.shape, bf16),
                     sems((3,)),
-                    sems((4,)),
+                    sems((2,)),
                 ],
             )
         )
@@ -414,7 +414,6 @@
                 )
                 span = span + lax.ppermute(span, "block", steps)
                 reach *= 2
-    carry[0], spectra[1] = lax.optimization_barrier((carry[0], spectra[1]))
     solved = []
     for odd in range(2):
         back = call(
@@ -451,7 +450,7 @@
         flops_y[1],
         [vmem, hbm, vmem],
         [hbm],
-        scratch=[vmem(half, f32), vmem((2, slab, length_y), f32), sems((2 * slab // lanes,)), sems((2 * slab // lanes,))],
+        scratch=[vmem(half, f32), vmem((2, slab, length_y), f32), sems((1,)), sems((2 * slab // lanes,))],
     )
     return fields[None]
 

time: 102 us -> 109 us (1.069)
  starting transfers between devices: 30.3 us -> 35.9 us
  waiting for transfers between devices: 46 us -> 44.7 us
  local copies, waits for them, and re-layouts: 0.03 us -> 1.25 us
    all_to_all x2, starting transfers between devices: 10.3 us -> 15.4 us  [on_device(): lax.all_to_all(back, group, split_axis=0, concat_axis=0, tiled=True)]
    ppermute x2, waiting for transfers between devices: 12.8 us -> 9.82 us  [on_device(): lax.ppermute(last, 'block', [(b, b + 1) for b in range(blocks - 1)])]
    all_to_all x2, waiting for transfers between devices: 19.8 us -> 21.5 us  [on_device(): lax.all_to_all(sent[odd], group, split_axis=0, concat_axis=0, tiled=True)]
    unnamed x12 -> x10, local copies, waits for them, and re-layouts: 0.03 us -> 1.25 us
  transfers between devices with their start and end apart: 6 -> 6, of which waited for: 4 -> 5; matrix products, arithmetic and copies ran while one was open for 0% -> 0% of each run, Pallas kernels for 16% -> 16%
where the time goes in v7:
time: 109 us; the launch traced here: 108 us
  waiting for transfers between devices  44.7 us (41%)
  starting transfers between devices  35.9 us (33%)
  Pallas kernels  25.4 us (23%)
  local copies, waits for them, and re-layouts  1.25 us (1%)
    pallas_call x10, Pallas kernels, call(): pl.pallas_call(kernel, in_specs=[pl.BlockSpec(memory_space=space) for spa...  25.4 us
    all_to_all x2, waiting for transfers between devices, on_device(): lax.all_to_all(sent[odd], group, split_axis=0, concat_axis=0, tiled=True)  21.5 us
    all_to_all x2, starting transfers between devices, on_device(): lax.all_to_all(back, group, split_axis=0, concat_axis=0, tiled=True)  15.4 us
    all_to_all x2, waiting for transfers between devices, on_device(): lax.all_to_all(back, group, split_axis=0, concat_axis=0, tiled=True)  13.4 us
    all_to_all x2, starting transfers between devices, on_device(): lax.all_to_all(sent[odd], group, split_axis=0, concat_axis=0, tiled=True)  10.7 us
    ppermute x2, waiting for transfers between devices, on_device(): lax.ppermute(last, 'block', [(b, b + 1) for b in range(blocks - 1)])  9.82 us
    ppermute x2, starting transfers between devices, on_device(): lax.ppermute(last, 'block', [(b, b + 1) for b in range(blocks - 1)])  9.81 us
  transfers between devices with their start and end apart: 6, of which 5 were waited for; matrix products, arithmetic and copies ran while one was open for 0% of the time, Pallas kernels for 16%

profile of v7, /device:TPU:0, one launch (start us, length us, event | category | flops | bytes accessed | tf_op | source)
XLA Modules:
  0.0 108.1 jit_solution(10794642982921083749)
XLA Ops:
  0.7 3.1 %shard_map.64 = f32[16,136,128]{2,1,0:T(8,128)} custom-call(s32[1]{0:T(128)S(6)} %copy.9.count_ref, f32[2,256,1024]{2,1,0:T(8,128)} %bitcast.7, bf16[2,2,256,256]{3,2,1,0:T(8,128)(2,1)} %constant.4.clone.table_hbm.refs_2_.refs_3_.even.table), custom_call_target="tpu_custom_call" | custom-call | flops 402653184 | bytes 3735556 | tf_op jit(solution)/shard_map/pallas_call | solution.py:317
  3.7 6.3 %all-to-all-start = ((f32[16,136,128]{2,1,0:T(8,128)}), f32[16,136,128]{2,1,0:T(8,128)S(1)}, u32[]{:S(2)}, u32[]{:S(2)}) async-start(f32[16,136,128]{2,1,0:T(8,128)} %shard_map.64), calls=%async_computation | async-start | bytes 2228224 | tf_op jit(solution)/shard_map/all_to_all | solution.py:381
  10.1 3.4 %shard_map.67 = f32[16,128,128]{2,1,0:T(8,128)} custom-call(s32[1]{0:T(128)S(6)} %copy.9.count_ref, f32[2,256,1024]{2,1,0:T(8,128)} %bitcast.8, bf16[2,2,256,256]{3,2,1,0:T(8,128)(2,1)} %constant.5.clone.refs_3_.table_hbm.refs_4_.mixing.table), custom_call_target="tpu_custom_call" | custom-call | flops 805306368 | bytes 3670020 | tf_op jit(solution)/shard_map/pallas_call | solution.py:317
  13.5 0.0 copy-start
  13.5 0.0 copy-start.1
  13.5 13.4 %all-to-all-done = f32[16,136,128]{2,1,0:T(8,128)S(1)} async-done(((f32[16,136,128]{2,1,0:T(8,128)}), f32[16,136,128]{2,1,0:T(8,128)S(1)}, u32[]{:S(2)}, u32[]{:S(2)}) %all-to-all-start) | async-done | bytes 1114144 | tf_op jit(solution)/shard_map/all_to_all | solution.py:381
  26.9 4.3 %all-to-all-start.1 = ((f32[16,128,128]{2,1,0:T(8,128)}), f32[16,128,128]{2,1,0:T(8,128)}, u32[]{:S(2)}, u32[]{:S(2)}) async-start(f32[16,128,128]{2,1,0:T(8,128)} %shard_map.67), calls=%async_computation.1 | async-start | bytes 2097152 | tf_op jit(solution)/shard_map/all_to_all | solution.py:381
  31.3 1.5 %shard_map.65.refs_1_.turns = f32[3,2,4,32,256]{4,3,2,1,0:T(8,128)} custom-call(), custom_call_target="tpu_custom_call" | custom-call | flops 5242880 | bytes 786432 | tf_op jit(solution)/shard_map/pallas_call | solution.py:317
  32.7 0.0 copy-start.2
  32.8 0.0 copy-done
  32.8 0.0 copy-done.1
  32.8 2.0 %shard_map.66 = (f32[4,4,2,32,256]{4,3,2,1,0:T(8,128)}, f32[2,32,1024]{2,1,0:T(8,128)S(1)}, s32[4]{0:T(128)S(4)}) custom-call(f32[4,4,136,128]{3,2,1,0:T(8,128)S(1)} %bitcast.6, f32[3,2,4,32,256]{4,3,2,1,0:T(8,128)} %shard_map.65.refs_1_.turns, bf16[2,2,256,256]{3,2,1,0:T(8,128)(2,1)S(1)} %copy-done.1, bf16[2,2,256,256]{3,2,1,0:T(8,128)(2,1)S(1)} %copy-done), custom_call_target="tpu_custom_call" | custom-call | flops 603979776 | bytes 4259856 | tf_op jit(solution)/shard_map/pallas_call | solution.py:317
  34.8 4.5 %collective-permute-start.1 = (f32[2,32,1024]{2,1,0:T(8,128)S(1)}, f32[2,32,1024]{2,1,0:T(8,128)S(1)}, u32[]{:S(2)}, u32[]{:S(2)}) collective-permute-start(f32[2,32,1024]{2,1,0:T(8,128)S(1)} %get-tuple-element.20), channel_id=1, source_target_pairs={{0,16},{1,17},{2,18},{3,19},{4,20},{5,21},{6,22},{7,23},{8,24},{9,... | collective-permute-start | bytes 786440 | tf_op jit(solution)/shard_map/ppermute | solution.py:399
  39.3 8.1 %all-to-all-done.1 = f32[16,128,128]{2,1,0:T(8,128)} async-done(((f32[16,128,128]{2,1,0:T(8,128)}), f32[16,128,128]{2,1,0:T(8,128)}, u32[]{:S(2)}, u32[]{:S(2)}) %all-to-all-start.1) | async-done | bytes 1048608 | tf_op jit(solution)/shard_map/all_to_all | solution.py:381
  47.4 1.6 %collective-permute-done.1.carry = f32[2,32,1024]{2,1,0:T(8,128)S(1)} collective-permute-done((f32[2,32,1024]{2,1,0:T(8,128)S(1)}, f32[2,32,1024]{2,1,0:T(8,128)S(1)}, u32[]{:S(2)}, u32[]{:S(2)}) %collective-permute-start.1) | collective-permute-done | bytes 262176 | tf_op jit(solution)/shard_map/ppermute | solution.py:399
  49.0 0.0 copy-done.2
  49.0 0.0 copy-start.3
  49.0 1.2 %copy-done.3 = f32[4,4,2,32,256]{4,3,2,1,0:T(8,128)S(1)} copy-done((f32[4,4,2,32,256]{4,3,2,1,0:T(8,128)S(1)}, f32[4,4,2,32,256]{4,3,2,1,0:T(8,128)}, u32[]{:S(2)}) %copy-start.3) | copy-done | bytes 1048600
  50.2 1.8 %shard_map.71 = f32[4,4,2,32,256]{4,3,2,1,0:T(8,128)} custom-call(s32[4]{0:T(128)S(4)} %get-tuple-element.14.refs_0_.count_ref, f32[4,4,2,32,256]{4,3,2,1,0:T(8,128)S(1)} %copy-done.3, f32[2,32,1024]{2,1,0:T(8,128)S(1)} %collective-permute-done.1.carry, f32[3,2,4,32,256]{4,3,2,1,0:T(8,128)S(1)} %copy-done.2, bf16[2,2,256,256]{3,2,1,0:T(8,128)(2,1)S(1)} %copy-done.1, ...), custom_call_target="tpu_custom_call" | custom-call | flops 603979776 | bytes 4194320 | tf_op jit(solution)/shard_map/pallas_call | solution.py:317
  52.1 6.8 %all-to-all-start.3 = ((f32[16,2,32,256]{3,2,1,0:T(8,128)}), f32[16,2,32,256]{3,2,1,0:T(8,128)S(1)}, u32[]{:S(2)}, u32[]{:S(2)}) async-start(f32[16,2,32,256]{3,2,1,0:T(8,128)} %bitcast.9), calls=%async_computation.3 | async-start | bytes 2097152 | tf_op jit(solution)/shard_map/all_to_all | solution.py:434
  58.9 1.5 %shard_map.68.refs_2_.turns = f32[3,2,4,32,256]{4,3,2,1,0:T(8,128)} custom-call(), custom_call_target="tpu_custom_call" | custom-call | flops 5242880 | bytes 786432 | tf_op jit(solution)/shard_map/pallas_call | solution.py:317
  60.4 3.2 %shard_map.69 = (f32[4,4,2,32,256]{4,3,2,1,0:T(8,128)}, f32[2,32,1024]{2,1,0:T(8,128)}) custom-call(s32[4]{0:T(128)S(4)} %get-tuple-element.14.refs_0_.count_ref, f32[4,4,128,128]{3,2,1,0:T(8,128)} %bitcast.2.refs_1_, f32[3,2,4,32,256]{4,3,2,1,0:T(8,128)} %shard_map.68.refs_2_.turns, bf16[2,2,256,256]{3,2,1,0:T(8,128)(2,1)S(1)} %copy-done.1, ...), custom_call_target="tpu_custom_call" | custom-call | flops 603979776 | bytes 4194320 | tf_op jit(solution)/shard_map/pallas_call | solution.py:317
  63.6 5.3 %collective-permute-start = (f32[2,32,1024]{2,1,0:T(8,128)}, f32[2,32,1024]{2,1,0:T(8,128)S(1)}, u32[]{:S(2)}, u32[]{:S(2)}) collective-permute-start(f32[2,32,1024]{2,1,0:T(8,128)} %get-tuple-element.18), channel_id=1, source_target_pairs={{0,16},{1,17},{2,18},{3,19},{4,20},{5,21},{6,22},{7,23},{8,24},{9,... | collective-permute-start | bytes 786440 | tf_op jit(solution)/shard_map/ppermute | solution.py:399
  68.9 8.2 %collective-permute-done.carry = f32[2,32,1024]{2,1,0:T(8,128)S(1)} collective-permute-done((f32[2,32,1024]{2,1,0:T(8,128)}, f32[2,32,1024]{2,1,0:T(8,128)S(1)}, u32[]{:S(2)}, u32[]{:S(2)}) %collective-permute-start) | collective-permute-done | bytes 262176 | tf_op jit(solution)/shard_map/ppermute | solution.py:399
  77.1 3.3 %shard_map.70 = f32[4,4,2,32,256]{4,3,2,1,0:T(8,128)} custom-call(s32[4]{0:T(128)S(4)} %get-tuple-element.14.refs_0_.count_ref, f32[4,4,2,32,256]{4,3,2,1,0:T(8,128)} %get-tuple-element.17.spectra, f32[2,32,1024]{2,1,0:T(8,128)S(1)} %collective-permute-done.carry, f32[3,2,4,32,256]{4,3,2,1,0:T(8,128)} %shard_map.68.refs_2_.turns, ...), custom_call_target="tpu_custom_call" | custom-call | flops 603979776 | bytes 4194320 | tf_op jit(solution)/shard_map/pallas_call | solution.py:317
  80.4 0.0 all-to-all-done.3.r_hbm
  80.4 0.0 copy-start.4
  80.4 8.6 %all-to-all-start.2 = ((f32[16,2,32,256]{3,2,1,0:T(8,128)}), f32[16,2,32,256]{3,2,1,0:T(8,128)S(1)}, u32[]{:S(2)}, u32[]{:S(2)}) async-start(f32[16,2,32,256]{3,2,1,0:T(8,128)} %bitcast.10), calls=%async_computation.2 | async-start | bytes 2097152 | tf_op jit(solution)/shard_map/all_to_all | solution.py:434
  89.1 0.0 copy-done.4
  89.1 2.7 %shard_map.72 = (f32[2,256,512]{2,1,0:T(8,128)}, f32[16,2,32,256]{3,2,1,0:T(8,128)}) custom-call(f32[16,2,32,256]{3,2,1,0:T(8,128)} %copy-done.4, bf16[2,2,256,256]{3,2,1,0:T(8,128)(2,1)S(1)} %copy-done.1), custom_call_target="tpu_custom_call", output_to_operand_aliasing={{1}: (0, {})} | custom-call | flops 402653184 | bytes 3670016 | tf_op jit(solution)/shard_map/pallas_call | solution.py:317
  91.8 13.4 %all-to-all-done.2.r_ref = f32[16,2,32,256]{3,2,1,0:T(8,128)S(1)} async-done(((f32[16,2,32,256]{3,2,1,0:T(8,128)}), f32[16,2,32,256]{3,2,1,0:T(8,128)S(1)}, u32[]{:S(2)}, u32[]{:S(2)}) %all-to-all-start.2) | async-done | bytes 1048608 | tf_op jit(solution)/shard_map/all_to_all | solution.py:434
  105.2 2.9 %shard_map.73 = f32[2,256,1024]{2,1,0:T(8,128)} custom-call(f32[16,2,32,256]{3,2,1,0:T(8,128)S(1)} %all-to-all-done.2.r_ref, f32[2,256,512]{2,1,0:T(8,128)} %get-tuple-element.22.even_hbm, bf16[2,2,256,256]{3,2,1,0:T(8,128)(2,1)S(1)} %copy-done), custom_call_target="tpu_custom_call" | custom-call | flops 805306368 | bytes 4718592 | tf_op jit(solution)/shard_map/pallas_call | solution.py:317
Async XLA Ops:
  3.7 23.2 %all-to-all-start = ((f32[16,136,128]{2,1,0:T(8,128)}), f32[16,136,128]{2,1,0:T(8,128)S(1)}, u32[]{:S(2)}, u32[]{:S(2)}) async-start(f32[16,136,128]{2,1,0:T(8,128)} %shard_map.64), calls=%async_computation | async-start | bytes 2228224 | tf_op jit(solution)/shard_map/all_to_all | solution.py:381
  13.5 19.2 %copy-start = (bf16[2,2,256,256]{3,2,1,0:T(8,128)(2,1)S(1)}, bf16[2,2,256,256]{3,2,1,0:T(8,128)(2,1)}, u32[]{:S(2)}) copy-start(bf16[2,2,256,256]{3,2,1,0:T(8,128)(2,1)} %constant.5.clone.refs_3_.table_hbm.refs_4_.mixing.table) | copy-start | bytes 1572868
  13.5 19.2 %copy-start.1 = (bf16[2,2,256,256]{3,2,1,0:T(8,128)(2,1)S(1)}, bf16[2,2,256,256]{3,2,1,0:T(8,128)(2,1)}, u32[]{:S(2)}) copy-start(bf16[2,2,256,256]{3,2,1,0:T(8,128)(2,1)} %constant.4.clone.table_hbm.refs_2_.refs_3_.even.table) | copy-start | bytes 1572868
  26.9 20.5 %all-to-all-start.1 = ((f32[16,128,128]{2,1,0:T(8,128)}), f32[16,128,128]{2,1,0:T(8,128)}, u32[]{:S(2)}, u32[]{:S(2)}) async-start(f32[16,128,128]{2,1,0:T(8,128)} %shard_map.67), calls=%async_computation.1 | async-start | bytes 2097152 | tf_op jit(solution)/shard_map/all_to_all | solution.py:381
  32.7 16.3 %copy-start.2 = (f32[3,2,4,32,256]{4,3,2,1,0:T(8,128)S(1)}, f32[3,2,4,32,256]{4,3,2,1,0:T(8,128)}, u32[]{:S(2)}) copy-start(f32[3,2,4,32,256]{4,3,2,1,0:T(8,128)} %shard_map.65.refs_1_.turns) | copy-start | bytes 2359300
  34.8 14.2 %collective-permute-start.1 = (f32[2,32,1024]{2,1,0:T(8,128)S(1)}, f32[2,32,1024]{2,1,0:T(8,128)S(1)}, u32[]{:S(2)}, u32[]{:S(2)}) collective-permute-start(f32[2,32,1024]{2,1,0:T(8,128)S(1)} %get-tuple-element.20), channel_id=1, source_target_pairs={{0,16},{1,17},{2,18},{3,19},{4,20},{5,21},{6,22},{7,23},{8,24},{9,... | collective-permute-start | bytes 786440 | tf_op jit(solution)/shard_map/ppermute | solution.py:399
  49.0 1.2 %copy-start.3 = (f32[4,4,2,32,256]{4,3,2,1,0:T(8,128)S(1)}, f32[4,4,2,32,256]{4,3,2,1,0:T(8,128)}, u32[]{:S(2)}) copy-start(f32[4,4,2,32,256]{4,3,2,1,0:T(8,128)} %get-tuple-element.19.spectra) | copy-start | bytes 3145732
  52.1 28.3 %all-to-all-start.3 = ((f32[16,2,32,256]{3,2,1,0:T(8,128)}), f32[16,2,32,256]{3,2,1,0:T(8,128)S(1)}, u32[]{:S(2)}, u32[]{:S(2)}) async-start(f32[16,2,32,256]{3,2,1,0:T(8,128)} %bitcast.9), calls=%async_computation.3 | async-start | bytes 2097152 | tf_op jit(solution)/shard_map/all_to_all | solution.py:434
  63.6 13.5 %collective-permute-start = (f32[2,32,1024]{2,1,0:T(8,128)}, f32[2,32,1024]{2,1,0:T(8,128)S(1)}, u32[]{:S(2)}, u32[]{:S(2)}) collective-permute-start(f32[2,32,1024]{2,1,0:T(8,128)} %get-tuple-element.18), channel_id=1, source_target_pairs={{0,16},{1,17},{2,18},{3,19},{4,20},{5,21},{6,22},{7,23},{8,24},{9,... | collective-permute-start | bytes 786440 | tf_op jit(solution)/shard_map/ppermute | solution.py:399
  80.4 8.7 %copy-start.4 = (f32[16,2,32,256]{3,2,1,0:T(8,128)}, f32[16,2,32,256]{3,2,1,0:T(8,128)S(1)}, u32[]{:S(2)}) copy-start(f32[16,2,32,256]{3,2,1,0:T(8,128)S(1)} %all-to-all-done.3.r_hbm) | copy-start | bytes 3145732
  80.4 24.8 %all-to-all-start.2 = ((f32[16,2,32,256]{3,2,1,0:T(8,128)}), f32[16,2,32,256]{3,2,1,0:T(8,128)S(1)}, u32[]{:S(2)}, u32[]{:S(2)}) async-start(f32[16,2,32,256]{3,2,1,0:T(8,128)} %bitcast.10), calls=%async_computation.2 | async-start | bytes 2097152 | tf_op jit(solution)/shard_map/all_to_all | solution.py:434
